TPU v7x, 512 devices: a 8x2x16 block of a 8x8x16 slice. The times are simulated.
512 devices in a mesh: groups: 2 (over y), expert: 32 (over z, core), tensor: 8 (over x).
Axes of the slice: x: 8, y: 2, z: 16, core: 2. Of those that a mesh axis runs over, the one named last changes fastest.
The devices are a block of a 8x8x16 slice.
Arguments:
- queries: bfloat16 [2048, 4096], P(('groups', 'expert')), parts along dimension 0, may hold values from -200 to 200
- own_kv: bfloat16 [2048, 1024], P(('groups', 'expert')), parts along dimension 0, may hold values from -6 to 6
- prompt_cache: bfloat16 [64, 256, 1024], P(('groups', 'expert'), 'tensor'), parts along dimension 0, may hold values from -8 to 8
- prompt_len: int32 [64], P(('groups', 'expert')), parts along dimension 0, may hold values from 2 to 256
- token_prompt: int32 [2048], P(('groups', 'expert')), parts along dimension 0, may hold values from 0 to 31, as said below
- residual: bfloat16 [2048, 2048], P(('groups', 'expert')), parts along dimension 0, may hold values from -3 to 3
- out_weight: bfloat16 [4096, 2048], P('tensor', 'expert'), may hold values from -0.1875 to 0.1875
- route_ids: int32 [2048, 8], P(('groups', 'expert')), parts along dimension 0, may hold values from 0 to 63, all different within a row; in each aligned block of 32 rows (0 to 31, 32 to 63, ...) at most 6 rows name the same one
- route_weights: float32 [2048, 8], P(('groups', 'expert')), parts along dimension 0, may hold values from 0.05 to 0.3
- w_gate: bfloat16 [64, 2048, 1024], P('expert', None, 'tensor'), may hold values from -0.125 to 0.125
- w_up: bfloat16 [64, 2048, 1024], P('expert', None, 'tensor'), may hold values from -0.125 to 0.125
- w_down: bfloat16 [64, 1024, 2048], P('expert', 'tensor'), may hold values from -0.25 to 0.25
Outputs:
- mixed: bfloat16 [2048, 2048], P(('groups', 'expert'), 'tensor'), parts along dimension 0
There are 2 independent parts, one for each index of `groups`. A program takes and returns all parts, laid end to end along the dimension named above; an argument that names none is the same for every part. Nothing has to cross between parts.
Inputs may be any that keep to these rules, and one draw needn't show every extreme that they name: `token_prompt`: each index of the expert axis holds 2 tokens of each of 16 prompts and none of the others; each prompt has tokens on exactly 16 indices. `route_ids`: A row names distinct experts. Within the 32 rows of one index of the expert axis no expert is named more than 6 times, and in some of these blocks one is named exactly 6 times.
All inputs are finite; a program needn't handle non-finite values.
Results may differ from a plain program's by a relative error of at most 0.015.
Values may be sent and summed in bfloat16 or wider, within the bound.
No kernel may reach another device: no remote copies, remote signals or barrier semaphores. Data moves between devices by JAX's collectives and lax.ppermute only.
A program may use at most 64 MiB of HBM per device.

v0:
```python
import jax
import jax.numpy as jnp
from jax import lax
from jax.sharding import Mesh
from jax.sharding import PartitionSpec as P

HD = 128
EXPERT = ("expert_0", "expert_1")
GROUPS_EXPERT = ("groups", "expert_0", "expert_1")


MASKED_SCORE = -1e30


def combined_all(x, axis, combine):
    everything = jax.tree.map(
        lambda part, kind: lax.all_gather(part.astype(kind), axis),
        x,
        jax.tree.map(lambda a: jnp.bfloat16 if a.dtype == jnp.float32 else a.dtype, x),
    )

    def take(k):
        return jax.tree.map(lambda part, own: part[k].astype(own.dtype), everything, x)

    return lax.fori_loop(
        1, lax.axis_size(axis), lambda k, so_far: combine(so_far, take(k)), take(0)
    )


def sent_to_all(x, axis):
    copies = jnp.broadcast_to(x, (lax.axis_size(axis), *x.shape))
    return lax.all_to_all(copies, axis, split_axis=0, concat_axis=0, tiled=True)


def joined_along(tiles, dim):
    tiles = jnp.moveaxis(tiles, 0, dim)
    shape = tiles.shape
    return tiles.reshape(*shape[:dim], shape[dim] * shape[dim + 1], *shape[dim + 2 :])


def gathered_copies(x, axis, dim):
    tiles = sent_to_all(x, axis)
    return joined_along(tiles, dim)


def in_blocks(x, dim, length):
    shape = x.shape
    tiles = x.reshape(*shape[:dim], length, shape[dim] // length, *shape[dim + 1 :])
    return jnp.moveaxis(tiles, dim, 0)


def exchange_in_order(tiles, axes, sequence):
    shape = [lax.axis_size(a) for a in axes]
    tiles = tiles.reshape(*shape, *tiles.shape[1:])
    for k in sequence:
        tiles = lax.all_to_all(tiles, axes[k], split_axis=k, concat_axis=k, tiled=True)
    return tiles.reshape(-1, *tiles.shape[len(axes) :])


def two_step_exchange(x, groups, sequence, split_dim, concat_dim):
    length = lax.axis_size(groups[0]) * lax.axis_size(groups[1])
    tiles = in_blocks(x, split_dim, length)
    return joined_along(exchange_in_order(tiles, groups, sequence), concat_dim)


def sent_and_summed(x, axis, dim):
    tiles = in_blocks(x, dim, lax.axis_size(axis))
    arrived = lax.all_to_all(tiles, axis, split_axis=0, concat_axis=0, tiled=True)
    return arrived.astype(jnp.float32).sum(axis=0)


def combine_parts(earlier, later):
    top_a, sum_a, value_a = earlier
    top_b, sum_b, value_b = later
    top_score = jnp.maximum(top_a, top_b)
    shrink_a = jnp.exp(top_a - top_score)
    shrink_b = jnp.exp(top_b - top_score)
    return (
        top_score,
        sum_a * shrink_a + sum_b * shrink_b,
        value_a * shrink_a[..., None] + value_b * shrink_b[..., None],
    )


def local(
    queries,
    own_kv,
    prompt_cache,
    prompt_len,
    token_prompt,
    residual,
    out_weight,
    route_ids,
    route_weights,
    w_gate,
    w_up,
    w_down,
):
    tokens = queries.shape[0]
    half_cols = own_kv.shape[1] // 2
    kv_heads = half_cols // HD
    head_count = queries.shape[1] // HD
    group_size = head_count // kv_heads
    score_scale = HD ** (-0.5)
    expert_groups = lax.axis_size(EXPERT)
    fan_count = expert_groups // 2
    per_prompt = tokens // fan_count
    order = jnp.argsort(token_prompt, stable=True)
    inverse = jnp.argsort(order)
    held_prompts = token_prompt[order].reshape(fan_count, per_prompt)[:, 0]
    sorted_query = queries[order].reshape(fan_count, per_prompt, kv_heads, group_size, HD)
    sorted_own = own_kv[order]
    own_keys = sorted_own[:, :half_cols].reshape(fan_count, per_prompt, kv_heads, HD)
    own_values = (
        sorted_own[:, half_cols:].reshape(fan_count, per_prompt, kv_heads, HD).astype(jnp.float32)
    )
    own_score = (
        jnp.einsum("imgjd,imgd->imgj", sorted_query, own_keys, preferred_element_type=jnp.float32)
        * score_scale
    )
    tensor_pos = lax.axis_index("tensor")
    leading = tensor_pos == 0
    start_top = jnp.where(leading, own_score, MASKED_SCORE)
    start_sum = jnp.where(leading, jnp.ones_like(own_score), jnp.zeros_like(own_score))
    start_values = jnp.where(
        leading,
        jnp.broadcast_to(
            own_values[:, :, :, None, :], (fan_count, per_prompt, kv_heads, group_size, HD)
        ),
        0.0,
    )
    block_len = prompt_cache.shape[1]
    positions = tensor_pos * block_len + jnp.arange(block_len, dtype=jnp.int32)
    cache_piece = lax.all_gather(prompt_cache, EXPERT, axis=0, tiled=True)
    length_piece = lax.all_gather(prompt_len, EXPERT, axis=0, tiled=True)
    shard_count = cache_piece.shape[0]
    owners = jnp.arange(shard_count, dtype=jnp.int32)
    matched = owners[:, None] == held_prompts[None, :]
    match_half = matched.astype(jnp.bfloat16)
    match_full = matched.astype(jnp.float32)
    present = jnp.any(matched, 0)
    piece_query = jnp.einsum(
        "qi,imgjd->qmgjd", match_half, sorted_query, preferred_element_type=jnp.float32
    ).astype(jnp.bfloat16)
    key_rows = cache_piece[:, :, :half_cols].reshape(shard_count, block_len, kv_heads, HD)
    value_rows = (
        cache_piece[:, :, half_cols:]
        .reshape(shard_count, block_len, kv_heads, HD)
        .astype(jnp.float32)
    )
    inside = (positions[None, :] < length_piece[:, None])[:, None, None, None, :]
    score_rows = (
        jnp.einsum("qmgjd,qpgd->qmgjp", piece_query, key_rows, preferred_element_type=jnp.float32)
        * score_scale
    )
    score_rows = jnp.where(inside, score_rows, MASKED_SCORE)
    piece_top = jnp.max(score_rows, -1)
    weights = jnp.where(inside, jnp.exp(score_rows - piece_top[..., None]), 0.0)
    piece_sum = jnp.sum(weights, -1)
    piece_values = jnp.einsum("qmgjp,qpgd->qmgjd", weights, value_rows)
    group_top = jnp.einsum("qi,qmgj->imgj", match_full, piece_top)
    group_top = jnp.where(present[:, None, None, None], group_top, MASKED_SCORE)
    group_sum = jnp.einsum("qi,qmgj->imgj", match_full, piece_sum)
    group_values = jnp.einsum("qi,qmgjd->imgjd", match_full, piece_values)
    folded = combine_parts(
        (start_top, start_sum, start_values), (group_top, group_sum, group_values)
    )
    top_score, weight_sum, value_sum = combined_all(folded, "tensor", combine_parts)
    attn_sorted = (value_sum / weight_sum[..., None]).reshape(tokens, head_count * HD)
    attn = attn_sorted[inverse].astype(jnp.bfloat16)
    rows_here = out_weight.shape[0]
    attn_mine = lax.dynamic_slice_in_dim(attn, tensor_pos * rows_here, rows_here, 1)
    column_terms = jnp.dot(
        gathered_copies(attn_mine, EXPERT, 0), out_weight, preferred_element_type=jnp.float32
    )
    partials = two_step_exchange(
        column_terms.astype(jnp.bfloat16), ("expert_0", "expert_1"), (1, 0), 0, 1
    ).astype(column_terms.dtype)
    model_width = residual.shape[1]
    col_width = model_width // lax.axis_size("tensor")
    col_start = tensor_pos * col_width
    resid_cols = lax.dynamic_slice_in_dim(residual, col_start, col_width, 1)
    experts_here = w_gate.shape[0]
    experts = experts_here * expert_groups
    picks = route_ids.shape[1]
    capacity = min(tokens, 3 * tokens * picks // (2 * experts))
    flat_ids = route_ids.reshape(-1)
    expert_marks = (flat_ids[:, None] == jnp.arange(experts, dtype=jnp.int32)[None, :]).astype(
        jnp.int32
    )
    slot_index = jnp.sum((jnp.cumsum(expert_marks, 0) - expert_marks) * expert_marks, 1)
    destination = flat_ids * capacity + slot_index
    source_rows = jnp.arange(tokens * picks, dtype=jnp.int32) // picks
    head_total = sent_and_summed(partials.astype(jnp.bfloat16), "tensor", 1)
    hidden_cols = (resid_cols.astype(jnp.float32) + head_total).astype(jnp.bfloat16)
    outgoing = (
        jnp.zeros((experts * capacity, col_width), jnp.bfloat16)
        .at[destination]
        .set(hidden_cols[source_rows])
    )
    outgoing = outgoing.reshape(expert_groups, experts_here, capacity, col_width)
    arrived = lax.all_to_all(outgoing, EXPERT, split_axis=0, concat_axis=0, tiled=True)
    arrived = gathered_copies(arrived, "tensor", 3)
    gate_proj = jnp.einsum("sxcd,xdf->sxcf", arrived, w_gate, preferred_element_type=jnp.float32)
    up_proj = jnp.einsum("sxcd,xdf->sxcf", arrived, w_up, preferred_element_type=jnp.float32)
    activated = (jax.nn.silu(gate_proj) * up_proj).astype(jnp.bfloat16)
    expert_partials = jnp.einsum(
        "sxcf,xfd->sxcd", activated, w_down, preferred_element_type=jnp.float32
    )
    summed = sent_and_summed(expert_partials.astype(jnp.bfloat16), "tensor", 3).astype(jnp.bfloat16)
    returned = lax.all_to_all(summed, EXPERT, split_axis=0, concat_axis=0, tiled=True).reshape(
        experts * capacity, col_width
    )
    picked = returned[destination].reshape(tokens, picks, col_width).astype(jnp.float32)
    expert_mix = jnp.sum(route_weights[:, :, None] * picked, 1)
    return (hidden_cols.astype(jnp.float32) + expert_mix).astype(jnp.bfloat16)


def solution(mesh):
    split = Mesh(
        mesh.devices.reshape(mesh.shape["groups"], 16, 2, mesh.shape["tensor"]),
        ("groups", "expert_0", "expert_1", "tensor"),
    )
    return jax.shard_map(
        local,
        mesh=split,
        in_specs=(
            P(GROUPS_EXPERT, None),
            P(GROUPS_EXPERT, None),
            P(GROUPS_EXPERT, "tensor", None),
            P(GROUPS_EXPERT),
            P(GROUPS_EXPERT),
            P(GROUPS_EXPERT, None),
            P("tensor", EXPERT),
            P(GROUPS_EXPERT, None),
            P(GROUPS_EXPERT, None),
            P(EXPERT, None, "tensor"),
            P(EXPERT, None, "tensor"),
            P(EXPERT, "tensor", None),
        ),
        out_specs=P(GROUPS_EXPERT, "tensor"),
        check_vma=False,
    )
```

profile of v0, /device:TPU:65, one launch (start us, length us, event | category | flops | bytes accessed | tf_op | source)
XLA Modules:
  0.0 455.3 jit_solution(9609944883478127839)
XLA Ops:
  6.6 0.7 all-gather.6.cloned.1.call-update
  7.4 2.3 sort.34
  9.7 1.6 sort.35
  11.3 1.4 gather_fusion.2
  12.6 0.7 gather_fusion
  14.2 0.6 gather_fusion.1
  15.3 1.3 dynamic-slice
  16.6 0.8 dynamic-update-slice
  17.3 57.1 %all-reduce = s32[32]{0:T(128)S(1)} all-reduce(s32[32]{0:T(128)S(1)} %dynamic-update-slice), channel_id=1, replica_groups=mesh['groups'=2,'expert_0'=16,'expert_1'=2,'tensor'=8] {'expert_0','expe..., use_global_device_ids=true, to_apply=%add | all-reduce | flops 32 | bytes 256
  74.8 1.2 convolution_convert_fusion.1
  76.0 42.0 %all-gather.6.cloned.1.call-done = bf16[32,32,1024]{2,1,0:T(8,128)(2,1)} async-done(((bf16[1,32,1024]{2,1,0:T(8,128)(2,1)}), bf16[32,32,1024]{2,1,0:T(8,128)(2,1)}) %all-gather.6.cloned.1.call-update) | async-done | bytes 2097168 | tf_op jit(solution)/shard_map/all_gather | solution.py:134
  118.1 2.7 fusion.51
  121.1 1.9 fusion.52
  123.2 0.8 fusion.16
  124.3 1.1 reshape.195
  125.4 1.7 convolution_bitcast_fusion
  127.2 1.3 fusion.6
  128.6 20.8 %all-gather = bf16[128,2,4,8]{3,2,1,0:T(4,128)(2,1)S(1)} all-gather(bf16[16,2,4,8]{3,2,1,0:T(4,128)(2,1)S(1)} %copy.80), channel_id=2, replica_groups=mesh['groups'=2,'expert_0'=16,'expert_1'=2,'tensor'=8] {'tensor'}, dimensions={0}, use_global_device_ids=true | all-gather | bytes 18432 | tf_op jit(solution)/shard_map/all_gather | solution.py:17
  149.6 21.1 %all-gather.1 = bf16[128,2,4,8]{3,2,1,0:T(4,128)(2,1)S(1)} all-gather(bf16[16,2,4,8]{3,2,1,0:T(4,128)(2,1)S(1)} %copy.82), channel_id=3, replica_groups=mesh['groups'=2,'expert_0'=16,'expert_1'=2,'tensor'=8] {'tensor'}, dimensions={0}, use_global_device_ids=true | all-gather | bytes 18432 | tf_op jit(solution)/shard_map/all_gather | solution.py:17
  171.3 4.4 all-gather.8.cloned.1.call-done
  175.7 1.0 slice_convert_fusion
  176.8 11.6 %while.19 = (s32[]{:T(128)}, f32[16,2,4,8]{0,3,2,1:T(8,128)S(1)}, f32[16,2,4,8]{0,3,2,1:T(8,128)S(1)}, f32[16,2,4,8,128]{4,3,2,1,0:T(8,128)S(1)}, bf16[8,16,2,4,...) while((s32[]{:T(128)}, f32[16,2,4,8]{0,3,2,1:T(8,128)S(1)}, ...), condition=%wide.region_5.6_spmd, body=%wide.region_4.5_spmd.sunk | while | flops 532485 | bytes 1888407 | solution.py:25
  176.9 1.0 constant_dynamic-slice_fusion.2
  178.1 0.4 fusion.65
  178.6 1.0 constant_dynamic-slice_fusion.2
  179.8 0.4 fusion.65
  180.2 1.0 constant_dynamic-slice_fusion.2
  181.4 0.4 fusion.65
  181.9 1.0 constant_dynamic-slice_fusion.2
  183.1 0.4 fusion.65
  183.5 1.0 constant_dynamic-slice_fusion.2
  184.7 0.4 fusion.65
  185.2 1.0 constant_dynamic-slice_fusion.2
  186.4 0.4 fusion.65
  186.9 1.0 constant_dynamic-slice_fusion.2
  188.1 0.4 fusion.65
  188.9 0.7 gather_fusion.3
  189.7 1.1 broadcast_in_dim.93
  190.8 18.3 %all-to-all-start = ((bf16[32,32,512]{2,1,0:T(8,128)(2,1)}), bf16[32,32,512]{2,1,0:T(8,128)(2,1)S(1)}, u32[]{:S(2)}, u32[]{:S(2)}) async-start(bf16[32,32,512]{2,1,0:T(8,128)(2,1)} %broadcast_in_dim.93), calls=%async_computation | async-start | bytes 2097152 | tf_op jit(solution)/shard_map/all_to_all | solution.py:32
  209.3 0.6 reduce-window.6
  209.9 54.7 %all-to-all-done = bf16[32,32,512]{2,1,0:T(8,128)(2,1)S(1)} async-done(((bf16[32,32,512]{2,1,0:T(8,128)(2,1)}), bf16[32,32,512]{2,1,0:T(8,128)(2,1)S(1)}, u32[]{:S(2)}, u32[]{:S(2)}) %all-to-all-start) | async-done | bytes 1048608 | tf_op jit(solution)/shard_map/all_to_all | solution.py:32
  264.6 0.4 convolution_convert_fusion.2
  265.5 4.0 all_to_all.40
  269.7 0.9 reshape.313
  270.6 4.1 all-to-all-start.2
  275.2 11.5 %all-to-all-done.2 = bf16[16,2,2048]{2,1,0:T(2,128)(2,1)S(1)} async-done(((bf16[16,2,2048]{2,1,0:T(2,128)(2,1)}), bf16[16,2,2048]{2,1,0:T(2,128)(2,1)S(1)}, u32[]{:S(2)}, u32[]{:S(2)}) %all-to-all-start.2) | async-done | bytes 131104 | tf_op jit(solution)/shard_map/all_to_all | solution.py:56
  287.2 0.7 copy.97
  287.9 4.0 all-to-all-start.3
  292.0 7.8 %all-to-all-done.3 = bf16[8,32,256]{2,1,0:T(8,128)(2,1)S(1)} async-done(((bf16[8,32,256]{2,1,0:T(8,128)(2,1)}), bf16[8,32,256]{2,1,0:T(8,128)(2,1)S(1)}, u32[]{:S(2)}, u32[]{:S(2)}) %all-to-all-start.3) | async-done | bytes 131104 | tf_op jit(solution)/shard_map/all_to_all | solution.py:68
  299.9 0.7 add_convert_fusion.1
  300.6 2.2 scatter_custom_fusion
  303.1 27.2 %all_to_all.41 = bf16[32,2,6,256]{3,1,2,0:T(2,128)(2,1)S(1)} all-to-all(bf16[32,2,6,256]{3,1,2,0:T(2,128)(2,1)S(1)} %copy.103), channel_id=1, replica_groups=mesh['groups'=2,'expert_0'=16,'expert_1'=2,'tensor'=8] {'expert_0','expe..., dimensions={0} | all-to-all | bytes 393216 | tf_op jit(solution)/shard_map/all_to_all | solution.py:202
  330.5 40.4 %all_to_all.42 = bf16[8,32,2,6,256]{4,1,3,2,0:T(8,128)(2,1)S(1)} all-to-all(bf16[8,32,2,6,256]{4,1,3,2,0:T(8,128)(2,1)S(1)} %broadcast_in_dim.95), channel_id=1, replica_groups=mesh['groups'=2,'expert_0'=16,'expert_1'=2,'tensor'=8] {'tensor'}, dimensions={0} | all-to-all | bytes 3145728 | tf_op jit(solution)/shard_map/all_to_all | solution.py:32
  371.1 1.0 copy-done.4
  372.1 0.6 convolution_bitcast_fusion.2
  372.7 3.3 convolution_convert_fusion
  376.1 1.6 copy.148
  377.7 40.0 %all_to_all.43 = bf16[8,32,2,6,256]{4,1,3,2,0:T(8,128)(2,1)S(1)} all-to-all(bf16[8,32,2,6,256]{4,1,3,2,0:T(8,128)(2,1)S(1)} %bitcast.142), channel_id=1, replica_groups=mesh['groups'=2,'expert_0'=16,'expert_1'=2,'tensor'=8] {'tensor'}, dimensions={0} | all-to-all | bytes 3145728 | tf_op jit(solution)/shard_map/all_to_all | solution.py:68
  417.7 0.3 reduce_sum.54
  418.0 0.9 copy.108
  418.9 9.0 %all-to-all-start.7 = ((bf16[32,2,6,256]{3,1,2,0:T(2,128)(2,1)}), bf16[32,2,6,256]{3,1,2,0:T(2,128)(2,1)S(1)}, u32[]{:S(2)}, u32[]{:S(2)}) async-start(bf16[32,2,6,256]{3,1,2,0:T(2,128)(2,1)} %copy.108), calls=%async_computation.7 | async-start | bytes 393216 | tf_op jit(solution)/shard_map/all_to_all | solution.py:211
  428.0 18.4 %all-to-all-done.7 = bf16[32,2,6,256]{3,1,2,0:T(2,128)(2,1)S(1)} async-done(((bf16[32,2,6,256]{3,1,2,0:T(2,128)(2,1)}), bf16[32,2,6,256]{3,1,2,0:T(2,128)(2,1)S(1)}, u32[]{:S(2)}, u32[]{:S(2)}) %all-to-all-start.7) | async-done | bytes 196640 | tf_op jit(solution)/shard_map/all_to_all | solution.py:211
  446.5 1.2 gather_fusion.4
  447.8 0.6 add_convert_fusion
  (111 shorter events, 8.0 us)
Async XLA Ops:
  6.5 366.2 %copy-start = (bf16[2,128,2048]{2,1,0:T(8,128)(2,1)S(1)}, bf16[2,128,2048]{2,1,0:T(8,128)(2,1)}, u32[]{:S(2)}) copy-start(bf16[2,128,2048]{2,1,0:T(8,128)(2,1)} %param.25) | copy-start | bytes 3145732
  6.6 6.1 %copy-start.1 = (bf16[32,4096]{1,0:T(8,128)(2,1)S(1)}, bf16[32,4096]{1,0:T(8,128)(2,1)}, u32[]{:S(2)}) copy-start(bf16[32,4096]{1,0:T(8,128)(2,1)} %param.14) | copy-start | bytes 786436
  6.6 111.5 %all-gather.6.cloned.1.call-start = ((), (), s32[]{:S(2)}) async-start(), calls=%async_computation.8 | async-start | bytes 2162688 | tf_op jit(solution)/shard_map/all_gather | solution.py:134
  7.3 168.4 %all-gather.8.cloned.1.call-start = ((), (), s32[]{:S(2)}) async-start(), calls=%async_computation.9 | async-start | bytes 2359296 | tf_op jit(solution)/shard_map/all_gather | solution.py:17
  12.6 1.5 copy-start.2
  122.9 1.4 copy-start.3
  189.7 19.4 %copy-start.6 = (s32[32,8]{0,1:T(8,128)S(1)}, s32[32,8]{0,1:T(8,128)}, u32[]{:S(2)}) copy-start(s32[32,8]{0,1:T(8,128)} %param.21) | copy-start | bytes 3076
  189.7 74.9 %copy-start.5 = (bf16[512,64]{0,1:T(8,128)(2,1)S(1)}, bf16[512,64]{0,1:T(8,128)(2,1)}, u32[]{:S(2)}) copy-start(bf16[512,64]{0,1:T(8,128)(2,1)} %param.20) | copy-start | bytes 196612
  190.8 73.8 %all-to-all-start = ((bf16[32,32,512]{2,1,0:T(8,128)(2,1)}), bf16[32,32,512]{2,1,0:T(8,128)(2,1)S(1)}, u32[]{:S(2)}, u32[]{:S(2)}) async-start(bf16[32,32,512]{2,1,0:T(8,128)(2,1)} %broadcast_in_dim.93), calls=%async_computation | async-start | bytes 2097152 | tf_op jit(solution)/shard_map/all_to_all | solution.py:32
  270.6 16.0 %all-to-all-start.2 = ((bf16[16,2,2048]{2,1,0:T(2,128)(2,1)}), bf16[16,2,2048]{2,1,0:T(2,128)(2,1)S(1)}, u32[]{:S(2)}, u32[]{:S(2)}) async-start(bf16[16,2,2048]{2,1,0:T(2,128)(2,1)} %reshape.313), calls=%async_computation.2 | async-start | bytes 262144 | tf_op jit(solution)/shard_map/all_to_all | solution.py:56
  287.9 12.0 %all-to-all-start.3 = ((bf16[8,32,256]{2,1,0:T(8,128)(2,1)}), bf16[8,32,256]{2,1,0:T(8,128)(2,1)S(1)}, u32[]{:S(2)}, u32[]{:S(2)}) async-start(bf16[8,32,256]{2,1,0:T(8,128)(2,1)} %copy.97), calls=%async_computation.3 | async-start | bytes 262144 | tf_op jit(solution)/shard_map/all_to_all | solution.py:68
  370.9 1.2 copy-start.4
  417.7 10.2 %copy-start.7 = (f32[32,8]{0,1:T(8,128)S(1)}, f32[32,8]{0,1:T(8,128)}, u32[]{:S(2)}) copy-start(f32[32,8]{0,1:T(8,128)} %param.22) | copy-start | bytes 3076
  418.9 27.5 %all-to-all-start.7 = ((bf16[32,2,6,256]{3,1,2,0:T(2,128)(2,1)}), bf16[32,2,6,256]{3,1,2,0:T(2,128)(2,1)S(1)}, u32[]{:S(2)}, u32[]{:S(2)}) async-start(bf16[32,2,6,256]{3,1,2,0:T(2,128)(2,1)} %copy.108), calls=%async_computation.7 | async-start | bytes 393216 | tf_op jit(solution)/shard_map/all_to_all | solution.py:211
Sparse Core Ops, SparseCore 0:
  9.5 108.5 all-gather.5
  128.6 46.9 all-gather.7
where the time goes:
time: 457 us; the launch traced here: 455 us
  blocking collectives  211 us (46%)
  waiting for transfers between devices  140 us (31%)
  starting transfers between devices  35.4 us (8%)
  local copies, waits for them, and re-layouts  31.7 us (7%)
  between operations  14.6 us (3%)
  other arithmetic  11.9 us (3%)
  matrix products  11.1 us (2%)
    unnamed x1, blocking collectives  57.1 us
    all_to_all x1, waiting for transfers between devices, sent_to_all(): return lax.all_to_all(copies, axis, split_axis=0, concat_axis=0, tiled=True)  54.7 us
    all_gather x1, waiting for transfers between devices, local(): cache_piece = lax.all_gather(prompt_cache, EXPERT, axis=0, tiled=True)  42 us
    all_gather x2, blocking collectives, combined_all(): lax.all_gather(part.astype(kind), axis)  41.9 us
    all_to_all x1, blocking collectives, sent_to_all(): return lax.all_to_all(copies, axis, split_axis=0, concat_axis=0, tiled=True)  40.4 us
    all_to_all x1, blocking collectives, sent_and_summed(): lax.all_to_all(tiles, axis, split_axis=0, concat_axis=0, tiled=True)  40 us
    all_to_all x1, blocking collectives, local(): lax.all_to_all(outgoing, EXPERT, split_axis=0, concat_axis=0, tiled=True)  27.2 us
    all_to_all x1, waiting for transfers between devices, local(): lax.all_to_all(summed, EXPERT, split_axis=0, concat_axis=0, tiled=True)  18.4 us
  transfers between devices with their start and end apart: 6, of which 6 were waited for; matrix products, arithmetic and copies ran while one was open for 3% of the time, Pallas kernels for 0%

commit v1 on v0

v1 whole, which is shorter than its diff:
```python
import jax
import jax.numpy as jnp
from jax import lax
from jax.sharding import PartitionSpec as P

HD = 128
MASKED_SCORE = -1e30


def exchange(tiles, axis):
    return lax.all_to_all(tiles, axis, split_axis=0, concat_axis=0, tiled=True)


def local(
    queries,
    own_kv,
    prompt_cache,
    prompt_len,
    token_prompt,
    residual,
    out_weight,
    route_ids,
    route_weights,
    w_gate,
    w_up,
    w_down,
):
    f32, bf16 = jnp.float32, jnp.bfloat16
    n_e = lax.axis_size("expert")
    n_x = lax.axis_size("tensor")
    pos_x = lax.axis_index("tensor")
    tokens = queries.shape[0]
    half_cols = own_kv.shape[1] // 2
    kv_heads = half_cols // HD
    head_count = queries.shape[1] // HD
    group_size = head_count // kv_heads
    heads_here = head_count // n_x
    q_cols = heads_here * HD
    per_prompt = tokens // (n_e // 2)
    block_len = prompt_cache.shape[1]
    model_width = residual.shape[1]
    col_width = model_width // n_x

    experts_here = w_gate.shape[0]
    keep = pos_x % experts_here
    give = 1 - keep
    swap = [(i, i ^ 1) for i in range(n_x)]
    up_pair = jnp.stack(
        [
            lax.dynamic_index_in_dim(w_gate, give, 0, keepdims=False),
            lax.dynamic_index_in_dim(w_up, give, 0, keepdims=False),
        ]
    )
    got_up = lax.ppermute(up_pair, "tensor", swap)
    got_down = lax.ppermute(
        lax.dynamic_index_in_dim(w_down, give, 0, keepdims=False), "tensor", swap
    )
    all_out = lax.all_gather(out_weight.T, "expert", axis=0, tiled=True)

    kv_pos = (pos_x * heads_here) // group_size
    payload = jnp.concatenate(
        [
            lax.dynamic_slice_in_dim(queries, pos_x * q_cols, q_cols, 1),
            lax.dynamic_slice_in_dim(own_kv, kv_pos * HD, HD, 1),
            lax.dynamic_slice_in_dim(own_kv, half_cols + kv_pos * HD, HD, 1),
        ],
        1,
    )
    earlier = jnp.arange(tokens)[None, :] < jnp.arange(tokens)[:, None]
    same = token_prompt[:, None] == token_prompt[None, :]
    rank = jnp.sum((same & earlier).astype(jnp.int32), 1)
    place = token_prompt * per_prompt + rank
    rows = n_e * per_prompt
    pick = (jnp.arange(rows)[:, None] == place[None, :]).astype(bf16)
    sent = jnp.dot(pick, payload, preferred_element_type=f32).astype(bf16)
    got = exchange(sent.reshape(n_e, per_prompt, q_cols + 2 * HD), "expert")
    got = got.reshape(rows, q_cols + 2 * HD)

    cache = prompt_cache[0].reshape(block_len, 2, kv_heads, HD)
    by_head = jnp.transpose(cache, (2, 0, 1, 3)).reshape(kv_heads, block_len, 2 * HD)
    by_head = jnp.repeat(by_head, n_x // kv_heads, axis=0)
    cache_all = exchange(by_head, "tensor").reshape(n_x * block_len, 2 * HD)
    keys, values = cache_all[:, :HD], cache_all[:, HD:]

    q_rows = got[:, :q_cols].reshape(rows, heads_here, HD)
    k_own = got[:, q_cols : q_cols + HD].astype(f32)
    v_own = got[:, q_cols + HD :].astype(f32)
    scale = HD ** (-0.5)
    scores = jnp.einsum("rhd,pd->rhp", q_rows, keys, preferred_element_type=f32) * scale
    own = jnp.sum(q_rows.astype(f32) * k_own[:, None, :], -1) * scale
    inside = jnp.arange(n_x * block_len) < prompt_len[0]
    scores = jnp.where(inside, scores, MASKED_SCORE)
    top = jnp.maximum(jnp.max(scores, -1), own)
    weights = jnp.where(inside, jnp.exp(scores - top[..., None]), 0.0)
    own_weight = jnp.exp(own - top)
    total = jnp.sum(weights, -1) + own_weight
    mix = jnp.einsum("rhp,pd->rhd", weights.astype(bf16), values, preferred_element_type=f32)
    mix = mix + own_weight[..., None] * v_own[:, None, :]
    attn = (mix / total[..., None]).astype(bf16)

    back = exchange(attn.reshape(n_e, per_prompt, q_cols), "expert").reshape(rows, q_cols)
    attn_home = lax.dot_general(
        pick, back, (((0,), (0,)), ((), ())), preferred_element_type=f32
    ).astype(bf16)
    partial = lax.dot_general(
        attn_home, all_out, (((1,), (1,)), ((), ())), preferred_element_type=f32
    ).astype(bf16)
    partial = jnp.transpose(partial.reshape(tokens, n_x, col_width), (1, 0, 2))
    head_total = jnp.sum(exchange(partial, "tensor").astype(f32), 0)
    resid_cols = lax.dynamic_slice_in_dim(residual, pos_x * col_width, col_width, 1)
    hidden = (resid_cols.astype(f32) + head_total).astype(bf16)

    experts = experts_here * n_e
    picks = route_ids.shape[1]
    capacity = min(tokens, 3 * tokens * picks // (2 * experts))
    hit = route_ids[:, :, None] == jnp.arange(experts, dtype=jnp.int32)
    marks = jnp.any(hit, 1)
    mark_weight = jnp.sum(jnp.where(hit, route_weights[:, :, None], 0.0), 1)
    slot = jnp.dot(
        earlier.astype(bf16), marks.astype(bf16), preferred_element_type=f32
    ).astype(jnp.int32)
    slot = jnp.where(marks, slot, -1)
    chosen = slot[:, :, None] == jnp.arange(capacity, dtype=jnp.int32)
    send_rows = chosen.reshape(tokens, experts * capacity).astype(bf16)
    mix_rows = (chosen * mark_weight[:, :, None]).reshape(tokens, experts * capacity)

    outgoing = lax.dot_general(
        send_rows, hidden, (((0,), (0,)), ((), ())), preferred_element_type=f32
    ).astype(bf16)
    arrived = exchange(outgoing.reshape(n_e, experts_here, capacity, col_width), "expert")
    by_expert = jnp.transpose(arrived, (1, 0, 2, 3)).reshape(
        experts_here, n_e * capacity, col_width
    )
    by_dest = jnp.tile(by_expert, (n_x // experts_here, 1, 1))
    rows_in = exchange(by_dest, "tensor")

    own_gate = lax.dynamic_index_in_dim(w_gate, keep, 0, keepdims=False)
    own_up = lax.dynamic_index_in_dim(w_up, keep, 0, keepdims=False)
    own_down = lax.dynamic_index_in_dim(w_down, keep, 0, keepdims=False)

    def project(weight):
        return jnp.einsum(
            "srd,sdf->rf",
            rows_in,
            weight.reshape(n_x, col_width, weight.shape[1]),
            preferred_element_type=f32,
        )

    def act_of(gate, up):
        return (jax.nn.silu(gate) * up).astype(bf16)

    act_own = act_of(project(own_gate), project(own_up))
    act_got = act_of(project(got_up[0]), project(got_up[1]))
    out = jnp.dot(act_own, own_down, preferred_element_type=f32) + jnp.dot(
        act_got, got_down, preferred_element_type=f32
    )
    out = jnp.transpose(out.astype(bf16).reshape(-1, n_x, col_width), (1, 0, 2))
    parts = exchange(out, "tensor")
    parts = parts.reshape(n_x // experts_here, experts_here, n_e, capacity, col_width)
    summed = jnp.sum(parts.astype(f32), 0).astype(bf16)
    returned = exchange(jnp.transpose(summed, (1, 0, 2, 3)), "expert")
    expert_mix = jnp.dot(
        mix_rows,
        returned.reshape(experts * capacity, col_width).astype(f32),
        precision=lax.Precision.HIGHEST,
    )
    return (hidden.astype(f32) + expert_mix).astype(bf16)


def solution(mesh):
    whole = ("groups", "expert")
    return jax.shard_map(
        local,
        mesh=mesh,
        in_specs=(
            P(whole, None),
            P(whole, None),
            P(whole, "tensor", None),
            P(whole),
            P(whole),
            P(whole, None),
            P("tensor", "expert"),
            P(whole, None),
            P(whole, None),
            P("expert", None, "tensor"),
            P("expert", None, "tensor"),
            P("expert", "tensor", None),
        ),
        out_specs=P(whole, "tensor"),
        check_vma=False,
    )
```

time: 457 us -> 276 us (0.60)
  blocking collectives: 211 us -> 23.4 us
  starting transfers between devices: 35.4 us -> 99.1 us
  waiting for transfers between devices: 140 us -> 110 us
  local copies, waits for them, and re-layouts: 31.7 us -> 15 us
  other arithmetic: 11.9 us -> 3.26 us
    all_to_all x4 -> x1, blocking collectives: 112 us -> 23.4 us  [exchange(): return lax.all_to_all(tiles, axis, split_axis=0, concat_axis=0, tiled=True)]
    all_to_all x4 -> x7, starting transfers between devices: 35.4 us -> 93.8 us  [exchange(): return lax.all_to_all(tiles, axis, split_axis=0, concat_axis=0, tiled=True)]
    unnamed x1 -> x0, blocking collectives: 57.1 us -> none
    all_gather x2 -> x0, blocking collectives: 41.9 us -> none  [combined_all(): lax.all_gather(part.astype(kind), axis)]
    all_gather x2 -> x1, waiting for transfers between devices: 46.4 us -> 9.7 us  [local(): all_out = lax.all_gather(out_weight.T, 'expert', axis=0, tiled=True)]
    ppermute x0 -> x2, waiting for transfers between devices: none -> 11.8 us  [the longest x1 9.42 us: local(): lax.ppermute(lax.dynamic_index_in_dim(w_down, give, 0, keepdims=False), '...]
    ppermute x0 -> x2, starting transfers between devices: none -> 5.31 us  [the longest x1 3.08 us: local(): lax.ppermute(lax.dynamic_index_in_dim(w_down, give, 0, keepdims=False), '...]
    all_to_all x4 -> x7, waiting for transfers between devices: 92.4 us -> 87.4 us  [exchange(): return lax.all_to_all(tiles, axis, split_axis=0, concat_axis=0, tiled=True)]
  transfers between devices with their start and end apart: 6 -> 10, of which waited for: 6 -> 10; matrix products, arithmetic and copies ran while one was open for 3% -> 6% of each run, Pallas kernels for 0% -> 0%
where the time goes in v1:
time: 276 us; the launch traced here: 275 us
  waiting for transfers between devices  110 us (40%)
  starting transfers between devices  99.1 us (36%)
  blocking collectives  23.4 us (8%)
  local copies, waits for them, and re-layouts  15 us (5%)
  between operations  14.4 us (5%)
  matrix products  10.3 us (4%)
  other arithmetic  3.26 us (1%)
    all_to_all x7, starting transfers between devices, exchange(): return lax.all_to_all(tiles, axis, split_axis=0, concat_axis=0, tiled=True)  93.8 us
    all_to_all x7, waiting for transfers between devices, exchange(): return lax.all_to_all(tiles, axis, split_axis=0, concat_axis=0, tiled=True)  87.4 us
    all_to_all x1, blocking collectives, exchange(): return lax.all_to_all(tiles, axis, split_axis=0, concat_axis=0, tiled=True)  23.4 us
    all_gather x1, waiting for transfers between devices, local(): all_out = lax.all_gather(out_weight.T, 'expert', axis=0, tiled=True)  9.7 us
    ppermute x1, waiting for transfers between devices, local(): lax.ppermute(lax.dynamic_index_in_dim(w_down, give, 0, keepdims=False), '...  9.42 us
  transfers between devices with their start and end apart: 10, of which 10 were waited for; matrix products, arithmetic and copies ran while one was open for 6% of the time, Pallas kernels for 0%

profile of v1, /device:TPU:65, one launch (start us, length us, event | category | flops | bytes accessed | tf_op | source)
XLA Modules:
  0.0 275.2 jit_solution(10119281844531938049)
XLA Ops:
  6.6 0.7 all-gather.2.cloned.1.call-update
  7.3 0.7 constant_dynamic-slice_fusion.5
  8.1 0.8 constant_dynamic-slice_fusion.6
  8.8 0.9 convert_reduce_fusion.1
  9.7 0.7 multiply_add_fusion
  10.4 0.2 convolution_convert_fusion.2
  10.6 0.7 reshape.119
  11.2 45.2 %all-to-all-start = ((bf16[32,2,768]{2,1,0:T(2,128)(2,1)}), bf16[32,2,768]{2,1,0:T(2,128)(2,1)S(1)}, u32[]{:S(2)}, u32[]{:S(2)}) async-start(bf16[32,2,768]{2,1,0:T(2,128)(2,1)} %reshape.119), calls=%async_computation | async-start | bytes 196608 | tf_op jit(solution)/shard_map/all_to_all | solution.py:11
  57.1 0.9 reshape_squeeze.9
  58.1 13.3 %all-to-all-done = bf16[32,2,768]{2,1,0:T(2,128)(2,1)S(1)} async-done(((bf16[32,2,768]{2,1,0:T(2,128)(2,1)}), bf16[32,2,768]{2,1,0:T(2,128)(2,1)S(1)}, u32[]{:S(2)}, u32[]{:S(2)}) %all-to-all-start) | async-done | bytes 98336 | tf_op jit(solution)/shard_map/all_to_all | solution.py:11
  71.4 0.7 broadcast_in_dim.31
  72.1 6.6 %all-to-all-start.1 = ((bf16[8,32,256]{2,1,0:T(8,128)(2,1)}), bf16[8,32,256]{2,1,0:T(8,128)(2,1)S(1)}, u32[]{:S(2)}, u32[]{:S(2)}) async-start(bf16[8,32,256]{2,1,0:T(8,128)(2,1)} %bitcast.2), calls=%async_computation.1 | async-start | bytes 262144 | tf_op jit(solution)/shard_map/all_to_all | solution.py:11
  78.8 0.1 multiply_reduce_fusion
  78.9 0.1 copy.68
  79.0 7.6 %all-to-all-done.1 = bf16[8,32,256]{2,1,0:T(8,128)(2,1)S(1)} async-done(((bf16[8,32,256]{2,1,0:T(8,128)(2,1)}), bf16[8,32,256]{2,1,0:T(8,128)(2,1)S(1)}, u32[]{:S(2)}, u32[]{:S(2)}) %all-to-all-start.1) | async-done | bytes 131104 | tf_op jit(solution)/shard_map/all_to_all | solution.py:11
  86.6 0.3 fusion.47
  86.9 0.2 fusion.12
  87.1 0.2 fusion.3
  87.4 0.1 copy.69
  87.5 0.7 reshape.125
  88.1 6.5 %all-to-all-start.2 = ((bf16[32,2,512]{2,1,0:T(2,128)(2,1)}), bf16[32,2,512]{2,1,0:T(2,128)(2,1)S(1)}, u32[]{:S(2)}, u32[]{:S(2)}) async-start(bf16[32,2,512]{2,1,0:T(2,128)(2,1)} %reshape.125), calls=%async_computation.2 | async-start | bytes 131072 | tf_op jit(solution)/shard_map/all_to_all | solution.py:11
  94.6 0.1 copy.71
  94.7 14.6 %all-to-all-done.2 = bf16[32,2,512]{2,1,0:T(2,128)(2,1)S(1)} async-done(((bf16[32,2,512]{2,1,0:T(2,128)(2,1)}), bf16[32,2,512]{2,1,0:T(2,128)(2,1)S(1)}, u32[]{:S(2)}, u32[]{:S(2)}) %all-to-all-start.2) | async-done | bytes 65568 | tf_op jit(solution)/shard_map/all_to_all | solution.py:11
  109.4 9.7 %all-gather.2.cloned.1.call-done = bf16[2048,512]{1,0:T(8,128)(2,1)} async-done(((bf16[64,512]{1,0:T(8,128)(2,1)}), bf16[2048,512]{1,0:T(8,128)(2,1)}) %all-gather.2.cloned.1.call-update) | async-done | bytes 2097168 | tf_op jit(solution)/shard_map/all_gather | solution.py:58
  119.1 2.4 convolution_convert_fusion
  121.5 0.7 copy.94
  122.2 6.1 %all-to-all-start.3 = ((bf16[8,32,256]{2,1,0:T(8,128)(2,1)}), bf16[8,32,256]{2,1,0:T(8,128)(2,1)S(1)}, u32[]{:S(2)}, u32[]{:S(2)}) async-start(bf16[8,32,256]{2,1,0:T(8,128)(2,1)} %bitcast.88), calls=%async_computation.3 | async-start | bytes 262144 | tf_op jit(solution)/shard_map/all_to_all | solution.py:11
  128.3 0.1 fusion.16
  128.4 0.1 fusion.8
  128.5 0.1 copy.72
  128.7 0.1 eq.87
  128.8 7.5 %all-to-all-done.3 = bf16[8,32,256]{2,1,0:T(8,128)(2,1)S(1)} async-done(((bf16[8,32,256]{2,1,0:T(8,128)(2,1)}), bf16[8,32,256]{2,1,0:T(8,128)(2,1)S(1)}, u32[]{:S(2)}, u32[]{:S(2)}) %all-to-all-start.3) | async-done | bytes 131104 | tf_op jit(solution)/shard_map/all_to_all | solution.py:11
  136.4 0.7 add_convert_fusion
  137.1 0.2 convolution_convert_fusion.1
  137.3 0.1 reshape.128
  137.4 0.8 copy.75
  138.3 10.2 %all-to-all-start.4 = ((bf16[32,2,6,256]{3,1,2,0:T(2,128)(2,1)}), bf16[32,2,6,256]{3,1,2,0:T(2,128)(2,1)S(1)}, u32[]{:S(2)}, u32[]{:S(2)}) async-start(bf16[32,2,6,256]{3,1,2,0:T(2,128)(2,1)} %copy.75), calls=%async_computation.4 | async-start | bytes 393216 | tf_op jit(solution)/shard_map/all_to_all | solution.py:11
  148.5 2.1 constant_dynamic-slice_fusion
  150.6 0.1 pad_maximum_fusion
  150.7 2.2 collective-permute-start
  152.9 14.0 %all-to-all-done.4 = bf16[32,2,6,256]{3,1,2,0:T(2,128)(2,1)S(1)} async-done(((bf16[32,2,6,256]{3,1,2,0:T(2,128)(2,1)}), bf16[32,2,6,256]{3,1,2,0:T(2,128)(2,1)S(1)}, u32[]{:S(2)}, u32[]{:S(2)}) %all-to-all-start.4) | async-done | bytes 196640 | tf_op jit(solution)/shard_map/all_to_all | solution.py:11
  167.0 1.0 tile.11
  167.9 3.8 %all-to-all-start.5 = ((bf16[8,192,256]{2,1,0:T(8,128)(2,1)}), bf16[8,192,256]{2,1,0:T(8,128)(2,1)S(1)}, u32[]{:S(2)}, u32[]{:S(2)}) async-start(bf16[8,192,256]{2,1,0:T(8,128)(2,1)} %bitcast.10), calls=%async_computation.5 | async-start | bytes 1572864 | tf_op jit(solution)/shard_map/all_to_all | solution.py:11
  171.7 0.9 dynamic-slice_bitcast_fusion
  172.6 3.1 %collective-permute-start.1 = (bf16[128,2048]{1,0:T(8,128)(2,1)}, bf16[128,2048]{1,0:T(8,128)(2,1)}, u32[]{:S(2)}, u32[]{:S(2)}) collective-permute-start(bf16[128,2048]{1,0:T(8,128)(2,1)} %dynamic-slice_bitcast_fusion), channel_id=1, source_target_pairs={{0,1},{1,0},{2,3},{3,2},{4,5},{5,4},{6,7},{7,6},{8,9},{9,8},{10,11... | collective-permute-start | bytes 1572872 | tf_op jit(solution)/shard_map/ppermute | solution.py:55
  175.7 2.4 collective-permute-done
  178.0 2.1 fusion.45
  180.1 12.3 %all-to-all-done.5 = bf16[8,192,256]{2,1,0:T(8,128)(2,1)S(1)} async-done(((bf16[8,192,256]{2,1,0:T(8,128)(2,1)}), bf16[8,192,256]{2,1,0:T(8,128)(2,1)S(1)}, u32[]{:S(2)}, u32[]{:S(2)}) %all-to-all-start.5) | async-done | bytes 786464 | tf_op jit(solution)/shard_map/all_to_all | solution.py:11
  192.4 1.0 convolution_bitcast_fusion
  193.4 0.3 convolution_bitcast_fusion.3
  193.7 1.7 fusion.6
  195.4 9.4 %collective-permute-done.1 = bf16[128,2048]{1,0:T(8,128)(2,1)} collective-permute-done((bf16[128,2048]{1,0:T(8,128)(2,1)}, bf16[128,2048]{1,0:T(8,128)(2,1)}, u32[]{:S(2)}, u32[]{:S(2)}) %collective-permute-start.1) | collective-permute-done | bytes 524320 | tf_op jit(solution)/shard_map/ppermute | solution.py:55
  204.9 2.8 %fusion = bf16[192,2048]{1,0:T(8,128)(2,1)} fusion(f32[192,2048]{1,0:T(8,128)S(1)} %fusion.6, bf16[128,2048]{1,0:T(8,128)(2,1)} %collective-permute-done.1, f32[192,128]{1,0:T(8,128)} %convolution_bitcast_fusion, bf16[8,192,256]{2,1,0:T(8,128)(2,1)S(1)} %all-to-all-done.5, bf16[8,256,128]{2,1,0:T(8,128)(2,1)} %bitcast.97), kind=kOutput, calls=%fused_computation.1 | convolution fusion | flops 202260480 | bytes 4292608 | tf_op jit(solution)/shard_map/dot_general | solution.py:154
  207.7 1.2 copy.93
  208.9 23.4 %all_to_all.40 = bf16[8,192,256]{2,1,0:T(8,128)(2,1)S(1)} all-to-all(bf16[8,192,256]{2,1,0:T(8,128)(2,1)S(1)} %bitcast.93), channel_id=1, replica_groups=mesh['groups'=2,'expert'=32,'tensor'=8] {'tensor'}, dimensions={0} | all-to-all | bytes 1572864 | tf_op jit(solution)/shard_map/all_to_all | solution.py:11
  232.3 0.2 reduce.1
  232.5 0.9 copy.80
  233.4 15.4 %all-to-all-start.7 = ((bf16[32,2,6,256]{3,1,2,0:T(2,128)(2,1)}), bf16[32,2,6,256]{3,1,2,0:T(2,128)(2,1)S(1)}, u32[]{:S(2)}, u32[]{:S(2)}) async-start(bf16[32,2,6,256]{3,1,2,0:T(2,128)(2,1)} %bitcast.24), calls=%async_computation.7 | async-start | bytes 393216 | tf_op jit(solution)/shard_map/all_to_all | solution.py:11
  248.8 0.1 copy.73
  248.9 0.1 select_reduce_fusion
  249.0 0.1 copy.74
  249.2 18.1 %all-to-all-done.7 = bf16[32,2,6,256]{3,1,2,0:T(2,128)(2,1)S(1)} async-done(((bf16[32,2,6,256]{3,1,2,0:T(2,128)(2,1)}), bf16[32,2,6,256]{3,1,2,0:T(2,128)(2,1)S(1)}, u32[]{:S(2)}, u32[]{:S(2)}) %all-to-all-start.7) | async-done | bytes 196640 | tf_op jit(solution)/shard_map/all_to_all | solution.py:11
  267.3 0.1 reshape.133
  267.4 0.9 fusion.7
  (31 shorter events, 0.5 us)
Async XLA Ops:
  6.5 165.2 %copy-start = (bf16[2,128,2048]{2,1,0:T(8,128)(2,1)S(1)}, bf16[2,128,2048]{2,1,0:T(8,128)(2,1)}, u32[]{:S(2)}) copy-start(bf16[2,128,2048]{2,1,0:T(8,128)(2,1)} %param.23) | copy-start | bytes 3145732
  6.6 112.5 %all-gather.2.cloned.1.call-start = ((), (), s32[]{:S(2)}) async-start(), calls=%async_computation.8 | async-start | bytes 2162688 | tf_op jit(solution)/shard_map/all_gather | solution.py:58
  11.2 60.2 %all-to-all-start = ((bf16[32,2,768]{2,1,0:T(2,128)(2,1)}), bf16[32,2,768]{2,1,0:T(2,128)(2,1)S(1)}, u32[]{:S(2)}, u32[]{:S(2)}) async-start(bf16[32,2,768]{2,1,0:T(2,128)(2,1)} %reshape.119), calls=%async_computation | async-start | bytes 196608 | tf_op jit(solution)/shard_map/all_to_all | solution.py:11
  72.1 22.6 %copy-start.4 = (s32[32,8]{0,1:T(8,128)S(1)}, s32[32,8]{0,1:T(8,128)}, u32[]{:S(2)}) copy-start(s32[32,8]{0,1:T(8,128)} %param.19) | copy-start | bytes 3076
  72.1 14.6 %all-to-all-start.1 = ((bf16[8,32,256]{2,1,0:T(8,128)(2,1)}), bf16[8,32,256]{2,1,0:T(8,128)(2,1)S(1)}, u32[]{:S(2)}, u32[]{:S(2)}) async-start(bf16[8,32,256]{2,1,0:T(8,128)(2,1)} %bitcast.2), calls=%async_computation.1 | async-start | bytes 262144 | tf_op jit(solution)/shard_map/all_to_all | solution.py:11
  88.1 21.2 %all-to-all-start.2 = ((bf16[32,2,512]{2,1,0:T(2,128)(2,1)}), bf16[32,2,512]{2,1,0:T(2,128)(2,1)S(1)}, u32[]{:S(2)}, u32[]{:S(2)}) async-start(bf16[32,2,512]{2,1,0:T(2,128)(2,1)} %reshape.125), calls=%async_computation.2 | async-start | bytes 131072 | tf_op jit(solution)/shard_map/all_to_all | solution.py:11
  122.2 26.3 %copy-start.1 = (bf16[2,2048,128]{2,1,0:T(8,128)(2,1)S(1)}, bf16[2,2048,128]{2,1,0:T(8,128)(2,1)}, u32[]{:S(2)}) copy-start(bf16[2,2048,128]{2,1,0:T(8,128)(2,1)} %param.22) | copy-start | bytes 3145732
  122.2 14.2 %all-to-all-start.3 = ((bf16[8,32,256]{2,1,0:T(8,128)(2,1)}), bf16[8,32,256]{2,1,0:T(8,128)(2,1)S(1)}, u32[]{:S(2)}, u32[]{:S(2)}) async-start(bf16[8,32,256]{2,1,0:T(8,128)(2,1)} %bitcast.88), calls=%async_computation.3 | async-start | bytes 262144 | tf_op jit(solution)/shard_map/all_to_all | solution.py:11
  137.1 13.5 %copy-start.2 = (bf16[32,256]{1,0:T(8,128)(2,1)}, bf16[32,256]{1,0:T(8,128)(2,1)S(1)}, u32[]{:S(2)}) copy-start(bf16[32,256]{1,0:T(8,128)(2,1)S(1)} %add_convert_fusion) | copy-start | bytes 49156
  138.3 28.7 %all-to-all-start.4 = ((bf16[32,2,6,256]{3,1,2,0:T(2,128)(2,1)}), bf16[32,2,6,256]{3,1,2,0:T(2,128)(2,1)S(1)}, u32[]{:S(2)}, u32[]{:S(2)}) async-start(bf16[32,2,6,256]{3,1,2,0:T(2,128)(2,1)} %copy.75), calls=%async_computation.4 | async-start | bytes 393216 | tf_op jit(solution)/shard_map/all_to_all | solution.py:11
  150.7 27.3 %collective-permute-start = (bf16[2,2048,128]{2,1,0:T(8,128)(2,1)S(1)}, bf16[2,2048,128]{2,1,0:T(8,128)(2,1)}, u32[]{:S(2)}, u32[]{:S(2)}) collective-permute-start(bf16[2,2048,128]{2,1,0:T(8,128)(2,1)S(1)} %pad_maximum_fusion), channel_id=1, source_target_pairs={{0,1},{1,0},{2,3},{3,2},{4,5},{5,4},{6,7},{7,6},{8,9},{9,8},{10,11... | collective-permute-start | bytes 3145736 | tf_op jit(solution)/shard_map/ppermute | solution.py:54
  167.9 24.4 %all-to-all-start.5 = ((bf16[8,192,256]{2,1,0:T(8,128)(2,1)}), bf16[8,192,256]{2,1,0:T(8,128)(2,1)S(1)}, u32[]{:S(2)}, u32[]{:S(2)}) async-start(bf16[8,192,256]{2,1,0:T(8,128)(2,1)} %bitcast.10), calls=%async_computation.5 | async-start | bytes 1572864 | tf_op jit(solution)/shard_map/all_to_all | solution.py:11
  172.6 32.3 %collective-permute-start.1 = (bf16[128,2048]{1,0:T(8,128)(2,1)}, bf16[128,2048]{1,0:T(8,128)(2,1)}, u32[]{:S(2)}, u32[]{:S(2)}) collective-permute-start(bf16[128,2048]{1,0:T(8,128)(2,1)} %dynamic-slice_bitcast_fusion), channel_id=1, source_target_pairs={{0,1},{1,0},{2,3},{3,2},{4,5},{5,4},{6,7},{7,6},{8,9},{9,8},{10,11... | collective-permute-start | bytes 1572872 | tf_op jit(solution)/shard_map/ppermute | solution.py:55
  208.9 39.9 %copy-start.5 = (f32[32,8]{0,1:T(8,128)S(1)}, f32[32,8]{0,1:T(8,128)}, u32[]{:S(2)}) copy-start(f32[32,8]{0,1:T(8,128)} %param.20) | copy-start | bytes 3076
  232.3 35.1 %copy-start.3 = (bf16[32,256]{1,0:T(8,128)(2,1)S(1)}, bf16[32,256]{1,0:T(8,128)(2,1)}, u32[]{:S(2)}) copy-start(bf16[32,256]{1,0:T(8,128)(2,1)} %copy-done.2) | copy-start | bytes 49156
  233.4 33.9 %all-to-all-start.7 = ((bf16[32,2,6,256]{3,1,2,0:T(2,128)(2,1)}), bf16[32,2,6,256]{3,1,2,0:T(2,128)(2,1)S(1)}, u32[]{:S(2)}, u32[]{:S(2)}) async-start(bf16[32,2,6,256]{3,1,2,0:T(2,128)(2,1)} %bitcast.24), calls=%async_computation.7 | async-start | bytes 393216 | tf_op jit(solution)/shard_map/all_to_all | solution.py:11
Sparse Core Ops, SparseCore 0:
  9.5 109.5 all-gather.1

commit v2 on v1

v2 whole, which is shorter than its diff:
```python
import jax
import jax.numpy as jnp
from jax import lax
from jax.experimental import pallas as pl
from jax.experimental.pallas import tpu as pltpu
from jax.sharding import Mesh
from jax.sharding import PartitionSpec as P

HD = 128
CORES = 2
EXPERT = ("chip", "core")
MASKED_SCORE = -1e30
f32, bf16, i32 = jnp.float32, jnp.bfloat16, jnp.int32


def exchange(tiles, axis):
    return lax.all_to_all(tiles, axis, split_axis=0, concat_axis=0, tiled=True)


def from_chip(x, shift):
    n = lax.axis_size("chip")
    return lax.ppermute(x, "chip", [(i, (i - shift) % n) for i in range(n)])


def other_core(x):
    return lax.ppermute(x, "core", [(0, 1), (1, 0)])


def count_earlier(marks):
    n = marks.shape[-1]
    before = (jnp.arange(n)[:, None] < jnp.arange(n)[None, :]).astype(bf16)
    return jnp.dot(marks.astype(bf16), before, preferred_element_type=f32).astype(i32)


def pick_rows(index, rows):
    chosen = (index[:, None] == jnp.arange(rows.shape[0], dtype=i32)).astype(bf16)
    return jnp.dot(chosen, rows, preferred_element_type=f32).astype(bf16)


def projection_kernel(at, attn, mine, theirs, out):
    chips = mine.shape[0]
    quarter = chips // 4
    first = at[1] == 0
    rows = attn[...]
    per_out = out.shape[2] // (2 * mine.shape[1])
    for dest in range(out.shape[0]):
        blocks = []
        for near in range(per_out):
            m = lax.rem(dest * per_out + near + chips - at[0], chips)
            k, kind = lax.div(m, 4), lax.rem(m, 4)
            place = jnp.where(kind == 1, quarter + k, k)
            place = jnp.where(kind == 2, 3 * quarter + k, place)
            place = jnp.where(kind == 3, 2 * quarter + lax.rem(k + 1, quarter), place)
            a, b = mine[place], theirs[place]
            blocks += [jnp.where(first, a, b), jnp.where(first, b, a)]
        weight = jnp.concatenate(blocks, 0)
        out[dest] = lax.dot_general(
            rows, weight, (((1,), (1,)), ((), ())), preferred_element_type=f32
        ).astype(bf16)


def project_out(chip, core, attn, mine, theirs, n_x, col_width):
    vmem = pl.BlockSpec(memory_space=pltpu.VMEM)
    flops = 2 * attn.shape[0] * 2 * mine.size
    return pl.pallas_call(
        projection_kernel,
        out_shape=jax.ShapeDtypeStruct((n_x, attn.shape[0], col_width), bf16),
        in_specs=[pl.BlockSpec(memory_space=pltpu.SMEM), vmem, vmem, vmem],
        out_specs=vmem,
        cost_estimate=pl.CostEstimate(
            flops=flops, bytes_accessed=4 * mine.size, transcendentals=0
        ),
        compiler_params=pltpu.CompilerParams(vmem_limit_bytes=8 << 20),
        name="project_out",
    )(jnp.stack([chip, core]).astype(i32), attn, mine, theirs)


def expert_kernel(keep, rows, gate, up, down, got_up, got_down, out):
    n_x, count, col_width = rows.shape
    ff = gate.shape[2]
    total = jnp.zeros((count, 4 * ff), f32)
    for s in range(n_x):
        at = pl.ds(s * col_width, col_width)
        weight = jnp.concatenate(
            [gate[0, at, :], got_up[0, at, :], up[0, at, :], got_up[1, at, :]], 1
        )
        total = total + jnp.dot(rows[s], weight, preferred_element_type=f32)
    gates, ups = total[:, : 2 * ff], total[:, 2 * ff :]
    act = (gates / (1.0 + jnp.exp(-gates)) * ups).astype(bf16)
    for d in range(n_x):
        at = pl.ds(d * col_width, col_width)
        weight = jnp.concatenate([down[0, :, at], got_down[:, at]], 0)
        out[d] = jnp.dot(act, weight, preferred_element_type=f32).astype(bf16)


def run_expert(keep, rows, gate, up, down, got_up, got_down):
    def whole(x):
        return pl.BlockSpec(x.shape, lambda i, k: (0,) * x.ndim)

    def kept(x):
        return pl.BlockSpec((1, *x.shape[1:]), lambda i, k: (k[0], 0, 0))

    flops = 2 * rows.size * got_up.shape[2] * 4 + 2 * rows.size * got_down.shape[0] * 2
    moved = 2 * (2 * rows.size + got_up.size + got_down.size) + 3 * gate.size
    return pl.pallas_call(
        expert_kernel,
        out_shape=jax.ShapeDtypeStruct(rows.shape, bf16),
        grid_spec=pltpu.PrefetchScalarGridSpec(
            num_scalar_prefetch=1,
            grid=(1,),
            in_specs=[
                whole(rows),
                kept(gate),
                kept(up),
                kept(down),
                whole(got_up),
                whole(got_down),
            ],
            out_specs=whole(rows),
        ),
        cost_estimate=pl.CostEstimate(
            flops=flops, bytes_accessed=moved, transcendentals=rows.shape[1] * 2 * HD
        ),
        compiler_params=pltpu.CompilerParams(vmem_limit_bytes=16 << 20),
        name="run_expert",
    )(jnp.reshape(keep, (1,)).astype(i32), rows, gate, up, down, got_up, got_down)


def layer(
    queries,
    own_kv,
    prompt_cache,
    prompt_len,
    token_prompt,
    residual,
    out_weight,
    route_ids,
    route_weights,
    w_gate,
    w_up,
    w_down,
):
    n_e = lax.axis_size(EXPERT)
    n_x = lax.axis_size("tensor")
    chips = lax.axis_size("chip")
    pos_x = lax.axis_index("tensor")
    chip = lax.axis_index("chip")
    core = lax.axis_index("core")
    pos_e = chip * CORES + core
    tokens = queries.shape[0]
    half_cols = own_kv.shape[1] // 2
    kv_heads = half_cols // HD
    head_count = queries.shape[1] // HD
    group_size = head_count // kv_heads
    heads_here = head_count // n_x
    q_cols = heads_here * HD
    per_prompt = tokens // (n_e // 2)
    block_len = prompt_cache.shape[1]
    model_width = residual.shape[1]
    col_width = model_width // n_x
    picks = route_ids.shape[1]
    experts_here = w_gate.shape[0]
    experts = experts_here * n_e
    capacity = min(tokens, 3 * tokens * picks // (2 * experts))

    cache = prompt_cache[0].reshape(block_len, 2, kv_heads, HD)
    by_head = jnp.transpose(cache, (2, 0, 1, 3)).reshape(kv_heads, block_len, 2 * HD)
    by_head = jnp.repeat(by_head, n_x // kv_heads, axis=0)
    cache_all = exchange(by_head, "tensor")
    cache_all = cache_all.reshape(n_x * block_len, 2 * HD)

    w_own = out_weight.T
    far = from_chip(w_own, chips // 2)
    ahead = from_chip(w_own, chips // 4)
    behind = from_chip(w_own, -(chips // 4))
    quarter = jnp.stack([w_own, ahead, far, behind])
    next_one = from_chip(quarter, 1)
    last_one = from_chip(quarter, -1)
    next_two = from_chip(quarter[:2], 2)
    last_two = from_chip(jnp.stack([quarter[3], quarter[0]]), -2)
    mine = jnp.concatenate([quarter, next_one, last_one, next_two, last_two])
    theirs = other_core(mine)

    kv_pos = (pos_x * heads_here) // group_size
    payload = jnp.concatenate(
        [
            lax.dynamic_slice_in_dim(queries, pos_x * q_cols, q_cols, 1),
            lax.dynamic_slice_in_dim(own_kv, kv_pos * HD, HD, 1),
            lax.dynamic_slice_in_dim(own_kv, half_cols + kv_pos * HD, HD, 1),
            lax.dynamic_slice_in_dim(residual, pos_x * col_width, col_width, 1),
        ],
        1,
    )
    width = payload.shape[1]
    same = token_prompt[:, None] == token_prompt[None, :]
    earlier = jnp.arange(tokens)[None, :] < jnp.arange(tokens)[:, None]
    rank = jnp.sum((same & earlier).astype(i32), 1)
    place = token_prompt * per_prompt + rank
    rows = n_e * per_prompt
    pick = (jnp.arange(rows)[:, None] == place[None, :]).astype(bf16)
    sent = jnp.dot(pick, payload, preferred_element_type=f32).astype(bf16)
    table = jnp.concatenate([token_prompt, route_ids.reshape(-1)]).astype(bf16)
    entries = table.shape[0]
    table_cols = -(-entries // (per_prompt * HD)) * HD
    table = jnp.pad(table, (0, per_prompt * table_cols - entries))
    table = jnp.broadcast_to(
        table.reshape(1, per_prompt, table_cols), (n_e, per_prompt, table_cols)
    )
    sent = jnp.concatenate([sent.reshape(n_e, per_prompt, width), table], 2)
    sent, cache_all = lax.optimization_barrier((sent, cache_all))
    keys, values = cache_all[:, :HD], cache_all[:, HD:]
    got = exchange(sent, EXPERT)
    table = got[:, :, width:].reshape(n_e, per_prompt * table_cols)[:, :entries].astype(i32)
    prompts = table[:, :tokens]
    routes = table[:, tokens:].reshape(n_e, tokens, picks)

    owner = jnp.arange(n_e, dtype=i32)
    holds = jnp.any(prompts[None, :, :] == owner[:, None, None], -1)
    order = count_earlier(holds)
    peers = prompts[:, :, None] == prompts[:, None, :]
    rank_all = jnp.sum((peers & earlier[None]).astype(i32), 2)
    block_order = jnp.sum(
        jnp.where(prompts[:, :, None] == owner, order.T[:, None, :], 0), 2
    )
    source = jnp.where(prompts % CORES == core, 0, chips) + prompts // CORES
    source = source * tokens + block_order * per_prompt + rank_all

    own_holds = jnp.any(prompts == pos_e, 1)
    own_order = count_earlier(own_holds[None])[0]
    slot_here = own_order[:, None] * per_prompt + jnp.arange(per_prompt, dtype=i32)
    slot_here = jnp.where(own_holds[:, None], slot_here, -1).reshape(rows)
    compact = (jnp.arange(tokens, dtype=i32)[:, None] == slot_here[None, :]).astype(bf16)
    got = jnp.dot(
        compact, got[:, :, :width].reshape(rows, width), preferred_element_type=f32
    ).astype(bf16)

    q_rows = got[:, :q_cols].reshape(tokens, heads_here, HD)
    k_own = got[:, q_cols : q_cols + HD].astype(f32)
    v_own = got[:, q_cols + HD : q_cols + 2 * HD].astype(f32)
    resid = got[:, q_cols + 2 * HD :].astype(f32)
    scale = HD ** (-0.5)
    scores = jnp.einsum("rhd,pd->rhp", q_rows, keys, preferred_element_type=f32) * scale
    own = jnp.sum(q_rows.astype(f32) * k_own[:, None, :], -1) * scale
    inside = jnp.arange(n_x * block_len) < prompt_len[0]
    scores = jnp.where(inside, scores, MASKED_SCORE)
    top = jnp.maximum(jnp.max(scores, -1), own)
    weights = jnp.where(inside, jnp.exp(scores - top[..., None]), 0.0)
    own_weight = jnp.exp(own - top)
    total = jnp.sum(weights, -1) + own_weight
    mix = jnp.einsum("rhp,pd->rhd", weights.astype(bf16), values, preferred_element_type=f32)
    mix = mix + own_weight[..., None] * v_own[:, None, :]
    attn = (mix / total[..., None]).astype(bf16).reshape(tokens, q_cols)

    partial = project_out(chip, core, attn, mine, theirs, n_x, col_width)
    parts = exchange(partial, "tensor")
    hidden = (resid + jnp.sum(parts.astype(f32), 0)).astype(bf16)

    keep = pos_x % experts_here
    give = 1 - keep
    swap = [(i, i ^ 1) for i in range(n_x)]
    up_pair = jnp.stack(
        [
            lax.dynamic_index_in_dim(w_gate, give, 0, keepdims=False),
            lax.dynamic_index_in_dim(w_up, give, 0, keepdims=False),
        ]
    )
    got_up = lax.ppermute(up_pair, "tensor", swap)
    down = lax.dynamic_index_in_dim(w_down, give, 0, keepdims=False)
    got_down = lax.ppermute(down, "tensor", swap)

    near = exchange(jnp.broadcast_to(hidden, (chips, *hidden.shape)), "chip")
    across = other_core(near)
    everyone = jnp.concatenate([near, across], 0).reshape(n_e * tokens, col_width)
    mine_e = pos_e * experts_here + jnp.arange(experts_here, dtype=i32)
    named = jnp.any(routes[None] == mine_e[:, None, None, None], -1)
    slot = jnp.where(named, count_earlier(named), -1)
    filled = slot[:, :, None, :] == jnp.arange(capacity, dtype=i32)[None, None, :, None]
    expert_rows = jnp.sum(jnp.where(filled, source[None, :, None, :] + 1, 0), -1) - 1
    home_rows = lax.dynamic_index_in_dim(source, pos_e, 0, keepdims=False)
    hidden_home = pick_rows(home_rows, everyone)
    by_expert = pick_rows(expert_rows.reshape(-1), everyone)
    by_expert = by_expert.reshape(experts_here, n_e * capacity, col_width)
    by_dest = jnp.tile(by_expert, (n_x // experts_here, 1, 1))
    rows_in = exchange(by_dest, "tensor")

    out = run_expert(keep, rows_in, w_gate, w_up, w_down, got_up, got_down)
    parts = exchange(out, "tensor")
    parts = parts.reshape(n_x // experts_here, experts_here, n_e, capacity, col_width)
    summed = jnp.sum(parts.astype(f32), 0).astype(bf16)
    returned = exchange(jnp.transpose(summed, (1, 0, 2, 3)), EXPERT)

    hit = route_ids[:, :, None] == jnp.arange(experts, dtype=i32)
    marks = jnp.any(hit, 1)
    mark_weight = jnp.sum(jnp.where(hit, route_weights[:, :, None], 0.0), 1)
    slot = jnp.dot(
        earlier.astype(bf16), marks.astype(bf16), preferred_element_type=f32
    ).astype(i32)
    slot = jnp.where(marks, slot, -1)
    chosen = slot[:, :, None] == jnp.arange(capacity, dtype=i32)
    mix_rows = (chosen * mark_weight[:, :, None]).reshape(tokens, experts * capacity)
    expert_mix = jnp.dot(
        mix_rows,
        returned.reshape(experts * capacity, col_width).astype(f32),
        precision=lax.Precision.HIGHEST,
    )
    return (hidden_home.astype(f32) + expert_mix).astype(bf16)


def solution(mesh):
    split = Mesh(
        mesh.devices.reshape(
            mesh.shape["groups"],
            mesh.shape["expert"] // CORES,
            CORES,
            mesh.shape["tensor"],
        ),
        ("groups", *EXPERT, "tensor"),
    )
    whole = ("groups", *EXPERT)
    return jax.shard_map(
        layer,
        mesh=split,
        in_specs=(
            P(whole, None),
            P(whole, None),
            P(whole, "tensor", None),
            P(whole),
            P(whole),
            P(whole, None),
            P("tensor", EXPERT),
            P(whole, None),
            P(whole, None),
            P(EXPERT, None, "tensor"),
            P(EXPERT, None, "tensor"),
            P(EXPERT, "tensor", None),
        ),
        out_specs=P(whole, "tensor"),
        check_vma=False,
    )
```

time: 276 us -> 281 us (1.018)
  starting transfers between devices: 99.1 us -> 132 us
  blocking collectives: 23.4 us -> 0 us
  between operations: 14.4 us -> 1.3 us
  waiting for transfers between devices: 110 us -> 120 us
  matrix products: 10.3 us -> 2.93 us
  Pallas kernels: 0 us -> 3.7 us
    ppermute x2 -> x11, starting transfers between devices: 5.31 us -> 82 us  [the longest x7 64.7 us: from_chip(): return lax.ppermute(x, 'chip', [(i, (i - shift) % n) for i in range(n)])]
    all_to_all x7, starting transfers between devices: 93.8 us -> 50.1 us  [exchange(): return lax.all_to_all(tiles, axis, split_axis=0, concat_axis=0, tiled=True)]
    ppermute x2 -> x11, waiting for transfers between devices: 11.8 us -> 47.2 us  [the longest x1 46.6 us: layer(): got_down = lax.ppermute(down, 'tensor', swap)]
    all_to_all x1 -> x0, blocking collectives: 23.4 us -> none  [exchange(): return lax.all_to_all(tiles, axis, split_axis=0, concat_axis=0, tiled=True)]
    all_to_all x7, waiting for transfers between devices: 87.4 us -> 72.9 us  [exchange(): return lax.all_to_all(tiles, axis, split_axis=0, concat_axis=0, tiled=True)]
    all_gather x1 -> x0, waiting for transfers between devices: 9.7 us -> none  [local(): all_out = lax.all_gather(out_weight.T, 'expert', axis=0, tiled=True)]
    dot_general x11, matrix products: 10.3 us -> 2.93 us  [the longest x1 0.93 us: layer(): jnp.dot(mix_rows, returned.reshape(experts * capacity, col_width).astype(...]
    unnamed x15 -> x41, local copies, waits for them, and re-layouts: 1.05 us -> 7.25 us
  transfers between devices with their start and end apart: 10 -> 18, of which waited for: 10 -> 7; matrix products, arithmetic and copies ran while one was open for 6% -> 4% of each run, Pallas kernels for 0% -> 0%
where the time goes in v2:
time: 281 us; the launch traced here: 279 us
  starting transfers between devices  132 us (47%)
  waiting for transfers between devices  120 us (43%)
  local copies, waits for them, and re-layouts  13.7 us (5%)
  other arithmetic  5.49 us (2%)
  Pallas kernels  3.7 us (1%)
  matrix products  2.93 us (1%)
    all_to_all x7, waiting for transfers between devices, exchange(): return lax.all_to_all(tiles, axis, split_axis=0, concat_axis=0, tiled=True)  72.9 us
    ppermute x7, starting transfers between devices, from_chip(): return lax.ppermute(x, 'chip', [(i, (i - shift) % n) for i in range(n)])  64.7 us
    all_to_all x7, starting transfers between devices, exchange(): return lax.all_to_all(tiles, axis, split_axis=0, concat_axis=0, tiled=True)  50.1 us
    ppermute x1, waiting for transfers between devices, layer(): got_down = lax.ppermute(down, 'tensor', swap)  46.6 us
    ppermute x2, starting transfers between devices, other_core(): return lax.ppermute(x, 'core', [(0, 1), (1, 0)])  11.8 us
    unnamed x41, local copies, waits for them, and re-layouts  7.25 us
  transfers between devices with their start and end apart: 18, of which 7 were waited for; matrix products, arithmetic and copies ran while one was open for 4% of the time, Pallas kernels for 0%

profile of v2, /device:TPU:65, one launch (start us, length us, event | category | flops | bytes accessed | tf_op | source)
XLA Modules:
  0.0 279.3 jit_solution(3208541623122977414)
XLA Ops:
  0.0 39.5 %collective-permute-start = (bf16[64,512]{1,0:T(8,128)(2,1)}, bf16[64,512]{1,0:T(8,128)(2,1)S(1)}, u32[]{:S(2)}, u32[]{:S(2)}) collective-permute-start(bf16[64,512]{1,0:T(8,128)(2,1)} %bitcast.81), channel_id=1, source_target_pairs={{0,192},{16,208},{32,224},{48,240},{64,0},{80,16},{96,32},{112,48}... | collective-permute-start | bytes 196616 | tf_op jit(solution)/shard_map/ppermute | solution.py:22
  39.5 2.0 collective-permute-start.1
  41.5 7.0 %collective-permute-start.2 = (bf16[64,512]{1,0:T(8,128)(2,1)}, bf16[64,512]{1,0:T(8,128)(2,1)S(1)}, u32[]{:S(2)}, u32[]{:S(2)}) collective-permute-start(bf16[64,512]{1,0:T(8,128)(2,1)} %bitcast.83), channel_id=1, source_target_pairs={{0,64},{16,80},{32,96},{48,112},{64,128},{80,144},{96,160},{112,17... | collective-permute-start | bytes 196616 | tf_op jit(solution)/shard_map/ppermute | solution.py:22
  48.5 0.9 reshape_squeeze.3
  49.5 0.7 broadcast_in_dim.79
  50.2 7.0 %all-to-all-start = ((bf16[8,32,256]{2,1,0:T(8,128)(2,1)}), bf16[8,32,256]{2,1,0:T(8,128)(2,1)S(1)}, u32[]{:S(2)}, u32[]{:S(2)}) async-start(bf16[8,32,256]{2,1,0:T(8,128)(2,1)} %bitcast.1), calls=%async_computation | async-start | bytes 262144 | tf_op jit(solution)/shard_map/all_to_all | solution.py:17
  57.2 0.8 constant_dynamic-update-slice_fusion.7
  58.1 0.7 convert.9
  59.0 0.2 convert_reduce_fusion.2
  59.3 0.7 constant_dynamic-slice_fusion.3
  60.0 0.7 constant_dynamic-slice_fusion.5
  60.7 0.2 convolution_convert_fusion
  61.6 0.8 pad_maximum_fusion.3
  62.6 7.4 %collective-permute-start.3 = (bf16[4,64,512]{2,1,0:T(8,128)(2,1)S(1)}, bf16[4,64,512]{2,1,0:T(8,128)(2,1)S(1)}, u32[]{:S(2)}, u32[]{:S(2)}) collective-permute-start(bf16[4,64,512]{2,1,0:T(8,128)(2,1)S(1)} %pad_maximum_fusion.2), channel_id=1, source_target_pairs={{0,240},{16,0},{32,16},{48,32},{64,48},{80,64},{96,80},{112,96},{1... | collective-permute-start | bytes 786440 | tf_op jit(solution)/shard_map/ppermute | solution.py:22
  70.0 2.0 collective-permute-start.4
  72.0 3.1 %collective-permute-start.5 = (bf16[2,64,512]{2,1,0:T(8,128)(2,1)S(1)}, bf16[2,64,512]{2,1,0:T(8,128)(2,1)S(1)}, u32[]{:S(2)}, u32[]{:S(2)}) collective-permute-start(bf16[2,64,512]{2,1,0:T(8,128)(2,1)S(1)} %get-tuple-element.16), channel_id=1, source_target_pairs={{0,224},{16,240},{32,0},{48,16},{64,32},{80,48},{96,64},{112,80},{... | collective-permute-start | bytes 393224 | tf_op jit(solution)/shard_map/ppermute | solution.py:22
  75.1 3.7 %collective-permute-start.6 = (bf16[2,64,512]{2,1,0:T(8,128)(2,1)S(1)}, bf16[2,64,512]{2,1,0:T(8,128)(2,1)S(1)}, u32[]{:S(2)}, u32[]{:S(2)}) collective-permute-start(bf16[2,64,512]{2,1,0:T(8,128)(2,1)S(1)} %get-tuple-element.15), channel_id=1, source_target_pairs={{0,32},{16,48},{32,64},{48,80},{64,96},{80,112},{96,128},{112,144}... | collective-permute-start | bytes 393224 | tf_op jit(solution)/shard_map/ppermute | solution.py:22
  78.9 15.8 %all-to-all-start.1 = ((bf16[32,2,1280]{2,1,0:T(2,128)(2,1)}), bf16[32,2,1280]{2,1,0:T(2,128)(2,1)S(1)}, u32[]{:S(2)}, u32[]{:S(2)}) async-start(bf16[32,2,1280]{2,1,0:T(2,128)(2,1)} %pad_maximum_fusion.3), calls=%async_computation.1 | async-start | bytes 327680 | tf_op jit(solution)/shard_map/all_to_all | solution.py:17
  94.9 2.6 collective-permute-start.7
  97.5 14.2 %all-to-all-done.1 = bf16[32,2,1280]{2,1,0:T(2,128)(2,1)S(1)} async-done(((bf16[32,2,1280]{2,1,0:T(2,128)(2,1)}), bf16[32,2,1280]{2,1,0:T(2,128)(2,1)S(1)}, u32[]{:S(2)}, u32[]{:S(2)}) %all-to-all-start.1) | async-done | bytes 163872 | tf_op jit(solution)/shard_map/all_to_all | solution.py:17
  112.1 0.1 fusion.11
  112.4 0.1 convolution_convert_fusion.1
  112.8 0.3 fusion.59
  113.1 0.2 fusion.16
  113.2 0.2 fusion.5
  113.5 1.9 project_out.1
  115.4 6.9 %all-to-all-start.2 = ((bf16[8,32,256]{2,1,0:T(8,128)(2,1)}), bf16[8,32,256]{2,1,0:T(8,128)(2,1)S(1)}, u32[]{:S(2)}, u32[]{:S(2)}) async-start(bf16[8,32,256]{2,1,0:T(8,128)(2,1)} %project_out.1), calls=%async_computation.2 | async-start | bytes 262144 | tf_op jit(solution)/shard_map/all_to_all | solution.py:17
  122.5 0.1 copy.89
  122.7 7.6 %all-to-all-done.2 = bf16[8,32,256]{2,1,0:T(8,128)(2,1)S(1)} async-done(((bf16[8,32,256]{2,1,0:T(8,128)(2,1)}), bf16[8,32,256]{2,1,0:T(8,128)(2,1)S(1)}, u32[]{:S(2)}, u32[]{:S(2)}) %all-to-all-start.2) | async-done | bytes 131104 | tf_op jit(solution)/shard_map/all_to_all | solution.py:17
  130.3 0.7 broadcast_in_dim.140
  131.1 4.1 %all-to-all-start.3 = ((bf16[16,32,256]{2,1,0:T(8,128)(2,1)}), bf16[16,32,256]{2,1,0:T(8,128)(2,1)S(1)}, u32[]{:S(2)}, u32[]{:S(2)}) async-start(bf16[16,32,256]{2,1,0:T(8,128)(2,1)} %broadcast_in_dim.140), calls=%async_computation.3 | async-start | bytes 524288 | tf_op jit(solution)/shard_map/all_to_all | solution.py:17
  135.2 0.2 compare_reduce_fusion
  135.4 0.6 fusion.13
  136.0 0.2 convolution_convert_fusion.4
  136.2 1.3 select_reduce_fusion
  137.5 0.1 fusion.6
  137.7 10.0 %all-to-all-done.3 = bf16[16,32,256]{2,1,0:T(8,128)(2,1)S(1)} async-done(((bf16[16,32,256]{2,1,0:T(8,128)(2,1)}), bf16[16,32,256]{2,1,0:T(8,128)(2,1)S(1)}, u32[]{:S(2)}, u32[]{:S(2)}) %all-to-all-start.3) | async-done | bytes 262176 | tf_op jit(solution)/shard_map/all_to_all | solution.py:17
  147.7 9.2 %collective-permute-start.8 = (bf16[16,32,256]{2,1,0:T(8,128)(2,1)S(1)}, bf16[16,32,256]{2,1,0:T(8,128)(2,1)S(1)}, u32[]{:S(2)}, u32[]{:S(2)}) collective-permute-start(bf16[16,32,256]{2,1,0:T(8,128)(2,1)S(1)} %all-to-all-done.3), channel_id=1, source_target_pairs={{0,8},{8,0},{1,9},{9,1},{2,10},{10,2},{3,11},{11,3},{4,12},{12,4},... | collective-permute-start | bytes 786440 | tf_op jit(solution)/shard_map/ppermute | solution.py:26
  156.9 0.3 select_reduce_fusion.1
  157.3 0.1 sub.43
  157.4 0.6 collective-permute-done.8
  158.1 0.4 fusion.1
  158.6 1.0 tile.11
  159.5 3.8 %all-to-all-start.4 = ((bf16[8,192,256]{2,1,0:T(8,128)(2,1)}), bf16[8,192,256]{2,1,0:T(8,128)(2,1)S(1)}, u32[]{:S(2)}, u32[]{:S(2)}) async-start(bf16[8,192,256]{2,1,0:T(8,128)(2,1)} %bitcast.78), calls=%async_computation.4 | async-start | bytes 1572864 | tf_op jit(solution)/shard_map/all_to_all | solution.py:17
  163.5 3.2 %collective-permute-start.9 = (bf16[2,2048,128]{2,1,0:T(8,128)(2,1)S(1)}, bf16[2,2048,128]{2,1,0:T(8,128)(2,1)S(1)}, u32[]{:S(2)}, u32[]{:S(2)}) collective-permute-start(bf16[2,2048,128]{2,1,0:T(8,128)(2,1)S(1)} %pad_maximum_fusion), channel_id=1, source_target_pairs={{0,1},{1,0},{2,3},{3,2},{4,5},{5,4},{6,7},{7,6},{8,9},{9,8},{10,11... | collective-permute-start | bytes 3145736 | tf_op jit(solution)/shard_map/ppermute | solution.py:267
  166.8 2.2 collective-permute-start.10
  169.1 46.6 %collective-permute-done.10.got_down = bf16[128,2048]{1,0:T(8,128)(2,1)S(1)} collective-permute-done((bf16[128,2048]{1,0:T(8,128)(2,1)S(1)}, bf16[128,2048]{1,0:T(8,128)(2,1)S(1)}, u32[]{:S(2)}, u32[]{:S(2)}) %collective-permute-start.10) | collective-permute-done | bytes 524320 | tf_op jit(solution)/shard_map/ppermute | solution.py:269
  215.7 0.8 copy-done.7
  216.5 1.0 copy-done.5
  217.4 1.2 copy-done.4
  218.7 1.2 copy-done.6
  219.9 1.0 copy-done.8
  220.9 1.8 run_expert.1
  222.7 6.5 %all-to-all-start.5 = ((bf16[8,192,256]{2,1,0:T(8,128)(2,1)}), bf16[8,192,256]{2,1,0:T(8,128)(2,1)S(1)}, u32[]{:S(2)}, u32[]{:S(2)}) async-start(bf16[8,192,256]{2,1,0:T(8,128)(2,1)} %run_expert.1), calls=%async_computation.5 | async-start | bytes 1572864 | tf_op jit(solution)/shard_map/all_to_all | solution.py:17
  229.3 0.1 select_reduce_fusion.2
  229.6 0.1 fusion.15
  229.7 23.1 %all-to-all-done.5 = bf16[8,192,256]{2,1,0:T(8,128)(2,1)S(1)} async-done(((bf16[8,192,256]{2,1,0:T(8,128)(2,1)}), bf16[8,192,256]{2,1,0:T(8,128)(2,1)S(1)}, u32[]{:S(2)}, u32[]{:S(2)}) %all-to-all-start.5) | async-done | bytes 786464 | tf_op jit(solution)/shard_map/all_to_all | solution.py:17
  252.8 0.2 reduce.1
  252.9 0.9 copy.93
  253.8 5.9 %all-to-all-start.6 = ((bf16[32,2,6,256]{3,1,2,0:T(2,128)(2,1)}), bf16[32,2,6,256]{3,1,2,0:T(2,128)(2,1)S(1)}, u32[]{:S(2)}, u32[]{:S(2)}) async-start(bf16[32,2,6,256]{3,1,2,0:T(2,128)(2,1)} %bitcast.26), calls=%async_computation.6 | async-start | bytes 393216 | tf_op jit(solution)/shard_map/all_to_all | solution.py:17
  259.7 0.1 fusion.9
  260.1 0.2 fusion.8
  260.3 18.0 %all-to-all-done.6 = bf16[32,2,6,256]{3,1,2,0:T(2,128)(2,1)S(1)} async-done(((bf16[32,2,6,256]{3,1,2,0:T(2,128)(2,1)}), bf16[32,2,6,256]{3,1,2,0:T(2,128)(2,1)S(1)}, u32[]{:S(2)}, u32[]{:S(2)}) %all-to-all-start.6) | async-done | bytes 196640 | tf_op jit(solution)/shard_map/all_to_all | solution.py:17
  278.4 0.9 fusion.7
  (96 shorter events, 2.6 us)
Async XLA Ops:
  0.0 60.0 %copy-start = (bf16[32,4096]{1,0:T(8,128)(2,1)S(1)}, bf16[32,4096]{1,0:T(8,128)(2,1)}, u32[]{:S(2)}) copy-start(bf16[32,4096]{1,0:T(8,128)(2,1)} %param.12) | copy-start | bytes 786436
  0.0 59.0 %copy-start.14 = (s32[32]{0:T(128)S(1)}, s32[32]{0:T(128)}, u32[]{:S(2)}) copy-start(s32[32]{0:T(128)} %param.16) | copy-start | bytes 388
  0.0 62.5 %copy-start.11 = (bf16[512,64]{0,1:T(8,128)(2,1)S(1)}, bf16[512,64]{0,1:T(8,128)(2,1)}, u32[]{:S(2)}) copy-start(bf16[512,64]{0,1:T(8,128)(2,1)} %param.18) | copy-start | bytes 196612
  0.0 62.5 %collective-permute-start = (bf16[64,512]{1,0:T(8,128)(2,1)}, bf16[64,512]{1,0:T(8,128)(2,1)S(1)}, u32[]{:S(2)}, u32[]{:S(2)}) collective-permute-start(bf16[64,512]{1,0:T(8,128)(2,1)} %bitcast.81), channel_id=1, source_target_pairs={{0,192},{16,208},{32,224},{48,240},{64,0},{80,16},{96,32},{112,48}... | collective-permute-start | bytes 196616 | tf_op jit(solution)/shard_map/ppermute | solution.py:22
  39.5 23.0 %collective-permute-start.1 = (bf16[64,512]{1,0:T(8,128)(2,1)}, bf16[64,512]{1,0:T(8,128)(2,1)S(1)}, u32[]{:S(2)}, u32[]{:S(2)}) collective-permute-start(bf16[64,512]{1,0:T(8,128)(2,1)} %bitcast.82), channel_id=1, source_target_pairs={{0,128},{16,144},{32,160},{48,176},{64,192},{80,208},{96,224},{112... | collective-permute-start | bytes 196616 | tf_op jit(solution)/shard_map/ppermute | solution.py:22
  41.5 21.0 %collective-permute-start.2 = (bf16[64,512]{1,0:T(8,128)(2,1)}, bf16[64,512]{1,0:T(8,128)(2,1)S(1)}, u32[]{:S(2)}, u32[]{:S(2)}) collective-permute-start(bf16[64,512]{1,0:T(8,128)(2,1)} %bitcast.83), channel_id=1, source_target_pairs={{0,64},{16,80},{32,96},{48,112},{64,128},{80,144},{96,160},{112,17... | collective-permute-start | bytes 196616 | tf_op jit(solution)/shard_map/ppermute | solution.py:22
  50.2 28.7 %all-to-all-start = ((bf16[8,32,256]{2,1,0:T(8,128)(2,1)}), bf16[8,32,256]{2,1,0:T(8,128)(2,1)S(1)}, u32[]{:S(2)}, u32[]{:S(2)}) async-start(bf16[8,32,256]{2,1,0:T(8,128)(2,1)} %bitcast.1), calls=%async_computation | async-start | bytes 262144 | tf_op jit(solution)/shard_map/all_to_all | solution.py:17
  62.6 32.2 %collective-permute-start.3 = (bf16[4,64,512]{2,1,0:T(8,128)(2,1)S(1)}, bf16[4,64,512]{2,1,0:T(8,128)(2,1)S(1)}, u32[]{:S(2)}, u32[]{:S(2)}) collective-permute-start(bf16[4,64,512]{2,1,0:T(8,128)(2,1)S(1)} %pad_maximum_fusion.2), channel_id=1, source_target_pairs={{0,240},{16,0},{32,16},{48,32},{64,48},{80,64},{96,80},{112,96},{1... | collective-permute-start | bytes 786440 | tf_op jit(solution)/shard_map/ppermute | solution.py:22
  70.0 24.8 %collective-permute-start.4 = (bf16[4,64,512]{2,1,0:T(8,128)(2,1)S(1)}, bf16[4,64,512]{2,1,0:T(8,128)(2,1)S(1)}, u32[]{:S(2)}, u32[]{:S(2)}) collective-permute-start(bf16[4,64,512]{2,1,0:T(8,128)(2,1)S(1)} %pad_maximum_fusion.2), channel_id=1, source_target_pairs={{0,16},{16,32},{32,48},{48,64},{64,80},{80,96},{96,112},{112,128},... | collective-permute-start | bytes 786440 | tf_op jit(solution)/shard_map/ppermute | solution.py:22
  72.0 22.9 %collective-permute-start.5 = (bf16[2,64,512]{2,1,0:T(8,128)(2,1)S(1)}, bf16[2,64,512]{2,1,0:T(8,128)(2,1)S(1)}, u32[]{:S(2)}, u32[]{:S(2)}) collective-permute-start(bf16[2,64,512]{2,1,0:T(8,128)(2,1)S(1)} %get-tuple-element.16), channel_id=1, source_target_pairs={{0,224},{16,240},{32,0},{48,16},{64,32},{80,48},{96,64},{112,80},{... | collective-permute-start | bytes 393224 | tf_op jit(solution)/shard_map/ppermute | solution.py:22
  75.1 19.8 %collective-permute-start.6 = (bf16[2,64,512]{2,1,0:T(8,128)(2,1)S(1)}, bf16[2,64,512]{2,1,0:T(8,128)(2,1)S(1)}, u32[]{:S(2)}, u32[]{:S(2)}) collective-permute-start(bf16[2,64,512]{2,1,0:T(8,128)(2,1)S(1)} %get-tuple-element.15), channel_id=1, source_target_pairs={{0,32},{16,48},{32,64},{48,80},{64,96},{80,112},{96,128},{112,144}... | collective-permute-start | bytes 393224 | tf_op jit(solution)/shard_map/ppermute | solution.py:22
  78.9 32.8 %all-to-all-start.1 = ((bf16[32,2,1280]{2,1,0:T(2,128)(2,1)}), bf16[32,2,1280]{2,1,0:T(2,128)(2,1)S(1)}, u32[]{:S(2)}, u32[]{:S(2)}) async-start(bf16[32,2,1280]{2,1,0:T(2,128)(2,1)} %pad_maximum_fusion.3), calls=%async_computation.1 | async-start | bytes 327680 | tf_op jit(solution)/shard_map/all_to_all | solution.py:17
  94.9 18.6 %collective-permute-start.7 = (bf16[16,64,512]{2,1,0:T(8,128)(2,1)S(1)}, bf16[16,64,512]{2,1,0:T(8,128)(2,1)S(1)}, u32[]{:S(2)}, u32[]{:S(2)}) collective-permute-start(bf16[16,64,512]{2,1,0:T(8,128)(2,1)S(1)} %constant_dynamic-update-slice_fusion.mine), channel_id=1, source_target_pairs={{0,8},{8,0},{1,9},{9,1},{2,10},{10,2},{3,11},{11,3},{4,12},{12,4},... | collective-permute-start | bytes 3145736 | tf_op jit(solution)/shard_map/ppermute | solution.py:26
  115.4 14.9 %all-to-all-start.2 = ((bf16[8,32,256]{2,1,0:T(8,128)(2,1)}), bf16[8,32,256]{2,1,0:T(8,128)(2,1)S(1)}, u32[]{:S(2)}, u32[]{:S(2)}) async-start(bf16[8,32,256]{2,1,0:T(8,128)(2,1)} %project_out.1), calls=%async_computation.2 | async-start | bytes 262144 | tf_op jit(solution)/shard_map/all_to_all | solution.py:17
  131.1 16.7 %all-to-all-start.3 = ((bf16[16,32,256]{2,1,0:T(8,128)(2,1)}), bf16[16,32,256]{2,1,0:T(8,128)(2,1)S(1)}, u32[]{:S(2)}, u32[]{:S(2)}) async-start(bf16[16,32,256]{2,1,0:T(8,128)(2,1)} %broadcast_in_dim.140), calls=%async_computation.3 | async-start | bytes 524288 | tf_op jit(solution)/shard_map/all_to_all | solution.py:17
  147.7 10.3 %collective-permute-start.8 = (bf16[16,32,256]{2,1,0:T(8,128)(2,1)S(1)}, bf16[16,32,256]{2,1,0:T(8,128)(2,1)S(1)}, u32[]{:S(2)}, u32[]{:S(2)}) collective-permute-start(bf16[16,32,256]{2,1,0:T(8,128)(2,1)S(1)} %all-to-all-done.3), channel_id=1, source_target_pairs={{0,8},{8,0},{1,9},{9,1},{2,10},{10,2},{3,11},{11,3},{4,12},{12,4},... | collective-permute-start | bytes 786440 | tf_op jit(solution)/shard_map/ppermute | solution.py:26
  158.1 1.4 copy-start.9
  158.6 4.8 %copy-start.1 = (bf16[2,2048,128]{2,1,0:T(8,128)(2,1)S(1)}, bf16[2,2048,128]{2,1,0:T(8,128)(2,1)}, u32[]{:S(2)}) copy-start(bf16[2,2048,128]{2,1,0:T(8,128)(2,1)} %gate.1) | copy-start | bytes 3145732
  158.6 4.8 %copy-start.2 = (bf16[2,2048,128]{2,1,0:T(8,128)(2,1)S(1)}, bf16[2,2048,128]{2,1,0:T(8,128)(2,1)}, u32[]{:S(2)}) copy-start(bf16[2,2048,128]{2,1,0:T(8,128)(2,1)} %up.1) | copy-start | bytes 3145732
  159.5 57.9 %all-to-all-start.4 = ((bf16[8,192,256]{2,1,0:T(8,128)(2,1)}), bf16[8,192,256]{2,1,0:T(8,128)(2,1)S(1)}, u32[]{:S(2)}, u32[]{:S(2)}) async-start(bf16[8,192,256]{2,1,0:T(8,128)(2,1)} %bitcast.78), calls=%async_computation.4 | async-start | bytes 1572864 | tf_op jit(solution)/shard_map/all_to_all | solution.py:17
  163.4 3.4 %copy-start.3 = (bf16[2,128,2048]{2,1,0:T(8,128)(2,1)S(1)}, bf16[2,128,2048]{2,1,0:T(8,128)(2,1)}, u32[]{:S(2)}) copy-start(bf16[2,128,2048]{2,1,0:T(8,128)(2,1)} %down.1) | copy-start | bytes 3145732
  163.5 52.9 %collective-permute-start.9 = (bf16[2,2048,128]{2,1,0:T(8,128)(2,1)S(1)}, bf16[2,2048,128]{2,1,0:T(8,128)(2,1)S(1)}, u32[]{:S(2)}, u32[]{:S(2)}) collective-permute-start(bf16[2,2048,128]{2,1,0:T(8,128)(2,1)S(1)} %pad_maximum_fusion), channel_id=1, source_target_pairs={{0,1},{1,0},{2,3},{3,2},{4,5},{5,4},{6,7},{7,6},{8,9},{9,8},{10,11... | collective-permute-start | bytes 3145736 | tf_op jit(solution)/shard_map/ppermute | solution.py:267
  166.8 48.8 %collective-permute-start.10 = (bf16[128,2048]{1,0:T(8,128)(2,1)S(1)}, bf16[128,2048]{1,0:T(8,128)(2,1)S(1)}, u32[]{:S(2)}, u32[]{:S(2)}) collective-permute-start(bf16[128,2048]{1,0:T(8,128)(2,1)S(1)} %dynamic-slice_bitcast_fusion), channel_id=1, source_target_pairs={{0,1},{1,0},{2,3},{3,2},{4,5},{5,4},{6,7},{7,6},{8,9},{9,8},{10,11... | collective-permute-start | bytes 1572872 | tf_op jit(solution)/shard_map/ppermute | solution.py:269
  215.7 0.8 copy-start.7
  216.5 1.0 copy-start.5
  217.4 1.2 copy-start.4
  218.7 1.2 copy-start.6
  219.9 1.0 copy-start.8
  222.7 6.5 %copy-start.12 = (s32[32,8]{0,1:T(8,128)S(1)}, s32[32,8]{0,1:T(8,128)}, u32[]{:S(2)}) copy-start(s32[32,8]{0,1:T(8,128)} %param.19) | copy-start | bytes 3076
  222.7 6.5 %copy-start.13 = (f32[32,8]{0,1:T(8,128)S(1)}, f32[32,8]{0,1:T(8,128)}, u32[]{:S(2)}) copy-start(f32[32,8]{0,1:T(8,128)} %param.20) | copy-start | bytes 3076
  222.7 30.0 %all-to-all-start.5 = ((bf16[8,192,256]{2,1,0:T(8,128)(2,1)}), bf16[8,192,256]{2,1,0:T(8,128)(2,1)S(1)}, u32[]{:S(2)}, u32[]{:S(2)}) async-start(bf16[8,192,256]{2,1,0:T(8,128)(2,1)} %run_expert.1), calls=%async_computation.5 | async-start | bytes 1572864 | tf_op jit(solution)/shard_map/all_to_all | solution.py:17
  252.9 7.1 %copy-start.10 = (bf16[32,32,256]{2,1,0:T(8,128)(2,1)S(1)}, bf16[32,32,256]{2,1,0:T(8,128)(2,1)}, u32[]{:S(2)}) copy-start(bf16[32,32,256]{2,1,0:T(8,128)(2,1)} %copy-done.9) | copy-start | bytes 1572868
  253.8 24.4 %all-to-all-start.6 = ((bf16[32,2,6,256]{3,1,2,0:T(2,128)(2,1)}), bf16[32,2,6,256]{3,1,2,0:T(2,128)(2,1)S(1)}, u32[]{:S(2)}, u32[]{:S(2)}) async-start(bf16[32,2,6,256]{3,1,2,0:T(2,128)(2,1)} %bitcast.26), calls=%async_computation.6 | async-start | bytes 393216 | tf_op jit(solution)/shard_map/all_to_all | solution.py:17

commit v3 on v2

--- a/solution.py
+++ b/solution.py
@@ -17,9 +17,22 @@
     return lax.all_to_all(tiles, axis, split_axis=0, concat_axis=0, tiled=True)
 
 
-def from_chip(x, shift):
+def along_chips(x, shift):
     n = lax.axis_size("chip")
-    return lax.ppermute(x, "chip", [(i, (i - shift) % n) for i in range(n)])
+    moves = []
+    for c in range(n):
+        moves.append((c * CORES, (c - shift) % n * CORES))
+        moves.append((c * CORES + 1, (c + shift) % n * CORES + 1))
+    return lax.ppermute(x, EXPERT, moves)
+
+
+def across_chips(x):
+    n = lax.axis_size("chip")
+    moves = []
+    for c in range(n):
+        moves.append((c * CORES, (c + 1) % n * CORES + 1))
+        moves.append((c * CORES + 1, (c - 1) % n * CORES))
+    return lax.ppermute(x, EXPERT, moves)
 
 
 def other_core(x):
@@ -39,20 +52,32 @@
 
 def projection_kernel(at, attn, mine, theirs, out):
     chips = mine.shape[0]
-    quarter = chips // 4
+    half = chips // 2
     first = at[1] == 0
     rows = attn[...]
     per_out = out.shape[2] // (2 * mine.shape[1])
+
+    def block(use_zero, offset, kind):
+        spot, n, bit = 0, 1, half // 2
+        while bit:
+            spot = spot + lax.rem(lax.div(offset, n), 2) * bit
+            n, bit = 2 * n, bit // 2
+        spot = spot * 2 + kind
+        return jnp.where(use_zero == first, mine[spot], theirs[spot])
+
     for dest in range(out.shape[0]):
         blocks = []
         for near in range(per_out):
-            m = lax.rem(dest * per_out + near + chips - at[0], chips)
-            k, kind = lax.div(m, 4), lax.rem(m, 4)
-            place = jnp.where(kind == 1, quarter + k, k)
-            place = jnp.where(kind == 2, 3 * quarter + k, place)
-            place = jnp.where(kind == 3, 2 * quarter + lax.rem(k + 1, quarter), place)
-            a, b = mine[place], theirs[place]
-            blocks += [jnp.where(first, a, b), jnp.where(first, b, a)]
+            ahead = lax.rem(dest * per_out + near + chips - at[0], chips)
+            behind = lax.rem(chips - ahead, chips)
+            zero = ahead < half
+            blocks.append(
+                block(zero, jnp.where(zero, ahead, behind - 1), jnp.where(zero, 0, 1))
+            )
+            one = (ahead >= 1) & (ahead <= half)
+            blocks.append(
+                block(one, jnp.where(one, ahead - 1, behind), jnp.where(one, 1, 0))
+            )
         weight = jnp.concatenate(blocks, 0)
         out[dest] = lax.dot_general(
             rows, weight, (((1,), (1,)), ((), ())), preferred_element_type=f32
@@ -170,15 +195,11 @@
     cache_all = cache_all.reshape(n_x * block_len, 2 * HD)
 
     w_own = out_weight.T
-    far = from_chip(w_own, chips // 2)
-    ahead = from_chip(w_own, chips // 4)
-    behind = from_chip(w_own, -(chips // 4))
-    quarter = jnp.stack([w_own, ahead, far, behind])
-    next_one = from_chip(quarter, 1)
-    last_one = from_chip(quarter, -1)
-    next_two = from_chip(quarter[:2], 2)
-    last_two = from_chip(jnp.stack([quarter[3], quarter[0]]), -2)
-    mine = jnp.concatenate([quarter, next_one, last_one, next_two, last_two])
+    mine = jnp.stack([w_own, across_chips(w_own)])
+    shift = chips // 4
+    while shift:
+        mine = jnp.concatenate([mine, along_chips(mine, shift)])
+        shift //= 2
     theirs = other_core(mine)
 
     kv_pos = (pos_x * heads_here) // group_size

time: 281 us -> 275 us (0.979)
  starting transfers between devices: 132 us -> 116 us
  waiting for transfers between devices: 120 us -> 130 us
    ppermute x7 -> x4, waiting for transfers between devices: 0.02 us -> 21.9 us  [the longest x3 21.9 us: along_chips(): return lax.ppermute(x, EXPERT, moves)]
    all_to_all x7, waiting for transfers between devices: 72.9 us -> 59.1 us  [exchange(): return lax.all_to_all(tiles, axis, split_axis=0, concat_axis=0, tiled=True)]
    ppermute x7 -> x4, starting transfers between devices: 64.7 us -> 52.1 us  [the longest x1 44.5 us: across_chips(): return lax.ppermute(x, EXPERT, moves)]
    unnamed x41 -> x36, local copies, waits for them, and re-layouts: 7.25 us -> 6.37 us
  transfers between devices with their start and end apart: 18 -> 15, of which waited for: 7 -> 10; matrix products, arithmetic and copies ran while one was open for 4% -> 4% of each run, Pallas kernels for 0% -> 0%
where the time goes in v3:
time: 275 us; the launch traced here: 274 us
  waiting for transfers between devices  130 us (47%)
  starting transfers between devices  116 us (42%)
  local copies, waits for them, and re-layouts  12.8 us (5%)
  other arithmetic  7 us (3%)
  Pallas kernels  3.73 us (1%)
  matrix products  2.94 us (1%)
    all_to_all x7, waiting for transfers between devices, exchange(): return lax.all_to_all(tiles, axis, split_axis=0, concat_axis=0, tiled=True)  59.1 us
    all_to_all x7, starting transfers between devices, exchange(): return lax.all_to_all(tiles, axis, split_axis=0, concat_axis=0, tiled=True)  47.8 us
    ppermute x1, waiting for transfers between devices, layer(): got_down = lax.ppermute(down, 'tensor', swap)  46.6 us
    ppermute x1, starting transfers between devices, across_chips(): return lax.ppermute(x, EXPERT, moves)  44.5 us
    ppermute x3, waiting for transfers between devices, along_chips(): return lax.ppermute(x, EXPERT, moves)  21.9 us
    ppermute x2, starting transfers between devices, other_core(): return lax.ppermute(x, 'core', [(0, 1), (1, 0)])  10.8 us
    ppermute x3, starting transfers between devices, along_chips(): return lax.ppermute(x, EXPERT, moves)  7.59 us
    unnamed x36, local copies, waits for them, and re-layouts  6.37 us
  transfers between devices with their start and end apart: 15, of which 10 were waited for; matrix products, arithmetic and copies ran while one was open for 4% of the time, Pallas kernels for 0%

profile of v3, /device:TPU:65, one launch (start us, length us, event | category | flops | bytes accessed | tf_op | source)
XLA Modules:
  0.0 273.8 jit_solution(17394139756476721419)
XLA Ops:
  0.0 0.9 reshape_squeeze.3
  1.0 0.7 broadcast_in_dim.79
  1.7 7.9 %all-to-all-start = ((bf16[8,32,256]{2,1,0:T(8,128)(2,1)}), bf16[8,32,256]{2,1,0:T(8,128)(2,1)S(1)}, u32[]{:S(2)}, u32[]{:S(2)}) async-start(bf16[8,32,256]{2,1,0:T(8,128)(2,1)} %bitcast.1), calls=%async_computation | async-start | bytes 262144 | tf_op jit(solution)/shard_map/all_to_all | solution.py:17
  9.6 44.5 %collective-permute-start = (bf16[64,512]{1,0:T(8,128)(2,1)}, bf16[64,512]{1,0:T(8,128)(2,1)S(1)}, u32[]{:S(2)}, u32[]{:S(2)}) collective-permute-start(bf16[64,512]{1,0:T(8,128)(2,1)} %bitcast.77), channel_id=1, source_target_pairs={{0,24},{8,240},{16,40},{24,0},{32,56},{40,16},{48,72},{56,32},{64,... | collective-permute-start | bytes 196616 | tf_op jit(solution)/shard_map/ppermute | solution.py:35
  54.1 0.7 convert.9
  55.0 0.9 convert_reduce_fusion.2
  55.9 0.7 multiply_add_fusion
  56.7 0.7 constant_dynamic-slice_fusion.3
  57.5 0.7 constant_dynamic-slice_fusion.5
  58.2 0.2 convolution_convert_fusion
  58.4 0.8 pad_maximum_fusion.4
  59.9 2.0 collective-permute-start.1
  62.0 7.4 %all-to-all-start.1 = ((bf16[32,2,1280]{2,1,0:T(2,128)(2,1)}), bf16[32,2,1280]{2,1,0:T(2,128)(2,1)S(1)}, u32[]{:S(2)}, u32[]{:S(2)}) async-start(bf16[32,2,1280]{2,1,0:T(2,128)(2,1)} %pad_maximum_fusion.4), calls=%async_computation.1 | async-start | bytes 327680 | tf_op jit(solution)/shard_map/all_to_all | solution.py:17
  69.4 0.5 collective-permute-done.1
  70.0 3.7 %collective-permute-start.2 = (bf16[4,64,512]{2,1,0:T(8,128)(2,1)S(1)}, bf16[4,64,512]{2,1,0:T(8,128)(2,1)S(1)}, u32[]{:S(2)}, u32[]{:S(2)}) collective-permute-start(bf16[4,64,512]{2,1,0:T(8,128)(2,1)S(1)} %pad_maximum_fusion.3), channel_id=1, source_target_pairs={{0,224},{8,40},{16,240},{24,56},{32,0},{40,72},{48,16},{56,88},{64... | collective-permute-start | bytes 786440 | tf_op jit(solution)/shard_map/ppermute | solution.py:26
  73.7 13.0 %collective-permute-done.2 = bf16[4,64,512]{2,1,0:T(8,128)(2,1)S(1)} collective-permute-done((bf16[4,64,512]{2,1,0:T(8,128)(2,1)S(1)}, bf16[4,64,512]{2,1,0:T(8,128)(2,1)S(1)}, u32[]{:S(2)}, u32[]{:S(2)}) %collective-permute-start.2) | collective-permute-done | bytes 262176 | tf_op jit(solution)/shard_map/ppermute | solution.py:26
  86.8 2.0 collective-permute-start.3
  89.0 0.1 fusion.11
  89.4 0.2 convolution_convert_fusion.1
  89.6 8.3 %collective-permute-done.3 = bf16[8,64,512]{2,1,0:T(8,128)(2,1)S(1)} collective-permute-done((bf16[8,64,512]{2,1,0:T(8,128)(2,1)S(1)}, bf16[8,64,512]{2,1,0:T(8,128)(2,1)S(1)}, u32[]{:S(2)}, u32[]{:S(2)}) %collective-permute-start.3) | collective-permute-done | bytes 524320 | tf_op jit(solution)/shard_map/ppermute | solution.py:26
  98.0 2.0 collective-permute-start.4
  100.2 0.3 fusion.59
  100.5 0.2 fusion.16
  100.6 0.2 fusion.5
  100.9 1.7 collective-permute-done.4.theirs
  102.6 1.9 project_out.1
  104.5 6.9 %all-to-all-start.2 = ((bf16[8,32,256]{2,1,0:T(8,128)(2,1)}), bf16[8,32,256]{2,1,0:T(8,128)(2,1)S(1)}, u32[]{:S(2)}, u32[]{:S(2)}) async-start(bf16[8,32,256]{2,1,0:T(8,128)(2,1)} %project_out.1), calls=%async_computation.2 | async-start | bytes 262144 | tf_op jit(solution)/shard_map/all_to_all | solution.py:17
  111.6 0.1 copy.89
  111.8 8.0 %all-to-all-done.2 = bf16[8,32,256]{2,1,0:T(8,128)(2,1)S(1)} async-done(((bf16[8,32,256]{2,1,0:T(8,128)(2,1)}), bf16[8,32,256]{2,1,0:T(8,128)(2,1)S(1)}, u32[]{:S(2)}, u32[]{:S(2)}) %all-to-all-start.2) | async-done | bytes 131104 | tf_op jit(solution)/shard_map/all_to_all | solution.py:17
  119.9 0.7 broadcast_in_dim.140
  120.6 9.1 %all-to-all-start.3 = ((bf16[16,32,256]{2,1,0:T(8,128)(2,1)}), bf16[16,32,256]{2,1,0:T(8,128)(2,1)S(1)}, u32[]{:S(2)}, u32[]{:S(2)}) async-start(bf16[16,32,256]{2,1,0:T(8,128)(2,1)} %broadcast_in_dim.140), calls=%async_computation.3 | async-start | bytes 524288 | tf_op jit(solution)/shard_map/all_to_all | solution.py:17
  129.7 0.2 compare_reduce_fusion
  129.9 0.6 fusion.13
  130.5 0.2 convolution_convert_fusion.4
  130.7 1.3 select_reduce_fusion
  132.0 0.1 fusion.6
  132.2 10.0 %all-to-all-done.3 = bf16[16,32,256]{2,1,0:T(8,128)(2,1)S(1)} async-done(((bf16[16,32,256]{2,1,0:T(8,128)(2,1)}), bf16[16,32,256]{2,1,0:T(8,128)(2,1)S(1)}, u32[]{:S(2)}, u32[]{:S(2)}) %all-to-all-start.3) | async-done | bytes 262176 | tf_op jit(solution)/shard_map/all_to_all | solution.py:17
  142.2 8.8 %collective-permute-start.5 = (bf16[16,32,256]{2,1,0:T(8,128)(2,1)S(1)}, bf16[16,32,256]{2,1,0:T(8,128)(2,1)S(1)}, u32[]{:S(2)}, u32[]{:S(2)}) collective-permute-start(bf16[16,32,256]{2,1,0:T(8,128)(2,1)S(1)} %all-to-all-done.3), channel_id=1, source_target_pairs={{0,8},{8,0},{1,9},{9,1},{2,10},{10,2},{3,11},{11,3},{4,12},{12,4},... | collective-permute-start | bytes 786440 | tf_op jit(solution)/shard_map/ppermute | solution.py:39
  151.1 0.3 select_reduce_fusion.1
  151.4 0.1 sub.43
  151.6 0.6 collective-permute-done.5
  152.3 0.4 fusion.1
  152.7 1.0 tile.11
  153.7 3.8 %all-to-all-start.4 = ((bf16[8,192,256]{2,1,0:T(8,128)(2,1)}), bf16[8,192,256]{2,1,0:T(8,128)(2,1)S(1)}, u32[]{:S(2)}, u32[]{:S(2)}) async-start(bf16[8,192,256]{2,1,0:T(8,128)(2,1)} %bitcast.74), calls=%async_computation.4 | async-start | bytes 1572864 | tf_op jit(solution)/shard_map/all_to_all | solution.py:17
  157.7 3.2 %collective-permute-start.6 = (bf16[2,2048,128]{2,1,0:T(8,128)(2,1)S(1)}, bf16[2,2048,128]{2,1,0:T(8,128)(2,1)S(1)}, u32[]{:S(2)}, u32[]{:S(2)}) collective-permute-start(bf16[2,2048,128]{2,1,0:T(8,128)(2,1)S(1)} %pad_maximum_fusion), channel_id=1, source_target_pairs={{0,1},{1,0},{2,3},{3,2},{4,5},{5,4},{6,7},{7,6},{8,9},{9,8},{10,11... | collective-permute-start | bytes 3145736 | tf_op jit(solution)/shard_map/ppermute | solution.py:288
  161.0 2.2 collective-permute-start.7
  163.2 46.6 %collective-permute-done.7.got_down = bf16[128,2048]{1,0:T(8,128)(2,1)S(1)} collective-permute-done((bf16[128,2048]{1,0:T(8,128)(2,1)S(1)}, bf16[128,2048]{1,0:T(8,128)(2,1)S(1)}, u32[]{:S(2)}, u32[]{:S(2)}) %collective-permute-start.7) | collective-permute-done | bytes 524320 | tf_op jit(solution)/shard_map/ppermute | solution.py:290
  209.8 0.8 copy-done.7
  210.6 1.0 copy-done.5
  211.6 1.2 copy-done.4
  212.8 1.2 copy-done.6
  214.0 1.0 copy-done.8
  215.0 1.8 run_expert.1
  216.8 6.5 %all-to-all-start.5 = ((bf16[8,192,256]{2,1,0:T(8,128)(2,1)}), bf16[8,192,256]{2,1,0:T(8,128)(2,1)S(1)}, u32[]{:S(2)}, u32[]{:S(2)}) async-start(bf16[8,192,256]{2,1,0:T(8,128)(2,1)} %run_expert.1), calls=%async_computation.5 | async-start | bytes 1572864 | tf_op jit(solution)/shard_map/all_to_all | solution.py:17
  223.5 0.1 select_reduce_fusion.2
  223.7 0.1 fusion.15
  223.8 23.1 %all-to-all-done.5 = bf16[8,192,256]{2,1,0:T(8,128)(2,1)S(1)} async-done(((bf16[8,192,256]{2,1,0:T(8,128)(2,1)}), bf16[8,192,256]{2,1,0:T(8,128)(2,1)S(1)}, u32[]{:S(2)}, u32[]{:S(2)}) %all-to-all-start.5) | async-done | bytes 786464 | tf_op jit(solution)/shard_map/all_to_all | solution.py:17
  246.9 0.2 reduce.1
  247.1 0.9 copy.93
  247.9 6.2 %all-to-all-start.6 = ((bf16[32,2,6,256]{3,1,2,0:T(2,128)(2,1)}), bf16[32,2,6,256]{3,1,2,0:T(2,128)(2,1)S(1)}, u32[]{:S(2)}, u32[]{:S(2)}) async-start(bf16[32,2,6,256]{3,1,2,0:T(2,128)(2,1)} %bitcast.24), calls=%async_computation.6 | async-start | bytes 393216 | tf_op jit(solution)/shard_map/all_to_all | solution.py:17
  254.2 0.1 fusion.9
  254.5 0.2 fusion.8
  254.7 18.0 %all-to-all-done.6 = bf16[32,2,6,256]{3,1,2,0:T(2,128)(2,1)S(1)} async-done(((bf16[32,2,6,256]{3,1,2,0:T(2,128)(2,1)}), bf16[32,2,6,256]{3,1,2,0:T(2,128)(2,1)S(1)}, u32[]{:S(2)}, u32[]{:S(2)}) %all-to-all-start.6) | async-done | bytes 196640 | tf_op jit(solution)/shard_map/all_to_all | solution.py:17
  272.8 0.9 fusion.7
  (86 shorter events, 2.6 us)
Async XLA Ops:
  0.0 57.4 %copy-start = (bf16[32,4096]{1,0:T(8,128)(2,1)S(1)}, bf16[32,4096]{1,0:T(8,128)(2,1)}, u32[]{:S(2)}) copy-start(bf16[32,4096]{1,0:T(8,128)(2,1)} %param.12) | copy-start | bytes 786436
  0.0 59.2 %copy-start.11 = (bf16[512,64]{0,1:T(8,128)(2,1)S(1)}, bf16[512,64]{0,1:T(8,128)(2,1)}, u32[]{:S(2)}) copy-start(bf16[512,64]{0,1:T(8,128)(2,1)} %param.18) | copy-start | bytes 196612
  1.7 60.3 %all-to-all-start = ((bf16[8,32,256]{2,1,0:T(8,128)(2,1)}), bf16[8,32,256]{2,1,0:T(8,128)(2,1)S(1)}, u32[]{:S(2)}, u32[]{:S(2)}) async-start(bf16[8,32,256]{2,1,0:T(8,128)(2,1)} %bitcast.1), calls=%async_computation | async-start | bytes 262144 | tf_op jit(solution)/shard_map/all_to_all | solution.py:17
  9.6 50.3 %collective-permute-start = (bf16[64,512]{1,0:T(8,128)(2,1)}, bf16[64,512]{1,0:T(8,128)(2,1)S(1)}, u32[]{:S(2)}, u32[]{:S(2)}) collective-permute-start(bf16[64,512]{1,0:T(8,128)(2,1)} %bitcast.77), channel_id=1, source_target_pairs={{0,24},{8,240},{16,40},{24,0},{32,56},{40,16},{48,72},{56,32},{64,... | collective-permute-start | bytes 196616 | tf_op jit(solution)/shard_map/ppermute | solution.py:35
  59.9 10.0 %collective-permute-start.1 = (bf16[2,64,512]{2,1,0:T(8,128)(2,1)S(1)}, bf16[2,64,512]{2,1,0:T(8,128)(2,1)S(1)}, u32[]{:S(2)}, u32[]{:S(2)}) collective-permute-start(bf16[2,64,512]{2,1,0:T(8,128)(2,1)S(1)} %pad_maximum_fusion.5), channel_id=1, source_target_pairs={{0,192},{8,72},{16,208},{24,88},{32,224},{40,104},{48,240},{56,120... | collective-permute-start | bytes 393224 | tf_op jit(solution)/shard_map/ppermute | solution.py:26
  62.0 26.8 %all-to-all-start.1 = ((bf16[32,2,1280]{2,1,0:T(2,128)(2,1)}), bf16[32,2,1280]{2,1,0:T(2,128)(2,1)S(1)}, u32[]{:S(2)}, u32[]{:S(2)}) async-start(bf16[32,2,1280]{2,1,0:T(2,128)(2,1)} %pad_maximum_fusion.4), calls=%async_computation.1 | async-start | bytes 327680 | tf_op jit(solution)/shard_map/all_to_all | solution.py:17
  70.0 16.8 %collective-permute-start.2 = (bf16[4,64,512]{2,1,0:T(8,128)(2,1)S(1)}, bf16[4,64,512]{2,1,0:T(8,128)(2,1)S(1)}, u32[]{:S(2)}, u32[]{:S(2)}) collective-permute-start(bf16[4,64,512]{2,1,0:T(8,128)(2,1)S(1)} %pad_maximum_fusion.3), channel_id=1, source_target_pairs={{0,224},{8,40},{16,240},{24,56},{32,0},{40,72},{48,16},{56,88},{64... | collective-permute-start | bytes 786440 | tf_op jit(solution)/shard_map/ppermute | solution.py:26
  86.8 11.2 %collective-permute-start.3 = (bf16[8,64,512]{2,1,0:T(8,128)(2,1)S(1)}, bf16[8,64,512]{2,1,0:T(8,128)(2,1)S(1)}, u32[]{:S(2)}, u32[]{:S(2)}) collective-permute-start(bf16[8,64,512]{2,1,0:T(8,128)(2,1)S(1)} %pad_maximum_fusion.1), channel_id=1, source_target_pairs={{0,240},{8,24},{16,0},{24,40},{32,16},{40,56},{48,32},{56,72},{64,... | collective-permute-start | bytes 1572872 | tf_op jit(solution)/shard_map/ppermute | solution.py:26
  98.0 4.6 %collective-permute-start.4 = (bf16[16,64,512]{2,1,0:T(8,128)(2,1)S(1)}, bf16[16,64,512]{2,1,0:T(8,128)(2,1)S(1)}, u32[]{:S(2)}, u32[]{:S(2)}) collective-permute-start(bf16[16,64,512]{2,1,0:T(8,128)(2,1)S(1)} %constant_dynamic-update-slice_fusion.mine), channel_id=1, source_target_pairs={{0,8},{8,0},{1,9},{9,1},{2,10},{10,2},{3,11},{11,3},{4,12},{12,4},... | collective-permute-start | bytes 3145736 | tf_op jit(solution)/shard_map/ppermute | solution.py:39
  104.5 15.3 %all-to-all-start.2 = ((bf16[8,32,256]{2,1,0:T(8,128)(2,1)}), bf16[8,32,256]{2,1,0:T(8,128)(2,1)S(1)}, u32[]{:S(2)}, u32[]{:S(2)}) async-start(bf16[8,32,256]{2,1,0:T(8,128)(2,1)} %project_out.1), calls=%async_computation.2 | async-start | bytes 262144 | tf_op jit(solution)/shard_map/all_to_all | solution.py:17
  120.6 21.6 %all-to-all-start.3 = ((bf16[16,32,256]{2,1,0:T(8,128)(2,1)}), bf16[16,32,256]{2,1,0:T(8,128)(2,1)S(1)}, u32[]{:S(2)}, u32[]{:S(2)}) async-start(bf16[16,32,256]{2,1,0:T(8,128)(2,1)} %broadcast_in_dim.140), calls=%async_computation.3 | async-start | bytes 524288 | tf_op jit(solution)/shard_map/all_to_all | solution.py:17
  142.2 10.0 %collective-permute-start.5 = (bf16[16,32,256]{2,1,0:T(8,128)(2,1)S(1)}, bf16[16,32,256]{2,1,0:T(8,128)(2,1)S(1)}, u32[]{:S(2)}, u32[]{:S(2)}) collective-permute-start(bf16[16,32,256]{2,1,0:T(8,128)(2,1)S(1)} %all-to-all-done.3), channel_id=1, source_target_pairs={{0,8},{8,0},{1,9},{9,1},{2,10},{10,2},{3,11},{11,3},{4,12},{12,4},... | collective-permute-start | bytes 786440 | tf_op jit(solution)/shard_map/ppermute | solution.py:39
  152.3 1.4 copy-start.9
  152.7 4.7 %copy-start.1 = (bf16[2,2048,128]{2,1,0:T(8,128)(2,1)S(1)}, bf16[2,2048,128]{2,1,0:T(8,128)(2,1)}, u32[]{:S(2)}) copy-start(bf16[2,2048,128]{2,1,0:T(8,128)(2,1)} %gate.1) | copy-start | bytes 3145732
  152.7 4.7 %copy-start.2 = (bf16[2,2048,128]{2,1,0:T(8,128)(2,1)S(1)}, bf16[2,2048,128]{2,1,0:T(8,128)(2,1)}, u32[]{:S(2)}) copy-start(bf16[2,2048,128]{2,1,0:T(8,128)(2,1)} %up.1) | copy-start | bytes 3145732
  153.7 57.9 %all-to-all-start.4 = ((bf16[8,192,256]{2,1,0:T(8,128)(2,1)}), bf16[8,192,256]{2,1,0:T(8,128)(2,1)S(1)}, u32[]{:S(2)}, u32[]{:S(2)}) async-start(bf16[8,192,256]{2,1,0:T(8,128)(2,1)} %bitcast.74), calls=%async_computation.4 | async-start | bytes 1572864 | tf_op jit(solution)/shard_map/all_to_all | solution.py:17
  157.5 3.4 %copy-start.3 = (bf16[2,128,2048]{2,1,0:T(8,128)(2,1)S(1)}, bf16[2,128,2048]{2,1,0:T(8,128)(2,1)}, u32[]{:S(2)}) copy-start(bf16[2,128,2048]{2,1,0:T(8,128)(2,1)} %down.1) | copy-start | bytes 3145732
  157.7 52.9 %collective-permute-start.6 = (bf16[2,2048,128]{2,1,0:T(8,128)(2,1)S(1)}, bf16[2,2048,128]{2,1,0:T(8,128)(2,1)S(1)}, u32[]{:S(2)}, u32[]{:S(2)}) collective-permute-start(bf16[2,2048,128]{2,1,0:T(8,128)(2,1)S(1)} %pad_maximum_fusion), channel_id=1, source_target_pairs={{0,1},{1,0},{2,3},{3,2},{4,5},{5,4},{6,7},{7,6},{8,9},{9,8},{10,11... | collective-permute-start | bytes 3145736 | tf_op jit(solution)/shard_map/ppermute | solution.py:288
  161.0 48.8 %collective-permute-start.7 = (bf16[128,2048]{1,0:T(8,128)(2,1)S(1)}, bf16[128,2048]{1,0:T(8,128)(2,1)S(1)}, u32[]{:S(2)}, u32[]{:S(2)}) collective-permute-start(bf16[128,2048]{1,0:T(8,128)(2,1)S(1)} %dynamic-slice_bitcast_fusion), channel_id=1, source_target_pairs={{0,1},{1,0},{2,3},{3,2},{4,5},{5,4},{6,7},{7,6},{8,9},{9,8},{10,11... | collective-permute-start | bytes 1572872 | tf_op jit(solution)/shard_map/ppermute | solution.py:290
  209.8 0.8 copy-start.7
  210.6 1.0 copy-start.5
  211.6 1.2 copy-start.4
  212.8 1.2 copy-start.6
  214.0 1.0 copy-start.8
  216.8 6.5 %copy-start.12 = (s32[32,8]{0,1:T(8,128)S(1)}, s32[32,8]{0,1:T(8,128)}, u32[]{:S(2)}) copy-start(s32[32,8]{0,1:T(8,128)} %param.19) | copy-start | bytes 3076
  216.8 6.6 %copy-start.13 = (f32[32,8]{0,1:T(8,128)S(1)}, f32[32,8]{0,1:T(8,128)}, u32[]{:S(2)}) copy-start(f32[32,8]{0,1:T(8,128)} %param.20) | copy-start | bytes 3076
  216.8 30.0 %all-to-all-start.5 = ((bf16[8,192,256]{2,1,0:T(8,128)(2,1)}), bf16[8,192,256]{2,1,0:T(8,128)(2,1)S(1)}, u32[]{:S(2)}, u32[]{:S(2)}) async-start(bf16[8,192,256]{2,1,0:T(8,128)(2,1)} %run_expert.1), calls=%async_computation.5 | async-start | bytes 1572864 | tf_op jit(solution)/shard_map/all_to_all | solution.py:17
  247.1 7.4 %copy-start.10 = (bf16[32,32,256]{2,1,0:T(8,128)(2,1)S(1)}, bf16[32,32,256]{2,1,0:T(8,128)(2,1)}, u32[]{:S(2)}) copy-start(bf16[32,32,256]{2,1,0:T(8,128)(2,1)} %copy-done.9) | copy-start | bytes 1572868
  247.9 24.8 %all-to-all-start.6 = ((bf16[32,2,6,256]{3,1,2,0:T(2,128)(2,1)}), bf16[32,2,6,256]{3,1,2,0:T(2,128)(2,1)S(1)}, u32[]{:S(2)}, u32[]{:S(2)}) async-start(bf16[32,2,6,256]{3,1,2,0:T(2,128)(2,1)} %bitcast.24), calls=%async_computation.6 | async-start | bytes 393216 | tf_op jit(solution)/shard_map/all_to_all | solution.py:17

commit v4 on v3

--- a/solution.py
+++ b/solution.py
@@ -45,17 +45,220 @@
     return jnp.dot(marks.astype(bf16), before, preferred_element_type=f32).astype(i32)
 
 
-def pick_rows(index, rows):
-    chosen = (index[:, None] == jnp.arange(rows.shape[0], dtype=i32)).astype(bf16)
-    return jnp.dot(chosen, rows, preferred_element_type=f32).astype(bf16)
-
-
-def projection_kernel(at, attn, mine, theirs, out):
-    chips = mine.shape[0]
-    half = chips // 2
+def one_hot(at, shape, dim):
+    return jnp.where(lax.broadcasted_iota(i32, shape, dim) == at, 1.0, 0.0).astype(bf16)
+
+
+def grouped_iota(groups, size, lanes, dim):
+    at = lax.broadcasted_iota(i32, (groups, size, lanes), dim)
+    return at.reshape(groups * size, lanes)
+
+
+def payload_kernel(places, target, q, k, v, resid, table, out):
+    chunks = [q[:, c : c + HD] for c in range(0, q.shape[1], HD)]
+    chunks += [k[...], v[...]]
+    chunks += [resid[:, c : c + HD] for c in range(0, resid.shape[1], HD)]
+    rows = jnp.concatenate([*chunks, table[...]], 0)
+    count, depth = out.shape[0], rows.shape[0]
+    groups = q.shape[0]
+    whole = lax.broadcasted_iota(i32, (count, depth), 0) == target[0:1, :]
+    local_row = grouped_iota(groups, count // groups, depth, 1) == target[1:2, :]
+    chosen = jnp.where(whole | local_row, 1.0, 0.0).astype(bf16)
+    out[...] = jnp.dot(chosen, rows, preferred_element_type=f32).astype(bf16)
+
+
+def build_payload(places, target, queries, own_kv, residual, table, q_cols, col_width, count):
+    tokens = queries.shape[0]
+
+    def cols(width, which):
+        return pl.BlockSpec((tokens, width), lambda i, at: (0, at[which]))
+
+    def whole(x):
+        return pl.BlockSpec(x.shape, lambda i, at: (0,) * x.ndim)
+
+    return pl.pallas_call(
+        payload_kernel,
+        out_shape=jax.ShapeDtypeStruct((count, HD), bf16),
+        grid_spec=pltpu.PrefetchScalarGridSpec(
+            num_scalar_prefetch=1,
+            grid=(1,),
+            in_specs=[
+                whole(target),
+                cols(q_cols, 0),
+                cols(HD, 1),
+                cols(HD, 2),
+                cols(col_width, 0),
+                whole(table),
+            ],
+            out_specs=pl.BlockSpec((count, HD), lambda i, at: (0, 0)),
+        ),
+        cost_estimate=pl.CostEstimate(
+            flops=2 * count * target.shape[1] * HD,
+            bytes_accessed=4 * count * HD,
+            transcendentals=0,
+        ),
+        compiler_params=pltpu.CompilerParams(vmem_limit_bytes=8 << 20),
+        name="build_payload",
+    )(places, target, queries, own_kv, own_kv, residual, table)
+
+
+def attention_kernel(at, got, cache, attn, resid):
+    tokens = attn.shape[0]
+    heads = attn.shape[1] // HD
+    chunks = heads + 2 + resid.shape[1] // HD
+    blocks = tokens
+    size = got.shape[0] // blocks
+    rows = got[...]
+    table_row = one_hot(
+        lax.broadcasted_iota(i32, (blocks, got.shape[0]), 0) * size + 2 * chunks,
+        (blocks, got.shape[0]),
+        1,
+    )
+    prompts = jnp.dot(table_row, rows, preferred_element_type=f32)[:, :tokens]
+    holds = jnp.max(jnp.where(prompts == at[0].astype(f32), 1.0, 0.0), 1, keepdims=True)
+    before = jnp.where(
+        lax.broadcasted_iota(i32, (blocks, blocks), 1)
+        < lax.broadcasted_iota(i32, (blocks, blocks), 0),
+        1.0,
+        0.0,
+    ).astype(bf16)
+    wide = jnp.broadcast_to(holds, (blocks, HD)).astype(bf16)
+    order = jnp.dot(before, wide, preferred_element_type=f32)
+    order = jnp.where(wide > 0, order * 2.0, -1024.0).astype(bf16)
+    spread = jnp.where(
+        grouped_iota(blocks, size, blocks, 0)
+        == lax.broadcasted_iota(i32, (blocks * size, blocks), 1),
+        1.0,
+        0.0,
+    ).astype(bf16)
+    order = jnp.dot(spread, order, preferred_element_type=f32)[:, :1].astype(i32)
+    place = grouped_iota(blocks, size, 1, 1)
+    second = jnp.where(place >= chunks, 1, 0)
+    target = (place - second * chunks) * tokens + order + second
+    target = jnp.where(place < 2 * chunks, target, -1)
+    chosen = one_hot(target, (got.shape[0], chunks * tokens), 1)
+    mine = lax.dot_general(
+        chosen, rows, (((0,), (0,)), ((), ())), preferred_element_type=f32
+    )
+
+    def chunk(c):
+        return mine[c * tokens : (c + 1) * tokens, :]
+
+    k_own, v_own = chunk(heads), chunk(heads + 1)
+    positions = cache.shape[0] * cache.shape[1]
+    both = cache[...].reshape(positions, cache.shape[2])
+    keys, values = both[:, :HD], both[:, HD:]
+    inside = lax.broadcasted_iota(i32, (tokens, positions), 1) < at[1]
+    scale = HD ** (-0.5)
+    for h in range(heads):
+        q = chunk(h)
+        scores = (
+            lax.dot_general(
+                q.astype(bf16), keys, (((1,), (1,)), ((), ())), preferred_element_type=f32
+            )
+            * scale
+        )
+        scores = jnp.where(inside, scores, MASKED_SCORE)
+        own = jnp.sum(q * k_own, 1, keepdims=True) * scale
+        top = jnp.maximum(jnp.max(scores, 1, keepdims=True), own)
+        weights = jnp.where(inside, jnp.exp(scores - top), 0.0)
+        own_weight = jnp.exp(own - top)
+        total = jnp.sum(weights, 1, keepdims=True) + own_weight
+        mix = jnp.dot(weights.astype(bf16), values, preferred_element_type=f32)
+        mix = (mix + own_weight * v_own) / total
+        attn[:, h * HD : (h + 1) * HD] = mix.astype(bf16)
+    for c in range(resid.shape[1] // HD):
+        resid[:, c * HD : (c + 1) * HD] = chunk(heads + 2 + c).astype(bf16)
+
+
+def attend(at, got, cache, tokens, q_cols, col_width):
+    vmem = pl.BlockSpec(memory_space=pltpu.VMEM)
+    return pl.pallas_call(
+        attention_kernel,
+        out_shape=(
+            jax.ShapeDtypeStruct((tokens, q_cols), bf16),
+            jax.ShapeDtypeStruct((tokens, col_width), bf16),
+        ),
+        in_specs=[pl.BlockSpec(memory_space=pltpu.SMEM), vmem, vmem],
+        out_specs=(vmem, vmem),
+        cost_estimate=pl.CostEstimate(
+            flops=4 * got.size * 256, bytes_accessed=2 * got.size, transcendentals=0
+        ),
+        compiler_params=pltpu.CompilerParams(vmem_limit_bytes=8 << 20),
+        name="attend",
+    )(at, got, cache)
+
+
+def hidden_kernel(parts, resid, out):
+    hidden = resid[...].astype(f32)
+    for s in range(parts.shape[0]):
+        hidden = hidden + parts[s].astype(f32)
+    hidden = hidden.astype(bf16)
+    for d in range(out.shape[0]):
+        out[d] = hidden
+
+
+def hidden_copies(parts, resid, copies):
+    vmem = pl.BlockSpec(memory_space=pltpu.VMEM)
+    return pl.pallas_call(
+        hidden_kernel,
+        out_shape=jax.ShapeDtypeStruct((copies, *resid.shape), bf16),
+        in_specs=[vmem, vmem],
+        out_specs=vmem,
+        cost_estimate=pl.CostEstimate(
+            flops=parts.size, bytes_accessed=4 * parts.size, transcendentals=0
+        ),
+        compiler_params=pltpu.CompilerParams(vmem_limit_bytes=4 << 20),
+        name="hidden_copies",
+    )(parts, resid)
+
+
+def select_kernel(experts_at, home_at, near, across, by_dest, home):
+    half = near.shape[0]
+
+    def picked(at):
+        shape = (at.shape[0], half)
+        return (
+            jnp.dot(one_hot(at, shape, 1), near[...], preferred_element_type=f32)
+            + jnp.dot(one_hot(at - half, shape, 1), across[...], preferred_element_type=f32)
+        ).astype(bf16)
+
+    home[...] = picked(home_at[...])
+    count = by_dest.shape[1]
+    kinds = experts_at.shape[0] // count
+    for kind in range(kinds):
+        rows = picked(experts_at[kind * count : (kind + 1) * count, :])
+        for d in range(kind, by_dest.shape[0], kinds):
+            by_dest[d] = rows
+
+
+def select_rows(experts_at, home_at, near, across, n_x, kinds):
+    vmem = pl.BlockSpec(memory_space=pltpu.VMEM)
+    count, width = experts_at.shape[0] // kinds, near.shape[1]
+    return pl.pallas_call(
+        select_kernel,
+        out_shape=(
+            jax.ShapeDtypeStruct((n_x, count, width), bf16),
+            jax.ShapeDtypeStruct((home_at.shape[0], width), bf16),
+        ),
+        in_specs=[vmem] * 4,
+        out_specs=(vmem, vmem),
+        cost_estimate=pl.CostEstimate(
+            flops=4 * experts_at.shape[0] * near.size,
+            bytes_accessed=4 * near.size,
+            transcendentals=0,
+        ),
+        compiler_params=pltpu.CompilerParams(vmem_limit_bytes=8 << 20),
+        name="select_rows",
+    )(experts_at, home_at, near, across)
+
+
+def projection_kernel(at, attn, mine_a, mine_b, theirs_a, theirs_b, out):
+    half = mine_a.shape[0]
+    chips = 2 * half
     first = at[1] == 0
     rows = attn[...]
-    per_out = out.shape[2] // (2 * mine.shape[1])
+    per_out = out.shape[2] // (2 * mine_a.shape[1])
 
     def block(use_zero, offset, kind):
         spot, n, bit = 0, 1, half // 2
@@ -63,7 +266,10 @@
             spot = spot + lax.rem(lax.div(offset, n), 2) * bit
             n, bit = 2 * n, bit // 2
         spot = spot * 2 + kind
-        return jnp.where(use_zero == first, mine[spot], theirs[spot])
+        low = spot < half
+        a, b = jnp.minimum(spot, half - 1), jnp.maximum(spot - half, 0)
+        ours = jnp.where(low, mine_a[a], mine_b[b])
+        return jnp.where(use_zero == first, ours, jnp.where(low, theirs_a[a], theirs_b[b]))
 
     for dest in range(out.shape[0]):
         blocks = []
@@ -84,20 +290,20 @@
         ).astype(bf16)
 
 
-def project_out(chip, core, attn, mine, theirs, n_x, col_width):
+def project_out(at, attn, halves, n_x, col_width):
     vmem = pl.BlockSpec(memory_space=pltpu.VMEM)
-    flops = 2 * attn.shape[0] * 2 * mine.size
+    size = sum(h.size for h in halves)
     return pl.pallas_call(
         projection_kernel,
         out_shape=jax.ShapeDtypeStruct((n_x, attn.shape[0], col_width), bf16),
-        in_specs=[pl.BlockSpec(memory_space=pltpu.SMEM), vmem, vmem, vmem],
+        in_specs=[pl.BlockSpec(memory_space=pltpu.SMEM), *[vmem] * 5],
         out_specs=vmem,
         cost_estimate=pl.CostEstimate(
-            flops=flops, bytes_accessed=4 * mine.size, transcendentals=0
+            flops=2 * attn.shape[0] * size, bytes_accessed=2 * size, transcendentals=0
         ),
         compiler_params=pltpu.CompilerParams(vmem_limit_bytes=8 << 20),
         name="project_out",
-    )(jnp.stack([chip, core]).astype(i32), attn, mine, theirs)
+    )(at, attn, *halves)
 
 
 def expert_kernel(keep, rows, gate, up, down, got_up, got_down, out):
@@ -192,48 +398,51 @@
     by_head = jnp.transpose(cache, (2, 0, 1, 3)).reshape(kv_heads, block_len, 2 * HD)
     by_head = jnp.repeat(by_head, n_x // kv_heads, axis=0)
     cache_all = exchange(by_head, "tensor")
-    cache_all = cache_all.reshape(n_x * block_len, 2 * HD)
 
     w_own = out_weight.T
     mine = jnp.stack([w_own, across_chips(w_own)])
     shift = chips // 4
-    while shift:
+    while shift > 1:
         mine = jnp.concatenate([mine, along_chips(mine, shift)])
         shift //= 2
-    theirs = other_core(mine)
+    mine_b = along_chips(mine, 1)
+    theirs_a = other_core(mine)
+    theirs_b = other_core(mine_b)
 
     kv_pos = (pos_x * heads_here) // group_size
-    payload = jnp.concatenate(
+    earlier = jnp.arange(tokens)[None, :] < jnp.arange(tokens)[:, None]
+    same = token_prompt[:, None] == token_prompt[None, :]
+    rank = jnp.sum((same & earlier).astype(i32), 1)
+    chunks = (q_cols + 2 * HD + col_width) // HD
+    entries = jnp.concatenate(
+        [jnp.pad(token_prompt, (0, HD - tokens)), route_ids.reshape(-1)]
+    )
+    table_rows = -(-entries.shape[0] // (8 * HD)) * 8
+    table = jnp.pad(entries, (0, HD * HD - entries.shape[0])).astype(bf16).reshape(HD, HD)
+    size = 2 * chunks + table_rows
+    place = token_prompt * size + rank * chunks
+    token_rows = (place[None, :] + jnp.arange(chunks, dtype=i32)[:, None]).reshape(-1)
+    spare = jnp.arange(HD, dtype=i32)
+    target = jnp.stack(
         [
-            lax.dynamic_slice_in_dim(queries, pos_x * q_cols, q_cols, 1),
-            lax.dynamic_slice_in_dim(own_kv, kv_pos * HD, HD, 1),
-            lax.dynamic_slice_in_dim(own_kv, half_cols + kv_pos * HD, HD, 1),
-            lax.dynamic_slice_in_dim(residual, pos_x * col_width, col_width, 1),
-        ],
-        1,
-    )
-    width = payload.shape[1]
-    same = token_prompt[:, None] == token_prompt[None, :]
-    earlier = jnp.arange(tokens)[None, :] < jnp.arange(tokens)[:, None]
-    rank = jnp.sum((same & earlier).astype(i32), 1)
-    place = token_prompt * per_prompt + rank
-    rows = n_e * per_prompt
-    pick = (jnp.arange(rows)[:, None] == place[None, :]).astype(bf16)
-    sent = jnp.dot(pick, payload, preferred_element_type=f32).astype(bf16)
-    table = jnp.concatenate([token_prompt, route_ids.reshape(-1)]).astype(bf16)
-    entries = table.shape[0]
-    table_cols = -(-entries // (per_prompt * HD)) * HD
-    table = jnp.pad(table, (0, per_prompt * table_cols - entries))
-    table = jnp.broadcast_to(
-        table.reshape(1, per_prompt, table_cols), (n_e, per_prompt, table_cols)
-    )
-    sent = jnp.concatenate([sent.reshape(n_e, per_prompt, width), table], 2)
+            jnp.pad(token_rows, (0, HD), constant_values=-1),
+            jnp.concatenate(
+                [
+                    jnp.full((tokens * chunks,), -1, i32),
+                    jnp.where(spare < table_rows, 2 * chunks + spare, -1),
+                ]
+            ),
+        ]
+    )
+    places = jnp.stack([pos_x, kv_pos, kv_heads + kv_pos]).astype(i32)
+    sent = build_payload(
+        places, target, queries, own_kv, residual, table, q_cols, col_width, n_e * size
+    )
     sent, cache_all = lax.optimization_barrier((sent, cache_all))
-    keys, values = cache_all[:, :HD], cache_all[:, HD:]
-    got = exchange(sent, EXPERT)
-    table = got[:, :, width:].reshape(n_e, per_prompt * table_cols)[:, :entries].astype(i32)
-    prompts = table[:, :tokens]
-    routes = table[:, tokens:].reshape(n_e, tokens, picks)
+    got = exchange(sent.reshape(n_e, size, HD), EXPERT)
+    table = got[:, 2 * chunks : 2 * chunks + 1 + tokens * picks // HD, :].astype(i32)
+    prompts = table[:, 0, :tokens]
+    routes = table[:, 1:, :].reshape(n_e, tokens, picks)
 
     owner = jnp.arange(n_e, dtype=i32)
     holds = jnp.any(prompts[None, :, :] == owner[:, None, None], -1)
@@ -246,35 +455,14 @@
     source = jnp.where(prompts % CORES == core, 0, chips) + prompts // CORES
     source = source * tokens + block_order * per_prompt + rank_all
 
-    own_holds = jnp.any(prompts == pos_e, 1)
-    own_order = count_earlier(own_holds[None])[0]
-    slot_here = own_order[:, None] * per_prompt + jnp.arange(per_prompt, dtype=i32)
-    slot_here = jnp.where(own_holds[:, None], slot_here, -1).reshape(rows)
-    compact = (jnp.arange(tokens, dtype=i32)[:, None] == slot_here[None, :]).astype(bf16)
-    got = jnp.dot(
-        compact, got[:, :, :width].reshape(rows, width), preferred_element_type=f32
-    ).astype(bf16)
-
-    q_rows = got[:, :q_cols].reshape(tokens, heads_here, HD)
-    k_own = got[:, q_cols : q_cols + HD].astype(f32)
-    v_own = got[:, q_cols + HD : q_cols + 2 * HD].astype(f32)
-    resid = got[:, q_cols + 2 * HD :].astype(f32)
-    scale = HD ** (-0.5)
-    scores = jnp.einsum("rhd,pd->rhp", q_rows, keys, preferred_element_type=f32) * scale
-    own = jnp.sum(q_rows.astype(f32) * k_own[:, None, :], -1) * scale
-    inside = jnp.arange(n_x * block_len) < prompt_len[0]
-    scores = jnp.where(inside, scores, MASKED_SCORE)
-    top = jnp.maximum(jnp.max(scores, -1), own)
-    weights = jnp.where(inside, jnp.exp(scores - top[..., None]), 0.0)
-    own_weight = jnp.exp(own - top)
-    total = jnp.sum(weights, -1) + own_weight
-    mix = jnp.einsum("rhp,pd->rhd", weights.astype(bf16), values, preferred_element_type=f32)
-    mix = mix + own_weight[..., None] * v_own[:, None, :]
-    attn = (mix / total[..., None]).astype(bf16).reshape(tokens, q_cols)
-
-    partial = project_out(chip, core, attn, mine, theirs, n_x, col_width)
+    at = jnp.concatenate([jnp.stack([pos_e]).astype(i32), prompt_len])
+    attn, resid = attend(
+        at, got.reshape(n_e * size, HD), cache_all, tokens, q_cols, col_width
+    )
+    at = jnp.stack([chip, core]).astype(i32)
+    partial = project_out(at, attn, (mine, mine_b, theirs_a, theirs_b), n_x, col_width)
     parts = exchange(partial, "tensor")
-    hidden = (resid + jnp.sum(parts.astype(f32), 0)).astype(bf16)
+    hidden = hidden_copies(parts, resid, chips)
 
     keep = pos_x % experts_here
     give = 1 - keep
@@ -289,19 +477,22 @@
     down = lax.dynamic_index_in_dim(w_down, give, 0, keepdims=False)
     got_down = lax.ppermute(down, "tensor", swap)
 
-    near = exchange(jnp.broadcast_to(hidden, (chips, *hidden.shape)), "chip")
+    near = exchange(hidden, "chip")
     across = other_core(near)
-    everyone = jnp.concatenate([near, across], 0).reshape(n_e * tokens, col_width)
     mine_e = pos_e * experts_here + jnp.arange(experts_here, dtype=i32)
     named = jnp.any(routes[None] == mine_e[:, None, None, None], -1)
     slot = jnp.where(named, count_earlier(named), -1)
     filled = slot[:, :, None, :] == jnp.arange(capacity, dtype=i32)[None, None, :, None]
     expert_rows = jnp.sum(jnp.where(filled, source[None, :, None, :] + 1, 0), -1) - 1
     home_rows = lax.dynamic_index_in_dim(source, pos_e, 0, keepdims=False)
-    hidden_home = pick_rows(home_rows, everyone)
-    by_expert = pick_rows(expert_rows.reshape(-1), everyone)
-    by_expert = by_expert.reshape(experts_here, n_e * capacity, col_width)
-    by_dest = jnp.tile(by_expert, (n_x // experts_here, 1, 1))
+    by_dest, hidden_home = select_rows(
+        expert_rows.reshape(-1, 1),
+        home_rows.reshape(-1, 1),
+        near.reshape(chips * tokens, col_width),
+        across.reshape(chips * tokens, col_width),
+        n_x,
+        experts_here,
+    )
     rows_in = exchange(by_dest, "tensor")
 
     out = run_expert(keep, rows_in, w_gate, w_up, w_down, got_up, got_down)

time: 275 us -> 274 us (level)
  blocking collectives: 0 us -> 28.1 us
  waiting for transfers between devices: 130 us -> 115 us
  starting transfers between devices: 116 us -> 107 us
  Pallas kernels: 3.73 us -> 8.06 us
  local copies, waits for them, and re-layouts: 12.8 us -> 8.95 us
  other arithmetic: 7 us -> 4.2 us
    all_to_all x0 -> x1, blocking collectives: none -> 28.1 us  [exchange(): return lax.all_to_all(tiles, axis, split_axis=0, concat_axis=0, tiled=True)]
    all_to_all x7 -> x6, waiting for transfers between devices: 59.1 us -> 47.1 us  [exchange(): return lax.all_to_all(tiles, axis, split_axis=0, concat_axis=0, tiled=True)]
    all_to_all x7 -> x6, starting transfers between devices: 47.8 us -> 37.1 us  [exchange(): return lax.all_to_all(tiles, axis, split_axis=0, concat_axis=0, tiled=True)]
    pallas_call x0 -> x4, Pallas kernels: none -> 5.06 us  [the longest x1 2.22 us: attend(): pl.pallas_call(attention_kernel, out_shape=(jax.ShapeDtypeStruct((tokens,...]
    ppermute x3, waiting for transfers between devices: 21.9 us -> 18.4 us  [along_chips(): return lax.ppermute(x, EXPERT, moves)]
    ppermute x2 -> x3, starting transfers between devices: 10.8 us -> 13.7 us  [other_core(): return lax.ppermute(x, 'core', [(0, 1), (1, 0)])]
    unnamed x36 -> x31, local copies, waits for them, and re-layouts: 6.37 us -> 6.06 us
  transfers between devices with their start and end apart: 15 -> 15, of which waited for: 10 -> 9; matrix products, arithmetic and copies ran while one was open for 4% -> 2% of each run, Pallas kernels for 0% -> 1%
where the time goes in v4:
time: 274 us; the launch traced here: 272 us
  waiting for transfers between devices  115 us (42%)
  starting transfers between devices  107 us (39%)
  blocking collectives  28.1 us (10%)
  local copies, waits for them, and re-layouts  8.95 us (3%)
  Pallas kernels  8.06 us (3%)
  other arithmetic  4.2 us (2%)
    all_to_all x6, waiting for transfers between devices, exchange(): return lax.all_to_all(tiles, axis, split_axis=0, concat_axis=0, tiled=True)  47.1 us
    ppermute x1, waiting for transfers between devices, layer(): got_down = lax.ppermute(down, 'tensor', swap)  46.6 us
    ppermute x1, starting transfers between devices, across_chips(): return lax.ppermute(x, EXPERT, moves)  44.5 us
    all_to_all x6, starting transfers between devices, exchange(): return lax.all_to_all(tiles, axis, split_axis=0, concat_axis=0, tiled=True)  37.1 us
    all_to_all x1, blocking collectives, exchange(): return lax.all_to_all(tiles, axis, split_axis=0, concat_axis=0, tiled=True)  28.1 us
    ppermute x3, waiting for transfers between devices, along_chips(): return lax.ppermute(x, EXPERT, moves)  18.4 us
    ppermute x3, starting transfers between devices, other_core(): return lax.ppermute(x, 'core', [(0, 1), (1, 0)])  13.7 us
    unnamed x31, local copies, waits for them, and re-layouts  6.06 us
  transfers between devices with their start and end apart: 15, of which 9 were waited for; matrix products, arithmetic and copies ran while one was open for 2% of the time, Pallas kernels for 1%

profile of v4, /device:TPU:65, one launch (start us, length us, event | category | flops | bytes accessed | tf_op | source)
XLA Modules:
  0.0 272.5 jit_solution(3725508619989986943)
XLA Ops:
  0.0 0.9 reshape_squeeze.3
  1.0 0.7 broadcast_in_dim.57
  1.7 8.0 %all-to-all-start = ((bf16[8,32,256]{2,1,0:T(8,128)(2,1)}), bf16[8,32,256]{2,1,0:T(8,128)(2,1)S(1)}, u32[]{:S(2)}, u32[]{:S(2)}) async-start(bf16[8,32,256]{2,1,0:T(8,128)(2,1)} %bitcast.5), calls=%async_computation | async-start | bytes 262144 | tf_op jit(solution)/shard_map/all_to_all | solution.py:17
  9.7 44.5 %collective-permute-start = (bf16[64,512]{1,0:T(8,128)(2,1)S(1)}, bf16[64,512]{1,0:T(8,128)(2,1)S(1)}, u32[]{:S(2)}, u32[]{:S(2)}) collective-permute-start(bf16[64,512]{1,0:T(8,128)(2,1)S(1)} %bitcast.49), channel_id=1, source_target_pairs={{0,24},{8,240},{16,40},{24,0},{32,56},{40,16},{48,72},{56,32},{64,... | collective-permute-start | bytes 196616 | tf_op jit(solution)/shard_map/ppermute | solution.py:35
  54.2 0.2 convert_reduce_fusion.1
  54.4 1.7 collective-permute-done
  56.1 2.0 collective-permute-start.1
  58.1 0.1 copy.63
  58.2 0.1 reshape.181
  58.3 10.1 %collective-permute-done.1 = bf16[2,64,512]{2,1,0:T(8,128)(2,1)S(1)} collective-permute-done((bf16[2,64,512]{2,1,0:T(8,128)(2,1)S(1)}, bf16[2,64,512]{2,1,0:T(8,128)(2,1)S(1)}, u32[]{:S(2)}, u32[]{:S(2)}) %collective-permute-start.1) | collective-permute-done | bytes 131104 | tf_op jit(solution)/shard_map/ppermute | solution.py:26
  68.4 2.0 collective-permute-start.2
  70.4 0.1 add.129
  70.6 8.3 %collective-permute-done.2 = bf16[4,64,512]{2,1,0:T(8,128)(2,1)S(1)} collective-permute-done((bf16[4,64,512]{2,1,0:T(8,128)(2,1)S(1)}, bf16[4,64,512]{2,1,0:T(8,128)(2,1)S(1)}, u32[]{:S(2)}, u32[]{:S(2)}) %collective-permute-start.2) | collective-permute-done | bytes 262176 | tf_op jit(solution)/shard_map/ppermute | solution.py:26
  79.0 2.0 collective-permute-start.3
  80.9 0.1 pad_add_fusion.1.places
  81.0 1.6 build_payload.1
  82.6 5.6 %all-to-all-start.1 = ((bf16[32,24,128]{2,1,0:T(8,128)(2,1)}), bf16[32,24,128]{2,1,0:T(8,128)(2,1)S(1)}, u32[]{:S(2)}, u32[]{:S(2)}) async-start(bf16[32,24,128]{2,1,0:T(8,128)(2,1)} %bitcast.6), calls=%async_computation.1 | async-start | bytes 393216 | tf_op jit(solution)/shard_map/all_to_all | solution.py:17
  88.9 2.9 %collective-permute-start.4 = (bf16[8,64,512]{2,1,0:T(8,128)(2,1)S(1)}, bf16[8,64,512]{2,1,0:T(8,128)(2,1)S(1)}, u32[]{:S(2)}, u32[]{:S(2)}) collective-permute-start(bf16[8,64,512]{2,1,0:T(8,128)(2,1)S(1)} %pad_maximum_fusion.1.mine_a), channel_id=1, source_target_pairs={{0,8},{8,0},{1,9},{9,1},{2,10},{10,2},{3,11},{11,3},{4,12},{12,4},... | collective-permute-start | bytes 1572872 | tf_op jit(solution)/shard_map/ppermute | solution.py:39
  91.9 2.0 collective-permute-start.5
  94.0 12.5 %all-to-all-done.1 = bf16[32,24,128]{2,1,0:T(8,128)(2,1)S(1)} async-done(((bf16[32,24,128]{2,1,0:T(8,128)(2,1)}), bf16[32,24,128]{2,1,0:T(8,128)(2,1)S(1)}, u32[]{:S(2)}, u32[]{:S(2)}) %all-to-all-start.1) | async-done | bytes 196640 | tf_op jit(solution)/shard_map/all_to_all | solution.py:17
  106.5 2.2 attend.1
  108.8 2.1 project_out.1
  110.9 7.6 %all-to-all-start.2 = ((bf16[8,32,256]{2,1,0:T(8,128)(2,1)}), bf16[8,32,256]{2,1,0:T(8,128)(2,1)S(1)}, u32[]{:S(2)}, u32[]{:S(2)}) async-start(bf16[8,32,256]{2,1,0:T(8,128)(2,1)} %project_out.1), calls=%async_computation.2 | async-start | bytes 262144 | tf_op jit(solution)/shard_map/all_to_all | solution.py:17
  118.5 0.1 copy.66
  118.6 0.1 copy.67
  118.7 0.6 fusion.2
  119.4 7.1 %all-to-all-done.2.parts = bf16[8,32,256]{2,1,0:T(8,128)(2,1)S(1)} async-done(((bf16[8,32,256]{2,1,0:T(8,128)(2,1)}), bf16[8,32,256]{2,1,0:T(8,128)(2,1)S(1)}, u32[]{:S(2)}, u32[]{:S(2)}) %all-to-all-start.2) | async-done | bytes 131104 | tf_op jit(solution)/shard_map/all_to_all | solution.py:17
  126.4 0.7 hidden_copies.1
  127.2 4.3 %all-to-all-start.3 = ((bf16[16,32,256]{2,1,0:T(8,128)(2,1)}), bf16[16,32,256]{2,1,0:T(8,128)(2,1)S(1)}, u32[]{:S(2)}, u32[]{:S(2)}) async-start(bf16[16,32,256]{2,1,0:T(8,128)(2,1)} %hidden_copies.1), calls=%async_computation.3 | async-start | bytes 524288 | tf_op jit(solution)/shard_map/all_to_all | solution.py:17
  131.5 0.2 compare_reduce_fusion
  131.7 0.2 convolution_convert_fusion.1
  131.9 1.3 select_reduce_fusion
  133.2 0.1 fusion
  133.4 0.3 select_reduce_fusion.1
  133.6 10.4 %all-to-all-done.3 = bf16[16,32,256]{2,1,0:T(8,128)(2,1)S(1)} async-done(((bf16[16,32,256]{2,1,0:T(8,128)(2,1)}), bf16[16,32,256]{2,1,0:T(8,128)(2,1)S(1)}, u32[]{:S(2)}, u32[]{:S(2)}) %all-to-all-start.3) | async-done | bytes 262176 | tf_op jit(solution)/shard_map/all_to_all | solution.py:17
  144.0 8.9 %collective-permute-start.6 = (bf16[16,32,256]{2,1,0:T(8,128)(2,1)S(1)}, bf16[16,32,256]{2,1,0:T(8,128)(2,1)S(1)}, u32[]{:S(2)}, u32[]{:S(2)}) collective-permute-start(bf16[16,32,256]{2,1,0:T(8,128)(2,1)S(1)} %all-to-all-done.3), channel_id=1, source_target_pairs={{0,8},{8,0},{1,9},{9,1},{2,10},{10,2},{3,11},{11,3},{4,12},{12,4},... | collective-permute-start | bytes 786440 | tf_op jit(solution)/shard_map/ppermute | solution.py:39
  152.9 0.1 copy.68
  153.0 0.1 sub.24.experts_at
  153.2 0.1 copy.70.home_at
  153.2 0.8 collective-permute-done.6
  154.0 0.5 select_rows.1
  154.5 0.9 copy-done.6
  155.5 3.8 %all-to-all-start.4 = ((bf16[8,192,256]{2,1,0:T(8,128)(2,1)}), bf16[8,192,256]{2,1,0:T(8,128)(2,1)S(1)}, u32[]{:S(2)}, u32[]{:S(2)}) async-start(bf16[8,192,256]{2,1,0:T(8,128)(2,1)} %copy-done.6), calls=%async_computation.4 | async-start | bytes 1572864 | tf_op jit(solution)/shard_map/all_to_all | solution.py:17
  159.4 0.1 pad_maximum_fusion
  159.5 3.2 %collective-permute-start.7 = (bf16[2,2048,128]{2,1,0:T(8,128)(2,1)S(1)}, bf16[2,2048,128]{2,1,0:T(8,128)(2,1)S(1)}, u32[]{:S(2)}, u32[]{:S(2)}) collective-permute-start(bf16[2,2048,128]{2,1,0:T(8,128)(2,1)S(1)} %pad_maximum_fusion), channel_id=1, source_target_pairs={{0,1},{1,0},{2,3},{3,2},{4,5},{5,4},{6,7},{7,6},{8,9},{9,8},{10,11... | collective-permute-start | bytes 3145736 | tf_op jit(solution)/shard_map/ppermute | solution.py:476
  162.8 2.2 collective-permute-start.8
  165.0 46.6 %collective-permute-done.8.got_down = bf16[128,2048]{1,0:T(8,128)(2,1)S(1)} collective-permute-done((bf16[128,2048]{1,0:T(8,128)(2,1)S(1)}, bf16[128,2048]{1,0:T(8,128)(2,1)S(1)}, u32[]{:S(2)}, u32[]{:S(2)}) %collective-permute-start.8) | collective-permute-done | bytes 524320 | tf_op jit(solution)/shard_map/ppermute | solution.py:478
  211.6 1.0 copy-done.4
  212.6 1.2 copy-done.3
  213.8 1.2 copy-done.5
  215.0 0.9 run_expert.1
  215.9 28.1 %all_to_all.35 = bf16[8,192,256]{2,1,0:T(8,128)(2,1)S(1)} all-to-all(bf16[8,192,256]{2,1,0:T(8,128)(2,1)S(1)} %run_expert.1), channel_id=1, replica_groups=mesh['groups'=2,'chip'=16,'core'=2,'tensor'=8] {'tensor'}, dimensions={0} | all-to-all | bytes 1572864 | tf_op jit(solution)/shard_map/all_to_all | solution.py:17
  244.1 0.2 reduce.1
  244.2 0.9 copy.77
  245.1 7.8 %all-to-all-start.6 = ((bf16[32,2,6,256]{3,1,2,0:T(2,128)(2,1)}), bf16[32,2,6,256]{3,1,2,0:T(2,128)(2,1)S(1)}, u32[]{:S(2)}, u32[]{:S(2)}) async-start(bf16[32,2,6,256]{3,1,2,0:T(2,128)(2,1)} %bitcast.25), calls=%async_computation.6 | async-start | bytes 393216 | tf_op jit(solution)/shard_map/all_to_all | solution.py:17
  253.0 0.6 copy-done.12
  253.7 0.1 select_reduce_fusion.2
  253.8 0.1 copy.74
  253.9 0.1 fusion.4
  254.1 0.1 fusion.1
  254.2 0.1 copy.72
  254.4 17.1 %all-to-all-done.6 = bf16[32,2,6,256]{3,1,2,0:T(2,128)(2,1)S(1)} async-done(((bf16[32,2,6,256]{3,1,2,0:T(2,128)(2,1)}), bf16[32,2,6,256]{3,1,2,0:T(2,128)(2,1)S(1)}, u32[]{:S(2)}, u32[]{:S(2)}) %all-to-all-start.6) | async-done | bytes 196640 | tf_op jit(solution)/shard_map/all_to_all | solution.py:17
  271.6 0.3 fusion.21
  271.9 0.6 add_convert_fusion
  (64 shorter events, 1.0 us)
Async XLA Ops:
  1.7 8.0 %copy-start.10 = (bf16[512,64]{0,1:T(8,128)(2,1)S(1)}, bf16[512,64]{0,1:T(8,128)(2,1)}, u32[]{:S(2)}) copy-start(bf16[512,64]{0,1:T(8,128)(2,1)} %param.18) | copy-start | bytes 196612
  1.7 81.0 %all-to-all-start = ((bf16[8,32,256]{2,1,0:T(8,128)(2,1)}), bf16[8,32,256]{2,1,0:T(8,128)(2,1)S(1)}, u32[]{:S(2)}, u32[]{:S(2)}) async-start(bf16[8,32,256]{2,1,0:T(8,128)(2,1)} %bitcast.5), calls=%async_computation | async-start | bytes 262144 | tf_op jit(solution)/shard_map/all_to_all | solution.py:17
  9.6 44.5 %copy-start.13 = (s32[32]{0:T(128)S(1)}, s32[32]{0:T(128)}, u32[]{:S(2)}) copy-start(s32[32]{0:T(128)} %param.16) | copy-start | bytes 388
  9.7 46.5 %collective-permute-start = (bf16[64,512]{1,0:T(8,128)(2,1)S(1)}, bf16[64,512]{1,0:T(8,128)(2,1)S(1)}, u32[]{:S(2)}, u32[]{:S(2)}) collective-permute-start(bf16[64,512]{1,0:T(8,128)(2,1)S(1)} %bitcast.49), channel_id=1, source_target_pairs={{0,24},{8,240},{16,40},{24,0},{32,56},{40,16},{48,72},{56,32},{64,... | collective-permute-start | bytes 196616 | tf_op jit(solution)/shard_map/ppermute | solution.py:35
  56.1 2.0 copy-start.11
  56.1 12.3 %collective-permute-start.1 = (bf16[2,64,512]{2,1,0:T(8,128)(2,1)S(1)}, bf16[2,64,512]{2,1,0:T(8,128)(2,1)S(1)}, u32[]{:S(2)}, u32[]{:S(2)}) collective-permute-start(bf16[2,64,512]{2,1,0:T(8,128)(2,1)S(1)} %pad_maximum_fusion.3), channel_id=1, source_target_pairs={{0,192},{8,72},{16,208},{24,88},{32,224},{40,104},{48,240},{56,120... | collective-permute-start | bytes 393224 | tf_op jit(solution)/shard_map/ppermute | solution.py:26
  68.4 10.5 %collective-permute-start.2 = (bf16[4,64,512]{2,1,0:T(8,128)(2,1)S(1)}, bf16[4,64,512]{2,1,0:T(8,128)(2,1)S(1)}, u32[]{:S(2)}, u32[]{:S(2)}) collective-permute-start(bf16[4,64,512]{2,1,0:T(8,128)(2,1)S(1)} %pad_maximum_fusion.2), channel_id=1, source_target_pairs={{0,224},{8,40},{16,240},{24,56},{32,0},{40,72},{48,16},{56,88},{64... | collective-permute-start | bytes 786440 | tf_op jit(solution)/shard_map/ppermute | solution.py:26
  70.6 10.4 %copy-start.7 = (bf16[32,4096]{1,0:T(8,128)(2,1)S(1)}, bf16[32,4096]{1,0:T(8,128)(2,1)}, u32[]{:S(2)}) copy-start(bf16[32,4096]{1,0:T(8,128)(2,1)} %q.1) | copy-start | bytes 786436
  70.6 10.4 %copy-start.8 = (bf16[32,1024]{1,0:T(8,128)(2,1)S(1)}, bf16[32,1024]{1,0:T(8,128)(2,1)}, u32[]{:S(2)}) copy-start(bf16[32,1024]{1,0:T(8,128)(2,1)} %v.1) | copy-start | bytes 196612
  70.6 10.4 %copy-start.9 = (bf16[32,2048]{1,0:T(8,128)(2,1)S(1)}, bf16[32,2048]{1,0:T(8,128)(2,1)}, u32[]{:S(2)}) copy-start(bf16[32,2048]{1,0:T(8,128)(2,1)} %resid.1) | copy-start | bytes 393220
  79.0 12.9 %collective-permute-start.3 = (bf16[8,64,512]{2,1,0:T(8,128)(2,1)S(1)}, bf16[8,64,512]{2,1,0:T(8,128)(2,1)S(1)}, u32[]{:S(2)}, u32[]{:S(2)}) collective-permute-start(bf16[8,64,512]{2,1,0:T(8,128)(2,1)S(1)} %pad_maximum_fusion.1.mine_a), channel_id=1, source_target_pairs={{0,240},{8,24},{16,0},{24,40},{32,16},{40,56},{48,32},{56,72},{64,... | collective-permute-start | bytes 1572872 | tf_op jit(solution)/shard_map/ppermute | solution.py:26
  82.6 23.9 %all-to-all-start.1 = ((bf16[32,24,128]{2,1,0:T(8,128)(2,1)}), bf16[32,24,128]{2,1,0:T(8,128)(2,1)S(1)}, u32[]{:S(2)}, u32[]{:S(2)}) async-start(bf16[32,24,128]{2,1,0:T(8,128)(2,1)} %bitcast.6), calls=%async_computation.1 | async-start | bytes 393216 | tf_op jit(solution)/shard_map/all_to_all | solution.py:17
  88.9 19.8 %collective-permute-start.4 = (bf16[8,64,512]{2,1,0:T(8,128)(2,1)S(1)}, bf16[8,64,512]{2,1,0:T(8,128)(2,1)S(1)}, u32[]{:S(2)}, u32[]{:S(2)}) collective-permute-start(bf16[8,64,512]{2,1,0:T(8,128)(2,1)S(1)} %pad_maximum_fusion.1.mine_a), channel_id=1, source_target_pairs={{0,8},{8,0},{1,9},{9,1},{2,10},{10,2},{3,11},{11,3},{4,12},{12,4},... | collective-permute-start | bytes 1572872 | tf_op jit(solution)/shard_map/ppermute | solution.py:39
  91.9 16.9 %collective-permute-start.5 = (bf16[8,64,512]{2,1,0:T(8,128)(2,1)S(1)}, bf16[8,64,512]{2,1,0:T(8,128)(2,1)S(1)}, u32[]{:S(2)}, u32[]{:S(2)}) collective-permute-start(bf16[8,64,512]{2,1,0:T(8,128)(2,1)S(1)} %collective-permute-done.3.mine_b), channel_id=1, source_target_pairs={{0,8},{8,0},{1,9},{9,1},{2,10},{10,2},{3,11},{11,3},{4,12},{12,4},... | collective-permute-start | bytes 1572872 | tf_op jit(solution)/shard_map/ppermute | solution.py:39
  110.9 15.5 %all-to-all-start.2 = ((bf16[8,32,256]{2,1,0:T(8,128)(2,1)}), bf16[8,32,256]{2,1,0:T(8,128)(2,1)S(1)}, u32[]{:S(2)}, u32[]{:S(2)}) async-start(bf16[8,32,256]{2,1,0:T(8,128)(2,1)} %project_out.1), calls=%async_computation.2 | async-start | bytes 262144 | tf_op jit(solution)/shard_map/all_to_all | solution.py:17
  127.2 16.9 %all-to-all-start.3 = ((bf16[16,32,256]{2,1,0:T(8,128)(2,1)}), bf16[16,32,256]{2,1,0:T(8,128)(2,1)S(1)}, u32[]{:S(2)}, u32[]{:S(2)}) async-start(bf16[16,32,256]{2,1,0:T(8,128)(2,1)} %hidden_copies.1), calls=%async_computation.3 | async-start | bytes 524288 | tf_op jit(solution)/shard_map/all_to_all | solution.py:17
  144.0 10.0 %collective-permute-start.6 = (bf16[16,32,256]{2,1,0:T(8,128)(2,1)S(1)}, bf16[16,32,256]{2,1,0:T(8,128)(2,1)S(1)}, u32[]{:S(2)}, u32[]{:S(2)}) collective-permute-start(bf16[16,32,256]{2,1,0:T(8,128)(2,1)S(1)} %all-to-all-done.3), channel_id=1, source_target_pairs={{0,8},{8,0},{1,9},{9,1},{2,10},{10,2},{3,11},{11,3},{4,12},{12,4},... | collective-permute-start | bytes 786440 | tf_op jit(solution)/shard_map/ppermute | solution.py:39
  154.0 5.2 %copy-start = (bf16[2,2048,128]{2,1,0:T(8,128)(2,1)S(1)}, bf16[2,2048,128]{2,1,0:T(8,128)(2,1)}, u32[]{:S(2)}) copy-start(bf16[2,2048,128]{2,1,0:T(8,128)(2,1)} %gate.1) | copy-start | bytes 3145732
  154.0 5.2 %copy-start.1 = (bf16[2,2048,128]{2,1,0:T(8,128)(2,1)S(1)}, bf16[2,2048,128]{2,1,0:T(8,128)(2,1)}, u32[]{:S(2)}) copy-start(bf16[2,2048,128]{2,1,0:T(8,128)(2,1)} %up.1) | copy-start | bytes 3145732
  154.5 0.9 copy-start.6
  155.5 57.1 %all-to-all-start.4 = ((bf16[8,192,256]{2,1,0:T(8,128)(2,1)}), bf16[8,192,256]{2,1,0:T(8,128)(2,1)S(1)}, u32[]{:S(2)}, u32[]{:S(2)}) async-start(bf16[8,192,256]{2,1,0:T(8,128)(2,1)} %copy-done.6), calls=%async_computation.4 | async-start | bytes 1572864 | tf_op jit(solution)/shard_map/all_to_all | solution.py:17
  159.3 3.4 %copy-start.2 = (bf16[2,128,2048]{2,1,0:T(8,128)(2,1)S(1)}, bf16[2,128,2048]{2,1,0:T(8,128)(2,1)}, u32[]{:S(2)}) copy-start(bf16[2,128,2048]{2,1,0:T(8,128)(2,1)} %down.1) | copy-start | bytes 3145732
  159.5 52.1 %collective-permute-start.7 = (bf16[2,2048,128]{2,1,0:T(8,128)(2,1)S(1)}, bf16[2,2048,128]{2,1,0:T(8,128)(2,1)S(1)}, u32[]{:S(2)}, u32[]{:S(2)}) collective-permute-start(bf16[2,2048,128]{2,1,0:T(8,128)(2,1)S(1)} %pad_maximum_fusion), channel_id=1, source_target_pairs={{0,1},{1,0},{2,3},{3,2},{4,5},{5,4},{6,7},{7,6},{8,9},{9,8},{10,11... | collective-permute-start | bytes 3145736 | tf_op jit(solution)/shard_map/ppermute | solution.py:476
  162.8 48.8 %collective-permute-start.8 = (bf16[128,2048]{1,0:T(8,128)(2,1)S(1)}, bf16[128,2048]{1,0:T(8,128)(2,1)S(1)}, u32[]{:S(2)}, u32[]{:S(2)}) collective-permute-start(bf16[128,2048]{1,0:T(8,128)(2,1)S(1)} %dynamic-slice_bitcast_fusion), channel_id=1, source_target_pairs={{0,1},{1,0},{2,3},{3,2},{4,5},{5,4},{6,7},{7,6},{8,9},{9,8},{10,11... | collective-permute-start | bytes 1572872 | tf_op jit(solution)/shard_map/ppermute | solution.py:478
  211.6 1.0 copy-start.4
  212.6 1.2 copy-start.3
  213.8 1.2 copy-start.5
  245.1 26.3 %all-to-all-start.6 = ((bf16[32,2,6,256]{3,1,2,0:T(2,128)(2,1)}), bf16[32,2,6,256]{3,1,2,0:T(2,128)(2,1)S(1)}, u32[]{:S(2)}, u32[]{:S(2)}) async-start(bf16[32,2,6,256]{3,1,2,0:T(2,128)(2,1)} %bitcast.25), calls=%async_computation.6 | async-start | bytes 393216 | tf_op jit(solution)/shard_map/all_to_all | solution.py:17
  252.9 0.7 copy-start.12

commit v5 on v4

--- a/solution.py
+++ b/solution.py
@@ -306,33 +306,71 @@
     )(at, attn, *halves)
 
 
-def expert_kernel(keep, rows, gate, up, down, got_up, got_down, out):
+def give_kernel(give, gate, up, down, out):
+    out[0] = gate[0]
+    out[1] = up[0]
+    ff = down.shape[1]
+    for t in range(down.shape[2] // HD):
+        out[2, t * ff : (t + 1) * ff, :] = down[0, :, t * HD : (t + 1) * HD]
+
+
+def give_weights(give, gate, up, down):
+    def part(x):
+        return pl.BlockSpec((1, *x.shape[1:]), lambda i, k: (k[0], 0, 0))
+
+    shape = (3, *gate.shape[1:])
+    return pl.pallas_call(
+        give_kernel,
+        out_shape=jax.ShapeDtypeStruct(shape, bf16),
+        grid_spec=pltpu.PrefetchScalarGridSpec(
+            num_scalar_prefetch=1,
+            grid=(1,),
+            in_specs=[part(gate), part(up), part(down)],
+            out_specs=pl.BlockSpec(shape, lambda i, k: (0, 0, 0)),
+        ),
+        cost_estimate=pl.CostEstimate(
+            flops=gate.size, bytes_accessed=6 * gate.size, transcendentals=0
+        ),
+        compiler_params=pltpu.CompilerParams(vmem_limit_bytes=12 << 20),
+        name="give_weights",
+    )(jnp.reshape(give, (1,)).astype(i32), gate, up, down)
+
+
+def expert_kernel(keep, rows, gate, up, got, down_hbm, out, down, sem):
     n_x, count, col_width = rows.shape
     ff = gate.shape[2]
+    copy = pltpu.make_async_copy(down_hbm.at[keep[0]], down, sem)
+    copy.start()
     total = jnp.zeros((count, 4 * ff), f32)
     for s in range(n_x):
         at = pl.ds(s * col_width, col_width)
         weight = jnp.concatenate(
-            [gate[0, at, :], got_up[0, at, :], up[0, at, :], got_up[1, at, :]], 1
+            [gate[0, at, :], got[0, at, :], up[0, at, :], got[1, at, :]], 1
         )
         total = total + jnp.dot(rows[s], weight, preferred_element_type=f32)
     gates, ups = total[:, : 2 * ff], total[:, 2 * ff :]
     act = (gates / (1.0 + jnp.exp(-gates)) * ups).astype(bf16)
+    copy.wait()
+    tiles = col_width // HD
     for d in range(n_x):
-        at = pl.ds(d * col_width, col_width)
-        weight = jnp.concatenate([down[0, :, at], got_down[:, at]], 0)
+        theirs = [
+            got[2, pl.ds((d * tiles + t) * ff, ff), :] for t in range(tiles)
+        ]
+        weight = jnp.concatenate(
+            [down[:, pl.ds(d * col_width, col_width)], jnp.concatenate(theirs, 1)], 0
+        )
         out[d] = jnp.dot(act, weight, preferred_element_type=f32).astype(bf16)
 
 
-def run_expert(keep, rows, gate, up, down, got_up, got_down):
+def run_expert(keep, rows, gate, up, down, got):
     def whole(x):
         return pl.BlockSpec(x.shape, lambda i, k: (0,) * x.ndim)
 
     def kept(x):
         return pl.BlockSpec((1, *x.shape[1:]), lambda i, k: (k[0], 0, 0))
 
-    flops = 2 * rows.size * got_up.shape[2] * 4 + 2 * rows.size * got_down.shape[0] * 2
-    moved = 2 * (2 * rows.size + got_up.size + got_down.size) + 3 * gate.size
+    flops = 2 * rows.size * gate.shape[2] * 6
+    moved = 2 * (2 * rows.size + got.size) + 3 * gate.size
     return pl.pallas_call(
         expert_kernel,
         out_shape=jax.ShapeDtypeStruct(rows.shape, bf16),
@@ -343,18 +381,21 @@
                 whole(rows),
                 kept(gate),
                 kept(up),
-                kept(down),
-                whole(got_up),
-                whole(got_down),
+                whole(got),
+                pl.BlockSpec(memory_space=pl.ANY),
             ],
             out_specs=whole(rows),
+            scratch_shapes=[
+                pltpu.VMEM(down.shape[1:], bf16),
+                pltpu.SemaphoreType.DMA,
+            ],
         ),
         cost_estimate=pl.CostEstimate(
             flops=flops, bytes_accessed=moved, transcendentals=rows.shape[1] * 2 * HD
         ),
         compiler_params=pltpu.CompilerParams(vmem_limit_bytes=16 << 20),
         name="run_expert",
-    )(jnp.reshape(keep, (1,)).astype(i32), rows, gate, up, down, got_up, got_down)
+    )(jnp.reshape(keep, (1,)).astype(i32), rows, gate, up, got, down)
 
 
 def layer(
@@ -467,15 +508,8 @@
     keep = pos_x % experts_here
     give = 1 - keep
     swap = [(i, i ^ 1) for i in range(n_x)]
-    up_pair = jnp.stack(
-        [
-            lax.dynamic_index_in_dim(w_gate, give, 0, keepdims=False),
-            lax.dynamic_index_in_dim(w_up, give, 0, keepdims=False),
-        ]
-    )
-    got_up = lax.ppermute(up_pair, "tensor", swap)
-    down = lax.dynamic_index_in_dim(w_down, give, 0, keepdims=False)
-    got_down = lax.ppermute(down, "tensor", swap)
+    giving = give_weights(give, w_gate, w_up, w_down)
+    got_weights = lax.ppermute(giving, "tensor", swap)
 
     near = exchange(hidden, "chip")
     across = other_core(near)
@@ -495,7 +529,7 @@
     )
     rows_in = exchange(by_dest, "tensor")
 
-    out = run_expert(keep, rows_in, w_gate, w_up, w_down, got_up, got_down)
+    out = run_expert(keep, rows_in, w_gate, w_up, w_down, got_weights)
     parts = exchange(out, "tensor")
     parts = parts.reshape(n_x // experts_here, experts_here, n_e, capacity, col_width)
     summed = jnp.sum(parts.astype(f32), 0).astype(bf16)

time: 274 us -> 265 us (0.967)
  waiting for transfers between devices: 115 us -> 86.5 us
  other arithmetic: 4.2 us -> 15.2 us
  Pallas kernels: 8.06 us -> 13.4 us
  starting transfers between devices: 107 us -> 112 us
    ppermute x2 -> x1, waiting for transfers between devices: 46.6 us -> 0.01 us  [layer(): got_weights = lax.ppermute(giving, 'tensor', swap)]
    all_to_all x6, waiting for transfers between devices: 47.1 us -> 68.4 us  [exchange(): return lax.all_to_all(tiles, axis, split_axis=0, concat_axis=0, tiled=True)]
    all_to_all x6, starting transfers between devices: 37.1 us -> 44.3 us  [exchange(): return lax.all_to_all(tiles, axis, split_axis=0, concat_axis=0, tiled=True)]
    concatenate x2, other arithmetic: 0.08 us -> 3.52 us  [layer(): mine = jnp.concatenate([mine, along_chips(mine, shift)])]
    unnamed x31 -> x27, local copies, waits for them, and re-layouts: 6.06 us -> 4.41 us
  transfers between devices with their start and end apart: 15 -> 14, of which waited for: 9 -> 8; matrix products, arithmetic and copies ran while one was open for 2% -> 7% of each run, Pallas kernels for 1% -> 4%
where the time goes in v5:
time: 265 us; the launch traced here: 263 us
  starting transfers between devices  112 us (42%)
  waiting for transfers between devices  86.5 us (33%)
  blocking collectives  25.5 us (10%)
  other arithmetic  15.2 us (6%)
  Pallas kernels  13.4 us (5%)
  local copies, waits for them, and re-layouts  8.52 us (3%)
    all_to_all x6, waiting for transfers between devices, exchange(): return lax.all_to_all(tiles, axis, split_axis=0, concat_axis=0, tiled=True)  68.4 us
    ppermute x1, starting transfers between devices, across_chips(): return lax.ppermute(x, EXPERT, moves)  44.5 us
    all_to_all x6, starting transfers between devices, exchange(): return lax.all_to_all(tiles, axis, split_axis=0, concat_axis=0, tiled=True)  44.3 us
    all_to_all x1, blocking collectives, exchange(): return lax.all_to_all(tiles, axis, split_axis=0, concat_axis=0, tiled=True)  25.5 us
    ppermute x3, waiting for transfers between devices, along_chips(): return lax.ppermute(x, EXPERT, moves)  17.8 us
    ppermute x3, starting transfers between devices, other_core(): return lax.ppermute(x, 'core', [(0, 1), (1, 0)])  14 us
    ppermute x3, starting transfers between devices, along_chips(): return lax.ppermute(x, EXPERT, moves)  5.82 us
  transfers between devices with their start and end apart: 14, of which 8 were waited for; matrix products, arithmetic and copies ran while one was open for 7% of the time, Pallas kernels for 4%

profile of v5, /device:TPU:65, one launch (start us, length us, event | category | flops | bytes accessed | tf_op | source)
XLA Modules:
  0.0 263.3 jit_solution(12710544684045983392)
XLA Ops:
  0.0 0.9 reshape_squeeze.3
  1.0 0.6 broadcast_in_dim.57
  1.7 7.9 %all-to-all-start = ((bf16[8,32,256]{2,1,0:T(8,128)(2,1)}), bf16[8,32,256]{2,1,0:T(8,128)(2,1)}, u32[]{:S(2)}, u32[]{:S(2)}) async-start(bf16[8,32,256]{2,1,0:T(8,128)(2,1)} %bitcast.5), calls=%async_computation | async-start | bytes 262144 | tf_op jit(solution)/shard_map/all_to_all | solution.py:17
  9.6 44.5 %collective-permute-start = (bf16[64,512]{1,0:T(8,128)(2,1)}, bf16[64,512]{1,0:T(8,128)(2,1)S(1)}, u32[]{:S(2)}, u32[]{:S(2)}) collective-permute-start(bf16[64,512]{1,0:T(8,128)(2,1)} %bitcast.47), channel_id=1, source_target_pairs={{0,24},{8,240},{16,40},{24,0},{32,56},{40,16},{48,72},{56,32},{64,... | collective-permute-start | bytes 196616 | tf_op jit(solution)/shard_map/ppermute | solution.py:35
  54.1 0.9 convert_reduce_fusion.1
  55.0 1.3 fusion.19
  56.2 0.6 copy-done.9
  56.9 1.7 pad_maximum_fusion.2
  58.5 1.9 collective-permute-start.1
  60.5 0.7 convert.13
  61.2 0.1 copy.63
  61.3 0.1 reshape.184
  61.4 0.7 fusion.17
  62.0 9.1 %collective-permute-done.1 = bf16[2,64,512]{2,1,0:T(8,128)(2,1)} collective-permute-done((bf16[2,64,512]{2,1,0:T(8,128)(2,1)}, bf16[2,64,512]{2,1,0:T(8,128)(2,1)}, u32[]{:S(2)}, u32[]{:S(2)}) %collective-permute-start.1) | collective-permute-done | bytes 131104 | tf_op jit(solution)/shard_map/ppermute | solution.py:26
  71.2 1.7 pad_maximum_fusion.1
  72.9 1.9 collective-permute-start.2
  75.0 8.6 %collective-permute-done.2 = bf16[4,64,512]{2,1,0:T(8,128)(2,1)} collective-permute-done((bf16[4,64,512]{2,1,0:T(8,128)(2,1)}, bf16[4,64,512]{2,1,0:T(8,128)(2,1)}, u32[]{:S(2)}, u32[]{:S(2)}) %collective-permute-start.2) | collective-permute-done | bytes 262176 | tf_op jit(solution)/shard_map/ppermute | solution.py:26
  83.6 1.8 pad_maximum_fusion.mine_a
  85.5 1.9 collective-permute-start.3
  87.5 0.9 copy-done.7
  88.4 1.6 build_payload.1
  90.0 5.7 %all-to-all-start.1 = ((bf16[32,24,128]{2,1,0:T(8,128)(2,1)}), bf16[32,24,128]{2,1,0:T(8,128)(2,1)S(1)}, u32[]{:S(2)}, u32[]{:S(2)}) async-start(bf16[32,24,128]{2,1,0:T(8,128)(2,1)} %bitcast.6), calls=%async_computation.1 | async-start | bytes 393216 | tf_op jit(solution)/shard_map/all_to_all | solution.py:17
  95.8 1.3 give_weights.1
  97.1 3.6 %collective-permute-start.7 = (bf16[3,2048,128]{2,1,0:T(8,128)(2,1)}, bf16[3,2048,128]{2,1,0:T(8,128)(2,1)}, u32[]{:S(2)}, u32[]{:S(2)}) collective-permute-start(bf16[3,2048,128]{2,1,0:T(8,128)(2,1)} %give_weights.1), channel_id=1, source_target_pairs={{0,1},{1,0},{2,3},{3,2},{4,5},{5,4},{6,7},{7,6},{8,9},{9,8},{10,11... | collective-permute-start | bytes 4718600 | tf_op jit(solution)/shard_map/ppermute | solution.py:512
  101.3 0.5 iota_add_fusion.2
  101.8 3.2 %collective-permute-start.4 = (bf16[8,64,512]{2,1,0:T(8,128)(2,1)}, bf16[8,64,512]{2,1,0:T(8,128)(2,1)}, u32[]{:S(2)}, u32[]{:S(2)}) collective-permute-start(bf16[8,64,512]{2,1,0:T(8,128)(2,1)} %pad_maximum_fusion.mine_a), channel_id=1, source_target_pairs={{0,8},{8,0},{1,9},{9,1},{2,10},{10,2},{3,11},{11,3},{4,12},{12,4},... | collective-permute-start | bytes 1572872 | tf_op jit(solution)/shard_map/ppermute | solution.py:39
  105.1 2.0 collective-permute-start.5
  107.2 0.6 iota_compare_fusion.6
  107.8 6.6 %all-to-all-done.1 = bf16[32,24,128]{2,1,0:T(8,128)(2,1)S(1)} async-done(((bf16[32,24,128]{2,1,0:T(8,128)(2,1)}), bf16[32,24,128]{2,1,0:T(8,128)(2,1)S(1)}, u32[]{:S(2)}, u32[]{:S(2)}) %all-to-all-start.1) | async-done | bytes 196640 | tf_op jit(solution)/shard_map/all_to_all | solution.py:17
  114.4 2.6 attend.1
  117.0 3.1 %project_out.1 = bf16[8,32,256]{2,1,0:T(8,128)(2,1)} custom-call(s32[2]{0:T(128)S(1)} %pad_add_fusion.2.at, bf16[32,512]{1,0:T(8,128)(2,1)S(1)} %get-tuple-element.13.attn, bf16[8,64,512]{2,1,0:T(8,128)(2,1)} %pad_maximum_fusion.mine_a, bf16[8,64,512]{2,1,0:T(8,128)(2,1)} %collective-permute-done.3.mine_b, ...), custom_call_target="tpu_custom_call" | custom-call | flops 67108864 | bytes 2097152 | tf_op jit(solution)/shard_map/project_out/pallas_call | solution.py:296
  120.1 7.0 %all-to-all-start.2 = ((bf16[8,32,256]{2,1,0:T(8,128)(2,1)}), bf16[8,32,256]{2,1,0:T(8,128)(2,1)S(1)}, u32[]{:S(2)}, u32[]{:S(2)}) async-start(bf16[8,32,256]{2,1,0:T(8,128)(2,1)} %project_out.1), calls=%async_computation.2 | async-start | bytes 262144 | tf_op jit(solution)/shard_map/all_to_all | solution.py:17
  127.1 0.1 copy.66
  127.2 0.8 copy.67
  128.0 0.6 fusion.2
  128.6 11.9 %all-to-all-done.2.parts = bf16[8,32,256]{2,1,0:T(8,128)(2,1)S(1)} async-done(((bf16[8,32,256]{2,1,0:T(8,128)(2,1)}), bf16[8,32,256]{2,1,0:T(8,128)(2,1)S(1)}, u32[]{:S(2)}, u32[]{:S(2)}) %all-to-all-start.2) | async-done | bytes 131104 | tf_op jit(solution)/shard_map/all_to_all | solution.py:17
  140.5 0.7 hidden_copies.1
  141.2 12.6 %all-to-all-start.3 = ((bf16[16,32,256]{2,1,0:T(8,128)(2,1)}), bf16[16,32,256]{2,1,0:T(8,128)(2,1)S(1)}, u32[]{:S(2)}, u32[]{:S(2)}) async-start(bf16[16,32,256]{2,1,0:T(8,128)(2,1)} %hidden_copies.1), calls=%async_computation.3 | async-start | bytes 524288 | tf_op jit(solution)/shard_map/all_to_all | solution.py:17
  153.8 1.1 compare_reduce_fusion
  154.9 0.2 convolution_convert_fusion.1
  155.1 2.0 select_reduce_fusion
  157.1 0.1 fusion
  157.3 0.3 select_reduce_fusion.1
  157.6 8.8 %all-to-all-done.3 = bf16[16,32,256]{2,1,0:T(8,128)(2,1)S(1)} async-done(((bf16[16,32,256]{2,1,0:T(8,128)(2,1)}), bf16[16,32,256]{2,1,0:T(8,128)(2,1)S(1)}, u32[]{:S(2)}, u32[]{:S(2)}) %all-to-all-start.3) | async-done | bytes 262176 | tf_op jit(solution)/shard_map/all_to_all | solution.py:17
  166.4 8.8 %collective-permute-start.6 = (bf16[16,32,256]{2,1,0:T(8,128)(2,1)S(1)}, bf16[16,32,256]{2,1,0:T(8,128)(2,1)}, u32[]{:S(2)}, u32[]{:S(2)}) collective-permute-start(bf16[16,32,256]{2,1,0:T(8,128)(2,1)S(1)} %all-to-all-done.3), channel_id=1, source_target_pairs={{0,8},{8,0},{1,9},{9,1},{2,10},{10,2},{3,11},{11,3},{4,12},{12,4},... | collective-permute-start | bytes 786440 | tf_op jit(solution)/shard_map/ppermute | solution.py:39
  175.2 0.1 copy.68
  175.3 0.8 sub.24.experts_at
  176.2 0.3 collective-permute-done.6
  176.5 0.9 copy-done.6
  177.4 1.4 select_rows.1
  178.8 0.9 copy-done.3
  179.7 4.4 %all-to-all-start.4 = ((bf16[8,192,256]{2,1,0:T(8,128)(2,1)}), bf16[8,192,256]{2,1,0:T(8,128)(2,1)}, u32[]{:S(2)}, u32[]{:S(2)}) async-start(bf16[8,192,256]{2,1,0:T(8,128)(2,1)} %copy-done.3), calls=%async_computation.4 | async-start | bytes 1572864 | tf_op jit(solution)/shard_map/all_to_all | solution.py:17
  184.1 23.5 %all-to-all-done.4.rows = bf16[8,192,256]{2,1,0:T(8,128)(2,1)} async-done(((bf16[8,192,256]{2,1,0:T(8,128)(2,1)}), bf16[8,192,256]{2,1,0:T(8,128)(2,1)}, u32[]{:S(2)}, u32[]{:S(2)}) %all-to-all-start.4) | async-done | bytes 786464 | tf_op jit(solution)/shard_map/all_to_all | solution.py:17
  207.6 2.7 %run_expert.1 = bf16[8,192,256]{2,1,0:T(8,128)(2,1)S(1)} custom-call(s32[1]{0:T(128)} %bitcast.21.keep, bf16[8,192,256]{2,1,0:T(8,128)(2,1)} %all-to-all-done.4.rows, bf16[2,2048,128]{2,1,0:T(8,128)(2,1)S(1)} %copy-done, bf16[2,2048,128]{2,1,0:T(8,128)(2,1)S(1)} %copy-done.1, bf16[3,2048,128]{2,1,0:T(8,128)(2,1)} %collective-permute-done.7.got, ...), custom_call_target="tpu_custom_call" | custom-call | flops 603979776 | bytes 4718592 | tf_op jit(solution)/shard_map/run_expert/pallas_call | solution.py:374
  210.3 25.5 %all_to_all.35 = bf16[8,192,256]{2,1,0:T(8,128)(2,1)S(1)} all-to-all(bf16[8,192,256]{2,1,0:T(8,128)(2,1)S(1)} %run_expert.1), channel_id=1, replica_groups=mesh['groups'=2,'chip'=16,'core'=2,'tensor'=8] {'tensor'}, dimensions={0} | all-to-all | bytes 1572864 | tf_op jit(solution)/shard_map/all_to_all | solution.py:17
  235.9 0.2 reduce.1
  236.0 0.9 copy.77
  236.9 6.8 %all-to-all-start.6 = ((bf16[32,2,6,256]{3,1,2,0:T(2,128)(2,1)}), bf16[32,2,6,256]{3,1,2,0:T(2,128)(2,1)S(1)}, u32[]{:S(2)}, u32[]{:S(2)}) async-start(bf16[32,2,6,256]{3,1,2,0:T(2,128)(2,1)} %bitcast.25), calls=%async_computation.6 | async-start | bytes 393216 | tf_op jit(solution)/shard_map/all_to_all | solution.py:17
  243.9 0.1 select_reduce_fusion.2
  244.1 0.1 fusion.4
  244.2 0.1 fusion.1
  244.5 17.7 %all-to-all-done.6 = bf16[32,2,6,256]{3,1,2,0:T(2,128)(2,1)S(1)} async-done(((bf16[32,2,6,256]{3,1,2,0:T(2,128)(2,1)}), bf16[32,2,6,256]{3,1,2,0:T(2,128)(2,1)S(1)}, u32[]{:S(2)}, u32[]{:S(2)}) %all-to-all-start.6) | async-done | bytes 196640 | tf_op jit(solution)/shard_map/all_to_all | solution.py:17
  262.3 0.3 fusion.20
  262.6 0.6 add_convert_fusion
  (56 shorter events, 1.2 us)
Async XLA Ops:
  0.0 83.6 %copy-start.8 = (bf16[512,64]{0,1:T(8,128)(2,1)S(1)}, bf16[512,64]{0,1:T(8,128)(2,1)}, u32[]{:S(2)}) copy-start(bf16[512,64]{0,1:T(8,128)(2,1)} %param.18) | copy-start | bytes 196612
  0.0 87.5 %copy-start.4 = (bf16[32,4096]{1,0:T(8,128)(2,1)S(1)}, bf16[32,4096]{1,0:T(8,128)(2,1)}, u32[]{:S(2)}) copy-start(bf16[32,4096]{1,0:T(8,128)(2,1)} %q.1) | copy-start | bytes 786436
  0.0 87.5 %copy-start.5 = (bf16[32,1024]{1,0:T(8,128)(2,1)S(1)}, bf16[32,1024]{1,0:T(8,128)(2,1)}, u32[]{:S(2)}) copy-start(bf16[32,1024]{1,0:T(8,128)(2,1)} %v.1) | copy-start | bytes 196612
  1.7 88.3 %all-to-all-start = ((bf16[8,32,256]{2,1,0:T(8,128)(2,1)}), bf16[8,32,256]{2,1,0:T(8,128)(2,1)}, u32[]{:S(2)}, u32[]{:S(2)}) async-start(bf16[8,32,256]{2,1,0:T(8,128)(2,1)} %bitcast.5), calls=%async_computation | async-start | bytes 262144 | tf_op jit(solution)/shard_map/all_to_all | solution.py:17
  9.6 46.7 %collective-permute-start = (bf16[64,512]{1,0:T(8,128)(2,1)}, bf16[64,512]{1,0:T(8,128)(2,1)S(1)}, u32[]{:S(2)}, u32[]{:S(2)}) collective-permute-start(bf16[64,512]{1,0:T(8,128)(2,1)} %bitcast.47), channel_id=1, source_target_pairs={{0,24},{8,240},{16,40},{24,0},{32,56},{40,16},{48,72},{56,32},{64,... | collective-permute-start | bytes 196616 | tf_op jit(solution)/shard_map/ppermute | solution.py:35
  56.2 0.6 copy-start.9
  56.9 38.9 %copy-start = (bf16[2,2048,128]{2,1,0:T(8,128)(2,1)S(1)}, bf16[2,2048,128]{2,1,0:T(8,128)(2,1)}, u32[]{:S(2)}) copy-start(bf16[2,2048,128]{2,1,0:T(8,128)(2,1)} %gate.3) | copy-start | bytes 3145732
  56.9 38.9 %copy-start.1 = (bf16[2,2048,128]{2,1,0:T(8,128)(2,1)S(1)}, bf16[2,2048,128]{2,1,0:T(8,128)(2,1)}, u32[]{:S(2)}) copy-start(bf16[2,2048,128]{2,1,0:T(8,128)(2,1)} %up.3) | copy-start | bytes 3145732
  56.9 38.9 %copy-start.2 = (bf16[2,128,2048]{2,1,0:T(8,128)(2,1)S(1)}, bf16[2,128,2048]{2,1,0:T(8,128)(2,1)}, u32[]{:S(2)}) copy-start(bf16[2,128,2048]{2,1,0:T(8,128)(2,1)} %down_hbm.1) | copy-start | bytes 3145732
  58.5 12.7 %collective-permute-start.1 = (bf16[2,64,512]{2,1,0:T(8,128)(2,1)}, bf16[2,64,512]{2,1,0:T(8,128)(2,1)}, u32[]{:S(2)}, u32[]{:S(2)}) collective-permute-start(bf16[2,64,512]{2,1,0:T(8,128)(2,1)} %pad_maximum_fusion.2), channel_id=1, source_target_pairs={{0,192},{8,72},{16,208},{24,88},{32,224},{40,104},{48,240},{56,120... | collective-permute-start | bytes 393224 | tf_op jit(solution)/shard_map/ppermute | solution.py:26
  72.9 10.8 %collective-permute-start.2 = (bf16[4,64,512]{2,1,0:T(8,128)(2,1)}, bf16[4,64,512]{2,1,0:T(8,128)(2,1)}, u32[]{:S(2)}, u32[]{:S(2)}) collective-permute-start(bf16[4,64,512]{2,1,0:T(8,128)(2,1)} %pad_maximum_fusion.1), channel_id=1, source_target_pairs={{0,224},{8,40},{16,240},{24,56},{32,0},{40,72},{48,16},{56,88},{64... | collective-permute-start | bytes 786440 | tf_op jit(solution)/shard_map/ppermute | solution.py:26
  85.5 19.6 %collective-permute-start.3 = (bf16[8,64,512]{2,1,0:T(8,128)(2,1)}, bf16[8,64,512]{2,1,0:T(8,128)(2,1)}, u32[]{:S(2)}, u32[]{:S(2)}) collective-permute-start(bf16[8,64,512]{2,1,0:T(8,128)(2,1)} %pad_maximum_fusion.mine_a), channel_id=1, source_target_pairs={{0,240},{8,24},{16,0},{24,40},{32,16},{40,56},{48,32},{56,72},{64,... | collective-permute-start | bytes 1572872 | tf_op jit(solution)/shard_map/ppermute | solution.py:26
  87.5 0.9 copy-start.7
  90.0 24.3 %all-to-all-start.1 = ((bf16[32,24,128]{2,1,0:T(8,128)(2,1)}), bf16[32,24,128]{2,1,0:T(8,128)(2,1)S(1)}, u32[]{:S(2)}, u32[]{:S(2)}) async-start(bf16[32,24,128]{2,1,0:T(8,128)(2,1)} %bitcast.6), calls=%async_computation.1 | async-start | bytes 393216 | tf_op jit(solution)/shard_map/all_to_all | solution.py:17
  97.1 87.1 %collective-permute-start.7 = (bf16[3,2048,128]{2,1,0:T(8,128)(2,1)}, bf16[3,2048,128]{2,1,0:T(8,128)(2,1)}, u32[]{:S(2)}, u32[]{:S(2)}) collective-permute-start(bf16[3,2048,128]{2,1,0:T(8,128)(2,1)} %give_weights.1), channel_id=1, source_target_pairs={{0,1},{1,0},{2,3},{3,2},{4,5},{5,4},{6,7},{7,6},{8,9},{9,8},{10,11... | collective-permute-start | bytes 4718600 | tf_op jit(solution)/shard_map/ppermute | solution.py:512
  101.8 15.2 %collective-permute-start.4 = (bf16[8,64,512]{2,1,0:T(8,128)(2,1)}, bf16[8,64,512]{2,1,0:T(8,128)(2,1)}, u32[]{:S(2)}, u32[]{:S(2)}) collective-permute-start(bf16[8,64,512]{2,1,0:T(8,128)(2,1)} %pad_maximum_fusion.mine_a), channel_id=1, source_target_pairs={{0,8},{8,0},{1,9},{9,1},{2,10},{10,2},{3,11},{11,3},{4,12},{12,4},... | collective-permute-start | bytes 1572872 | tf_op jit(solution)/shard_map/ppermute | solution.py:39
  105.1 11.9 %collective-permute-start.5 = (bf16[8,64,512]{2,1,0:T(8,128)(2,1)}, bf16[8,64,512]{2,1,0:T(8,128)(2,1)}, u32[]{:S(2)}, u32[]{:S(2)}) collective-permute-start(bf16[8,64,512]{2,1,0:T(8,128)(2,1)} %collective-permute-done.3.mine_b), channel_id=1, source_target_pairs={{0,8},{8,0},{1,9},{9,1},{2,10},{10,2},{3,11},{11,3},{4,12},{12,4},... | collective-permute-start | bytes 1572872 | tf_op jit(solution)/shard_map/ppermute | solution.py:39
  120.1 20.4 %all-to-all-start.2 = ((bf16[8,32,256]{2,1,0:T(8,128)(2,1)}), bf16[8,32,256]{2,1,0:T(8,128)(2,1)S(1)}, u32[]{:S(2)}, u32[]{:S(2)}) async-start(bf16[8,32,256]{2,1,0:T(8,128)(2,1)} %project_out.1), calls=%async_computation.2 | async-start | bytes 262144 | tf_op jit(solution)/shard_map/all_to_all | solution.py:17
  141.2 25.2 %all-to-all-start.3 = ((bf16[16,32,256]{2,1,0:T(8,128)(2,1)}), bf16[16,32,256]{2,1,0:T(8,128)(2,1)S(1)}, u32[]{:S(2)}, u32[]{:S(2)}) async-start(bf16[16,32,256]{2,1,0:T(8,128)(2,1)} %hidden_copies.1), calls=%async_computation.3 | async-start | bytes 524288 | tf_op jit(solution)/shard_map/all_to_all | solution.py:17
  166.4 10.1 %collective-permute-start.6 = (bf16[16,32,256]{2,1,0:T(8,128)(2,1)S(1)}, bf16[16,32,256]{2,1,0:T(8,128)(2,1)}, u32[]{:S(2)}, u32[]{:S(2)}) collective-permute-start(bf16[16,32,256]{2,1,0:T(8,128)(2,1)S(1)} %all-to-all-done.3), channel_id=1, source_target_pairs={{0,8},{8,0},{1,9},{9,1},{2,10},{10,2},{3,11},{11,3},{4,12},{12,4},... | collective-permute-start | bytes 786440 | tf_op jit(solution)/shard_map/ppermute | solution.py:39
  176.5 0.9 copy-start.6
  178.8 0.9 copy-start.3
  179.7 27.9 %all-to-all-start.4 = ((bf16[8,192,256]{2,1,0:T(8,128)(2,1)}), bf16[8,192,256]{2,1,0:T(8,128)(2,1)}, u32[]{:S(2)}, u32[]{:S(2)}) async-start(bf16[8,192,256]{2,1,0:T(8,128)(2,1)} %copy-done.3), calls=%async_computation.4 | async-start | bytes 1572864 | tf_op jit(solution)/shard_map/all_to_all | solution.py:17
  210.3 33.4 %copy-start.10 = (s32[32,8]{0,1:T(8,128)S(1)}, s32[32,8]{0,1:T(8,128)}, u32[]{:S(2)}) copy-start(s32[32,8]{0,1:T(8,128)} %param.19) | copy-start | bytes 3076
  210.3 33.4 %copy-start.11 = (f32[32,8]{0,1:T(8,128)S(1)}, f32[32,8]{0,1:T(8,128)}, u32[]{:S(2)}) copy-start(f32[32,8]{0,1:T(8,128)} %param.20) | copy-start | bytes 3076
  236.9 25.3 %all-to-all-start.6 = ((bf16[32,2,6,256]{3,1,2,0:T(2,128)(2,1)}), bf16[32,2,6,256]{3,1,2,0:T(2,128)(2,1)S(1)}, u32[]{:S(2)}, u32[]{:S(2)}) async-start(bf16[32,2,6,256]{3,1,2,0:T(2,128)(2,1)} %bitcast.25), calls=%async_computation.6 | async-start | bytes 393216 | tf_op jit(solution)/shard_map/all_to_all | solution.py:17

commit v6 on v5

--- a/solution.py
+++ b/solution.py
@@ -45,6 +45,10 @@
     return jnp.dot(marks.astype(bf16), before, preferred_element_type=f32).astype(i32)
 
 
+def in_hbm(*arrays):
+    return [pltpu.with_memory_space_constraint(x, pltpu.HBM) for x in arrays]
+
+
 def one_hot(at, shape, dim):
     return jnp.where(lax.broadcasted_iota(i32, shape, dim) == at, 1.0, 0.0).astype(bf16)
 
@@ -54,52 +58,116 @@
     return at.reshape(groups * size, lanes)
 
 
-def payload_kernel(places, target, q, k, v, resid, table, out):
-    chunks = [q[:, c : c + HD] for c in range(0, q.shape[1], HD)]
-    chunks += [k[...], v[...]]
-    chunks += [resid[:, c : c + HD] for c in range(0, resid.shape[1], HD)]
-    rows = jnp.concatenate([*chunks, table[...]], 0)
-    count, depth = out.shape[0], rows.shape[0]
-    groups = q.shape[0]
-    whole = lax.broadcasted_iota(i32, (count, depth), 0) == target[0:1, :]
-    local_row = grouped_iota(groups, count // groups, depth, 1) == target[1:2, :]
+def payload_kernel(at, prompts, routes, queries, own_kv, residual, out, q, kv, resid, sem):
+    tokens, q_cols = q.shape
+    col_width = resid.shape[1]
+
+    def cols(start, width):
+        return pl.ds(pl.multiple_of(start, HD), width)
+
+    copies = [
+        pltpu.make_async_copy(queries.at[:, cols(at[0] * q_cols, q_cols)], q, sem.at[0]),
+        pltpu.make_async_copy(own_kv.at[:, cols(at[1] * HD, HD)], kv.at[0], sem.at[1]),
+        pltpu.make_async_copy(own_kv.at[:, cols(at[2] * HD, HD)], kv.at[1], sem.at[2]),
+        pltpu.make_async_copy(
+            residual.at[:, cols(at[0] * col_width, col_width)], resid, sem.at[3]
+        ),
+    ]
+    for copy in copies:
+        copy.start()
+    count = out.shape[0]
+    size = count // tokens
+    chunks = (q_cols + 2 * HD + col_width) // HD
+    depth = chunks * tokens + HD
+    prompt = jnp.broadcast_to(prompts[...].astype(f32), (tokens, tokens))
+    sub = lax.broadcasted_iota(i32, (tokens, tokens), 0)
+    lane = lax.broadcasted_iota(i32, (tokens, tokens), 1)
+    alike = (prompt == prompt.T) & (sub < lane)
+    rank = jnp.sum(jnp.where(alike, 1.0, 0.0), 0, keepdims=True)
+    both = jnp.concatenate(
+        [jnp.broadcast_to(x, (8, tokens)) for x in (prompt[:1], rank)], 0
+    )
+    lanes = lax.broadcasted_iota(i32, (tokens, depth), 1)
+    repeat = jnp.where(
+        lax.rem(lanes, tokens) == lax.broadcasted_iota(i32, (tokens, depth), 0), 1.0, 0.0
+    )
+    spread = jnp.dot(both.astype(bf16), repeat.astype(bf16), preferred_element_type=f32)
+    lanes = lax.broadcasted_iota(i32, (1, depth), 1)
+    chunk = lax.div(lanes, tokens)
+    place = spread[:1].astype(i32) * size + spread[8:9].astype(i32) * chunks + chunk
+    place = jnp.where(chunk < chunks, place, -1)
+    spare = lanes - chunks * tokens
+    spare = jnp.where((spare >= 0) & (spare < size - 2 * chunks), 2 * chunks + spare, -1)
+    whole = lax.broadcasted_iota(i32, (count, depth), 0) == place
+    local_row = grouped_iota(tokens, size, depth, 1) == spare
     chosen = jnp.where(whole | local_row, 1.0, 0.0).astype(bf16)
+    picks = routes.shape[0]
+    at_lane = lax.broadcasted_iota(i32, (tokens, HD), 1)
+    at_sub = lax.broadcasted_iota(i32, (tokens, HD), 0)
+    first = jnp.where(at_lane == at_sub, 1.0, 0.0).astype(bf16)
+    second = jnp.where(at_lane == at_sub + tokens, 1.0, 0.0).astype(bf16)
+    table = jnp.dot(
+        routes[...].astype(f32).astype(bf16), first, preferred_element_type=f32
+    ) + jnp.dot(
+        jnp.broadcast_to(prompt[:1], (picks, tokens)).astype(bf16),
+        second,
+        preferred_element_type=f32,
+    )
+    table = jnp.concatenate([table, jnp.zeros((HD - picks, HD), f32)], 0).astype(bf16)
+    for copy in copies:
+        copy.wait()
+    rows = [q[:, c : c + HD] for c in range(0, q_cols, HD)]
+    rows += [kv[0], kv[1]]
+    rows += [resid[:, c : c + HD] for c in range(0, col_width, HD)]
+    rows = jnp.concatenate([*rows, table], 0)
     out[...] = jnp.dot(chosen, rows, preferred_element_type=f32).astype(bf16)
 
 
-def build_payload(places, target, queries, own_kv, residual, table, q_cols, col_width, count):
+def build_payload(at, prompts, routes, queries, own_kv, residual, q_cols, col_width, count):
+    vmem = pl.BlockSpec(memory_space=pltpu.VMEM)
+    hbm = pl.BlockSpec(memory_space=pltpu.HBM)
     tokens = queries.shape[0]
-
-    def cols(width, which):
-        return pl.BlockSpec((tokens, width), lambda i, at: (0, at[which]))
-
-    def whole(x):
-        return pl.BlockSpec(x.shape, lambda i, at: (0,) * x.ndim)
-
     return pl.pallas_call(
         payload_kernel,
         out_shape=jax.ShapeDtypeStruct((count, HD), bf16),
-        grid_spec=pltpu.PrefetchScalarGridSpec(
-            num_scalar_prefetch=1,
-            grid=(1,),
-            in_specs=[
-                whole(target),
-                cols(q_cols, 0),
-                cols(HD, 1),
-                cols(HD, 2),
-                cols(col_width, 0),
-                whole(table),
-            ],
-            out_specs=pl.BlockSpec((count, HD), lambda i, at: (0, 0)),
-        ),
-        cost_estimate=pl.CostEstimate(
-            flops=2 * count * target.shape[1] * HD,
-            bytes_accessed=4 * count * HD,
-            transcendentals=0,
-        ),
-        compiler_params=pltpu.CompilerParams(vmem_limit_bytes=8 << 20),
+        in_specs=[pl.BlockSpec(memory_space=pltpu.SMEM), vmem, vmem, hbm, hbm, hbm],
+        out_specs=vmem,
+        scratch_shapes=[
+            pltpu.VMEM((tokens, q_cols), bf16),
+            pltpu.VMEM((2, tokens, HD), bf16),
+            pltpu.VMEM((tokens, col_width), bf16),
+            pltpu.SemaphoreType.DMA((4,)),
+        ],
+        cost_estimate=pl.CostEstimate(
+            flops=2 * count * 384 * HD, bytes_accessed=4 * count * HD, transcendentals=0
+        ),
+        compiler_params=pltpu.CompilerParams(vmem_limit_bytes=6 << 20),
         name="build_payload",
-    )(places, target, queries, own_kv, own_kv, residual, table)
+    )(at, *in_hbm(prompts, routes, queries, own_kv, residual))
+
+
+def cache_kernel(cache, out):
+    copies, _, width = out.shape
+    heads = cache.shape[2] // width
+    for x in range(copies):
+        g = x * heads // copies
+        out[x, :, :HD] = cache[0, :, g * HD : (g + 1) * HD]
+        out[x, :, HD:] = cache[0, :, (heads + g) * HD : (heads + g + 1) * HD]
+
+
+def split_cache(cache, n_x):
+    vmem = pl.BlockSpec(memory_space=pltpu.VMEM)
+    return pl.pallas_call(
+        cache_kernel,
+        out_shape=jax.ShapeDtypeStruct((n_x, cache.shape[1], 2 * HD), bf16),
+        in_specs=[vmem],
+        out_specs=vmem,
+        cost_estimate=pl.CostEstimate(
+            flops=cache.size, bytes_accessed=6 * cache.size, transcendentals=0
+        ),
+        compiler_params=pltpu.CompilerParams(vmem_limit_bytes=2 << 20),
+        name="split_cache",
+    )(*in_hbm(cache))
 
 
 def attention_kernel(at, got, cache, attn, resid):
@@ -114,7 +182,9 @@
         (blocks, got.shape[0]),
         1,
     )
-    prompts = jnp.dot(table_row, rows, preferred_element_type=f32)[:, :tokens]
+    prompts = jnp.dot(table_row, rows, preferred_element_type=f32)
+    lane = lax.broadcasted_iota(i32, prompts.shape, 1)
+    prompts = jnp.where((lane >= tokens) & (lane < 2 * tokens), prompts, -1.0)
     holds = jnp.max(jnp.where(prompts == at[0].astype(f32), 1.0, 0.0), 1, keepdims=True)
     before = jnp.where(
         lax.broadcasted_iota(i32, (blocks, blocks), 1)
@@ -306,51 +376,64 @@
     )(at, attn, *halves)
 
 
-def give_kernel(give, gate, up, down, out):
-    out[0] = gate[0]
-    out[1] = up[0]
+def give_kernel(give, gate, up, down, out, mid, sem):
     ff = down.shape[1]
+    third = pltpu.make_async_copy(down.at[give[0]], mid, sem.at[0])
+    copies = [
+        pltpu.make_async_copy(gate.at[give[0]], out.at[0], sem.at[1]),
+        pltpu.make_async_copy(up.at[give[0]], out.at[1], sem.at[2]),
+    ]
+    third.start()
+    for copy in copies:
+        copy.start()
+    third.wait()
     for t in range(down.shape[2] // HD):
-        out[2, t * ff : (t + 1) * ff, :] = down[0, :, t * HD : (t + 1) * HD]
+        out[2, t * ff : (t + 1) * ff, :] = mid[:, t * HD : (t + 1) * HD]
+    for copy in copies:
+        copy.wait()
 
 
 def give_weights(give, gate, up, down):
-    def part(x):
-        return pl.BlockSpec((1, *x.shape[1:]), lambda i, k: (k[0], 0, 0))
-
-    shape = (3, *gate.shape[1:])
+    hbm = pl.BlockSpec(memory_space=pltpu.HBM)
     return pl.pallas_call(
         give_kernel,
-        out_shape=jax.ShapeDtypeStruct(shape, bf16),
-        grid_spec=pltpu.PrefetchScalarGridSpec(
-            num_scalar_prefetch=1,
-            grid=(1,),
-            in_specs=[part(gate), part(up), part(down)],
-            out_specs=pl.BlockSpec(shape, lambda i, k: (0, 0, 0)),
-        ),
+        out_shape=jax.ShapeDtypeStruct((3, *gate.shape[1:]), bf16),
+        in_specs=[pl.BlockSpec(memory_space=pltpu.SMEM), hbm, hbm, hbm],
+        out_specs=pl.BlockSpec(memory_space=pltpu.VMEM),
+        scratch_shapes=[
+            pltpu.VMEM(down.shape[1:], bf16),
+            pltpu.SemaphoreType.DMA((3,)),
+        ],
         cost_estimate=pl.CostEstimate(
             flops=gate.size, bytes_accessed=6 * gate.size, transcendentals=0
         ),
-        compiler_params=pltpu.CompilerParams(vmem_limit_bytes=12 << 20),
+        compiler_params=pltpu.CompilerParams(vmem_limit_bytes=6 << 20),
         name="give_weights",
-    )(jnp.reshape(give, (1,)).astype(i32), gate, up, down)
-
-
-def expert_kernel(keep, rows, gate, up, got, down_hbm, out, down, sem):
+    )(jnp.reshape(give, (1,)).astype(i32), *in_hbm(gate, up, down))
+
+
+def expert_kernel(keep, rows, got, gate_hbm, up_hbm, down_hbm, out, pair, down, sem):
     n_x, count, col_width = rows.shape
-    ff = gate.shape[2]
-    copy = pltpu.make_async_copy(down_hbm.at[keep[0]], down, sem)
-    copy.start()
+    ff = pair.shape[2]
+    copies = [
+        pltpu.make_async_copy(gate_hbm.at[keep[0]], pair.at[0], sem.at[0]),
+        pltpu.make_async_copy(up_hbm.at[keep[0]], pair.at[1], sem.at[1]),
+        pltpu.make_async_copy(down_hbm.at[keep[0]], down, sem.at[2]),
+    ]
+    for copy in copies:
+        copy.start()
+    copies[0].wait()
+    copies[1].wait()
     total = jnp.zeros((count, 4 * ff), f32)
     for s in range(n_x):
         at = pl.ds(s * col_width, col_width)
         weight = jnp.concatenate(
-            [gate[0, at, :], got[0, at, :], up[0, at, :], got[1, at, :]], 1
+            [pair[0, at, :], got[0, at, :], pair[1, at, :], got[1, at, :]], 1
         )
         total = total + jnp.dot(rows[s], weight, preferred_element_type=f32)
     gates, ups = total[:, : 2 * ff], total[:, 2 * ff :]
     act = (gates / (1.0 + jnp.exp(-gates)) * ups).astype(bf16)
-    copy.wait()
+    copies[2].wait()
     tiles = col_width // HD
     for d in range(n_x):
         theirs = [
@@ -363,39 +446,26 @@
 
 
 def run_expert(keep, rows, gate, up, down, got):
-    def whole(x):
-        return pl.BlockSpec(x.shape, lambda i, k: (0,) * x.ndim)
-
-    def kept(x):
-        return pl.BlockSpec((1, *x.shape[1:]), lambda i, k: (k[0], 0, 0))
-
+    vmem = pl.BlockSpec(memory_space=pltpu.VMEM)
+    hbm = pl.BlockSpec(memory_space=pltpu.HBM)
     flops = 2 * rows.size * gate.shape[2] * 6
     moved = 2 * (2 * rows.size + got.size) + 3 * gate.size
     return pl.pallas_call(
         expert_kernel,
         out_shape=jax.ShapeDtypeStruct(rows.shape, bf16),
-        grid_spec=pltpu.PrefetchScalarGridSpec(
-            num_scalar_prefetch=1,
-            grid=(1,),
-            in_specs=[
-                whole(rows),
-                kept(gate),
-                kept(up),
-                whole(got),
-                pl.BlockSpec(memory_space=pl.ANY),
-            ],
-            out_specs=whole(rows),
-            scratch_shapes=[
-                pltpu.VMEM(down.shape[1:], bf16),
-                pltpu.SemaphoreType.DMA,
-            ],
-        ),
+        in_specs=[pl.BlockSpec(memory_space=pltpu.SMEM), vmem, vmem, hbm, hbm, hbm],
+        out_specs=vmem,
+        scratch_shapes=[
+            pltpu.VMEM((2, *gate.shape[1:]), bf16),
+            pltpu.VMEM(down.shape[1:], bf16),
+            pltpu.SemaphoreType.DMA((3,)),
+        ],
         cost_estimate=pl.CostEstimate(
             flops=flops, bytes_accessed=moved, transcendentals=rows.shape[1] * 2 * HD
         ),
-        compiler_params=pltpu.CompilerParams(vmem_limit_bytes=16 << 20),
+        compiler_params=pltpu.CompilerParams(vmem_limit_bytes=12 << 20),
         name="run_expert",
-    )(jnp.reshape(keep, (1,)).astype(i32), rows, gate, up, got, down)
+    )(jnp.reshape(keep, (1,)).astype(i32), rows, got, *in_hbm(gate, up, down))
 
 
 def layer(
@@ -427,7 +497,6 @@
     heads_here = head_count // n_x
     q_cols = heads_here * HD
     per_prompt = tokens // (n_e // 2)
-    block_len = prompt_cache.shape[1]
     model_width = residual.shape[1]
     col_width = model_width // n_x
     picks = route_ids.shape[1]
@@ -435,9 +504,7 @@
     experts = experts_here * n_e
     capacity = min(tokens, 3 * tokens * picks // (2 * experts))
 
-    cache = prompt_cache[0].reshape(block_len, 2, kv_heads, HD)
-    by_head = jnp.transpose(cache, (2, 0, 1, 3)).reshape(kv_heads, block_len, 2 * HD)
-    by_head = jnp.repeat(by_head, n_x // kv_heads, axis=0)
+    by_head = split_cache(prompt_cache, n_x)
     cache_all = exchange(by_head, "tensor")
 
     w_own = out_weight.T
@@ -452,38 +519,25 @@
 
     kv_pos = (pos_x * heads_here) // group_size
     earlier = jnp.arange(tokens)[None, :] < jnp.arange(tokens)[:, None]
-    same = token_prompt[:, None] == token_prompt[None, :]
-    rank = jnp.sum((same & earlier).astype(i32), 1)
     chunks = (q_cols + 2 * HD + col_width) // HD
-    entries = jnp.concatenate(
-        [jnp.pad(token_prompt, (0, HD - tokens)), route_ids.reshape(-1)]
-    )
-    table_rows = -(-entries.shape[0] // (8 * HD)) * 8
-    table = jnp.pad(entries, (0, HD * HD - entries.shape[0])).astype(bf16).reshape(HD, HD)
-    size = 2 * chunks + table_rows
-    place = token_prompt * size + rank * chunks
-    token_rows = (place[None, :] + jnp.arange(chunks, dtype=i32)[:, None]).reshape(-1)
-    spare = jnp.arange(HD, dtype=i32)
-    target = jnp.stack(
-        [
-            jnp.pad(token_rows, (0, HD), constant_values=-1),
-            jnp.concatenate(
-                [
-                    jnp.full((tokens * chunks,), -1, i32),
-                    jnp.where(spare < table_rows, 2 * chunks + spare, -1),
-                ]
-            ),
-        ]
-    )
-    places = jnp.stack([pos_x, kv_pos, kv_heads + kv_pos]).astype(i32)
+    size = 2 * chunks + picks
+    at = jnp.stack([pos_x, kv_pos, kv_heads + kv_pos]).astype(i32)
     sent = build_payload(
-        places, target, queries, own_kv, residual, table, q_cols, col_width, n_e * size
+        at,
+        token_prompt.reshape(1, tokens),
+        route_ids.T,
+        queries,
+        own_kv,
+        residual,
+        q_cols,
+        col_width,
+        n_e * size,
     )
     sent, cache_all = lax.optimization_barrier((sent, cache_all))
     got = exchange(sent.reshape(n_e, size, HD), EXPERT)
-    table = got[:, 2 * chunks : 2 * chunks + 1 + tokens * picks // HD, :].astype(i32)
-    prompts = table[:, 0, :tokens]
-    routes = table[:, 1:, :].reshape(n_e, tokens, picks)
+    table = got[:, 2 * chunks :, :].astype(i32)
+    prompts = table[:, 0, tokens : 2 * tokens]
+    routes = table[:, :, :tokens]
 
     owner = jnp.arange(n_e, dtype=i32)
     holds = jnp.any(prompts[None, :, :] == owner[:, None, None], -1)
@@ -514,7 +568,7 @@
     near = exchange(hidden, "chip")
     across = other_core(near)
     mine_e = pos_e * experts_here + jnp.arange(experts_here, dtype=i32)
-    named = jnp.any(routes[None] == mine_e[:, None, None, None], -1)
+    named = jnp.any(routes[None] == mine_e[:, None, None, None], 2)
     slot = jnp.where(named, count_earlier(named), -1)
     filled = slot[:, :, None, :] == jnp.arange(capacity, dtype=i32)[None, None, :, None]
     expert_rows = jnp.sum(jnp.where(filled, source[None, :, None, :] + 1, 0), -1) - 1

time: 265 us -> 252 us (0.951)
  other arithmetic: 15.2 us -> 6.49 us
  local copies, waits for them, and re-layouts: 8.52 us -> 1.79 us
  waiting for transfers between devices: 86.5 us -> 90.9 us
  starting transfers between devices: 112 us -> 108 us
    all_to_all x6, waiting for transfers between devices: 68.4 us -> 77.4 us  [exchange(): return lax.all_to_all(tiles, axis, split_axis=0, concat_axis=0, tiled=True)]
    ppermute x3, waiting for transfers between devices: 17.8 us -> 10.5 us  [along_chips(): return lax.ppermute(x, EXPERT, moves)]
    unnamed x27 -> x7, local copies, waits for them, and re-layouts: 4.41 us -> 1.03 us
    all_to_all x6, starting transfers between devices: 44.3 us -> 41 us  [exchange(): return lax.all_to_all(tiles, axis, split_axis=0, concat_axis=0, tiled=True)]
  transfers between devices with their start and end apart: 14 -> 14, of which waited for: 8 -> 10; matrix products, arithmetic and copies ran while one was open for 7% -> 2% of each run, Pallas kernels for 4% -> 5%
where the time goes in v6:
time: 252 us; the launch traced here: 250 us
  starting transfers between devices  108 us (43%)
  waiting for transfers between devices  90.9 us (36%)
  blocking collectives  25.5 us (10%)
  Pallas kernels  16 us (6%)
  other arithmetic  6.49 us (3%)
    all_to_all x6, waiting for transfers between devices, exchange(): return lax.all_to_all(tiles, axis, split_axis=0, concat_axis=0, tiled=True)  77.4 us
    ppermute x1, starting transfers between devices, across_chips(): return lax.ppermute(x, EXPERT, moves)  45 us
    all_to_all x6, starting transfers between devices, exchange(): return lax.all_to_all(tiles, axis, split_axis=0, concat_axis=0, tiled=True)  41 us
    all_to_all x1, blocking collectives, exchange(): return lax.all_to_all(tiles, axis, split_axis=0, concat_axis=0, tiled=True)  25.5 us
    ppermute x3, starting transfers between devices, other_core(): return lax.ppermute(x, 'core', [(0, 1), (1, 0)])  13.7 us
    ppermute x3, waiting for transfers between devices, along_chips(): return lax.ppermute(x, EXPERT, moves)  10.5 us
    ppermute x3, starting transfers between devices, along_chips(): return lax.ppermute(x, EXPERT, moves)  5.85 us
  transfers between devices with their start and end apart: 14, of which 10 were waited for; matrix products, arithmetic and copies ran while one was open for 2% of the time, Pallas kernels for 5%

profile of v6, /device:TPU:65, one launch (start us, length us, event | category | flops | bytes accessed | tf_op | source)
XLA Modules:
  0.0 250.3 jit_solution(14810063343568555984)
XLA Ops:
  0.0 45.0 %collective-permute-start = (bf16[64,512]{1,0:T(8,128)(2,1)}, bf16[64,512]{1,0:T(8,128)(2,1)S(1)}, u32[]{:S(2)}, u32[]{:S(2)}) collective-permute-start(bf16[64,512]{1,0:T(8,128)(2,1)} %bitcast.45), channel_id=1, source_target_pairs={{0,24},{8,240},{16,40},{24,0},{32,56},{40,16},{48,72},{56,32},{64,... | collective-permute-start | bytes 196616 | tf_op jit(solution)/shard_map/ppermute | solution.py:35
  45.1 2.1 collective-permute-done
  47.2 0.9 pad_maximum_fusion.2
  48.1 2.0 collective-permute-start.1
  50.0 10.4 %collective-permute-done.1 = bf16[2,64,512]{2,1,0:T(8,128)(2,1)S(1)} collective-permute-done((bf16[2,64,512]{2,1,0:T(8,128)(2,1)S(1)}, bf16[2,64,512]{2,1,0:T(8,128)(2,1)S(1)}, u32[]{:S(2)}, u32[]{:S(2)}) %collective-permute-start.1) | collective-permute-done | bytes 131104 | tf_op jit(solution)/shard_map/ppermute | solution.py:26
  60.4 0.9 pad_maximum_fusion.1
  61.3 2.0 collective-permute-start.2
  63.2 1.5 split_cache.1
  64.7 6.9 %all-to-all-start = ((bf16[8,32,256]{2,1,0:T(8,128)(2,1)}), bf16[8,32,256]{2,1,0:T(8,128)(2,1)S(1)}, u32[]{:S(2)}, u32[]{:S(2)}) async-start(bf16[8,32,256]{2,1,0:T(8,128)(2,1)} %split_cache.1), calls=%async_computation | async-start | bytes 262144 | tf_op jit(solution)/shard_map/all_to_all | solution.py:17
  71.7 0.2 collective-permute-done.2
  71.8 0.9 pad_maximum_fusion.mine_a
  72.7 2.0 collective-permute-start.3
  74.7 0.1 pad_add_fusion.at
  74.8 2.5 %build_payload.1 = bf16[768,128]{1,0:T(8,128)(2,1)} custom-call(s32[3]{0:T(128)S(1)} %pad_add_fusion.at, s32[1,32]{1,0:T(1,128)} %bitcast.53, s32[8,32]{1,0:T(8,128)} %bitcast.52, bf16[32,4096]{1,0:T(8,128)(2,1)} %queries.1, bf16[32,1024]{1,0:T(8,128)(2,1)} %own_kv.1, bf16[32,2048]{1,0:T(8,128)(2,1)} %residual.1), custom_call_target="tpu_custom_call" | custom-call | flops 75497472 | bytes 393216 | tf_op jit(solution)/shard_map/build_payload/pallas_call | solution.py:130
  77.3 2.8 %all-to-all-done.cache = bf16[8,32,256]{2,1,0:T(8,128)(2,1)S(1)} async-done(((bf16[8,32,256]{2,1,0:T(8,128)(2,1)}), bf16[8,32,256]{2,1,0:T(8,128)(2,1)S(1)}, u32[]{:S(2)}, u32[]{:S(2)}) %all-to-all-start) | async-done | bytes 131104 | tf_op jit(solution)/shard_map/all_to_all | solution.py:17
  80.1 7.2 %all-to-all-start.1 = ((bf16[32,24,128]{2,1,0:T(8,128)(2,1)}), bf16[32,24,128]{2,1,0:T(8,128)(2,1)S(1)}, u32[]{:S(2)}, u32[]{:S(2)}) async-start(bf16[32,24,128]{2,1,0:T(8,128)(2,1)} %bitcast.5), calls=%async_computation.1 | async-start | bytes 393216 | tf_op jit(solution)/shard_map/all_to_all | solution.py:17
  87.4 1.4 give_weights.1
  88.8 2.2 collective-permute-start.7
  91.6 2.9 %collective-permute-start.4 = (bf16[8,64,512]{2,1,0:T(8,128)(2,1)S(1)}, bf16[8,64,512]{2,1,0:T(8,128)(2,1)S(1)}, u32[]{:S(2)}, u32[]{:S(2)}) collective-permute-start(bf16[8,64,512]{2,1,0:T(8,128)(2,1)S(1)} %pad_maximum_fusion.mine_a), channel_id=1, source_target_pairs={{0,8},{8,0},{1,9},{9,1},{2,10},{10,2},{3,11},{11,3},{4,12},{12,4},... | collective-permute-start | bytes 1572872 | tf_op jit(solution)/shard_map/ppermute | solution.py:39
  94.6 2.0 collective-permute-start.5
  96.5 0.1 pad_add_fusion.2.at
  96.6 0.1 pad_add_fusion.1.at
  96.7 9.1 %all-to-all-done.1 = bf16[32,24,128]{2,1,0:T(8,128)(2,1)S(1)} async-done(((bf16[32,24,128]{2,1,0:T(8,128)(2,1)}), bf16[32,24,128]{2,1,0:T(8,128)(2,1)S(1)}, u32[]{:S(2)}, u32[]{:S(2)}) %all-to-all-start.1) | async-done | bytes 196640 | tf_op jit(solution)/shard_map/all_to_all | solution.py:17
  105.9 2.2 attend.1
  108.2 2.6 %project_out.1 = bf16[8,32,256]{2,1,0:T(8,128)(2,1)} custom-call(s32[2]{0:T(128)S(1)} %pad_add_fusion.1.at, bf16[32,512]{1,0:T(8,128)(2,1)S(1)} %get-tuple-element.13.attn, bf16[8,64,512]{2,1,0:T(8,128)(2,1)S(1)} %pad_maximum_fusion.mine_a, bf16[8,64,512]{2,1,0:T(8,128)(2,1)S(1)} %collective-permute-done.3.mine_b, ...), custom_call_target="tpu_custom_call" | custom-call | flops 67108864 | bytes 2097152 | tf_op jit(solution)/shard_map/project_out/pallas_call | solution.py:366
  110.8 3.9 %all-to-all-start.2 = ((bf16[8,32,256]{2,1,0:T(8,128)(2,1)}), bf16[8,32,256]{2,1,0:T(8,128)(2,1)S(1)}, u32[]{:S(2)}, u32[]{:S(2)}) async-start(bf16[8,32,256]{2,1,0:T(8,128)(2,1)} %project_out.1), calls=%async_computation.2 | async-start | bytes 262144 | tf_op jit(solution)/shard_map/all_to_all | solution.py:17
  114.7 0.1 slice_bitcast_fusion
  114.7 0.1 copy.36
  114.8 0.6 fusion.2
  115.5 13.9 %all-to-all-done.2.parts = bf16[8,32,256]{2,1,0:T(8,128)(2,1)S(1)} async-done(((bf16[8,32,256]{2,1,0:T(8,128)(2,1)}), bf16[8,32,256]{2,1,0:T(8,128)(2,1)S(1)}, u32[]{:S(2)}, u32[]{:S(2)}) %all-to-all-start.2) | async-done | bytes 131104 | tf_op jit(solution)/shard_map/all_to_all | solution.py:17
  129.3 0.7 hidden_copies.1
  130.1 12.0 %all-to-all-start.3 = ((bf16[16,32,256]{2,1,0:T(8,128)(2,1)}), bf16[16,32,256]{2,1,0:T(8,128)(2,1)S(1)}, u32[]{:S(2)}, u32[]{:S(2)}) async-start(bf16[16,32,256]{2,1,0:T(8,128)(2,1)} %hidden_copies.1), calls=%async_computation.3 | async-start | bytes 524288 | tf_op jit(solution)/shard_map/all_to_all | solution.py:17
  142.1 0.2 compare_reduce_fusion
  142.2 0.2 convolution_convert_fusion.1
  142.4 1.3 select_reduce_fusion
  143.7 0.1 fusion
  143.9 0.1 broadcast_add_fusion
  144.0 0.3 select_reduce_fusion.1
  144.3 10.3 %all-to-all-done.3 = bf16[16,32,256]{2,1,0:T(8,128)(2,1)S(1)} async-done(((bf16[16,32,256]{2,1,0:T(8,128)(2,1)}), bf16[16,32,256]{2,1,0:T(8,128)(2,1)S(1)}, u32[]{:S(2)}, u32[]{:S(2)}) %all-to-all-start.3) | async-done | bytes 262176 | tf_op jit(solution)/shard_map/all_to_all | solution.py:17
  154.6 8.9 %collective-permute-start.6 = (bf16[16,32,256]{2,1,0:T(8,128)(2,1)S(1)}, bf16[16,32,256]{2,1,0:T(8,128)(2,1)S(1)}, u32[]{:S(2)}, u32[]{:S(2)}) collective-permute-start(bf16[16,32,256]{2,1,0:T(8,128)(2,1)S(1)} %all-to-all-done.3), channel_id=1, source_target_pairs={{0,8},{8,0},{1,9},{9,1},{2,10},{10,2},{3,11},{11,3},{4,12},{12,4},... | collective-permute-start | bytes 786440 | tf_op jit(solution)/shard_map/ppermute | solution.py:39
  163.5 0.1 copy.37
  163.6 0.1 sub.24.experts_at
  163.7 0.1 copy.39.home_at
  163.8 0.8 collective-permute-done.6
  164.6 1.4 select_rows.1
  166.0 4.2 %all-to-all-start.4 = ((bf16[8,192,256]{2,1,0:T(8,128)(2,1)}), bf16[8,192,256]{2,1,0:T(8,128)(2,1)S(1)}, u32[]{:S(2)}, u32[]{:S(2)}) async-start(bf16[8,192,256]{2,1,0:T(8,128)(2,1)} %get-tuple-element.16), calls=%async_computation.4 | async-start | bytes 1572864 | tf_op jit(solution)/shard_map/all_to_all | solution.py:17
  170.2 23.6 %all-to-all-done.4.rows = bf16[8,192,256]{2,1,0:T(8,128)(2,1)S(1)} async-done(((bf16[8,192,256]{2,1,0:T(8,128)(2,1)}), bf16[8,192,256]{2,1,0:T(8,128)(2,1)S(1)}, u32[]{:S(2)}, u32[]{:S(2)}) %all-to-all-start.4) | async-done | bytes 786464 | tf_op jit(solution)/shard_map/all_to_all | solution.py:17
  193.8 3.6 %run_expert.1 = bf16[8,192,256]{2,1,0:T(8,128)(2,1)S(1)} custom-call(s32[1]{0:T(128)} %bitcast.19.keep, bf16[8,192,256]{2,1,0:T(8,128)(2,1)S(1)} %all-to-all-done.4.rows, bf16[3,2048,128]{2,1,0:T(8,128)(2,1)} %collective-permute-done.7.got, bf16[2,2048,128]{2,1,0:T(8,128)(2,1)} %gate_hbm.1, bf16[2,2048,128]{2,1,0:T(8,128)(2,1)} %up_hbm.1, ...), custom_call_target="tpu_custom_call" | custom-call | flops 603979776 | bytes 4718592 | tf_op jit(solution)/shard_map/run_expert/pallas_call | solution.py:453
  197.4 0.0 copy-start
  197.4 25.5 %all_to_all.35 = bf16[8,192,256]{2,1,0:T(8,128)(2,1)S(1)} all-to-all(bf16[8,192,256]{2,1,0:T(8,128)(2,1)S(1)} %run_expert.1), channel_id=1, replica_groups=mesh['groups'=2,'chip'=16,'core'=2,'tensor'=8] {'tensor'}, dimensions={0} | all-to-all | bytes 1572864 | tf_op jit(solution)/shard_map/all_to_all | solution.py:17
  222.9 0.2 reduce.1
  223.1 0.9 copy.46
  224.0 6.8 %all-to-all-start.6 = ((bf16[32,2,6,256]{3,1,2,0:T(2,128)(2,1)}), bf16[32,2,6,256]{3,1,2,0:T(2,128)(2,1)S(1)}, u32[]{:S(2)}, u32[]{:S(2)}) async-start(bf16[32,2,6,256]{3,1,2,0:T(2,128)(2,1)} %bitcast.23), calls=%async_computation.6 | async-start | bytes 393216 | tf_op jit(solution)/shard_map/all_to_all | solution.py:17
  230.7 0.1 copy.40
  230.8 0.1 copy.42
  230.9 0.1 select_reduce_fusion.2
  231.1 0.1 copy.43
  231.1 0.1 fusion.4
  231.3 0.1 fusion.1
  231.4 0.1 copy.41
  231.6 17.7 %all-to-all-done.6 = bf16[32,2,6,256]{3,1,2,0:T(2,128)(2,1)S(1)} async-done(((bf16[32,2,6,256]{3,1,2,0:T(2,128)(2,1)}), bf16[32,2,6,256]{3,1,2,0:T(2,128)(2,1)S(1)}, u32[]{:S(2)}, u32[]{:S(2)}) %all-to-all-start.6) | async-done | bytes 196640 | tf_op jit(solution)/shard_map/all_to_all | solution.py:17
  249.3 0.1 reshape.176
  249.4 0.3 fusion.17
  249.7 0.6 add_convert_fusion
  (16 shorter events, 0.2 us)
Async XLA Ops:
  0.0 47.2 %collective-permute-start = (bf16[64,512]{1,0:T(8,128)(2,1)}, bf16[64,512]{1,0:T(8,128)(2,1)S(1)}, u32[]{:S(2)}, u32[]{:S(2)}) collective-permute-start(bf16[64,512]{1,0:T(8,128)(2,1)} %bitcast.45), channel_id=1, source_target_pairs={{0,24},{8,240},{16,40},{24,0},{32,56},{40,16},{48,72},{56,32},{64,... | collective-permute-start | bytes 196616 | tf_op jit(solution)/shard_map/ppermute | solution.py:35
  48.1 12.3 %collective-permute-start.1 = (bf16[2,64,512]{2,1,0:T(8,128)(2,1)S(1)}, bf16[2,64,512]{2,1,0:T(8,128)(2,1)S(1)}, u32[]{:S(2)}, u32[]{:S(2)}) collective-permute-start(bf16[2,64,512]{2,1,0:T(8,128)(2,1)S(1)} %pad_maximum_fusion.2), channel_id=1, source_target_pairs={{0,192},{8,72},{16,208},{24,88},{32,224},{40,104},{48,240},{56,120... | collective-permute-start | bytes 393224 | tf_op jit(solution)/shard_map/ppermute | solution.py:26
  61.3 10.6 %collective-permute-start.2 = (bf16[4,64,512]{2,1,0:T(8,128)(2,1)S(1)}, bf16[4,64,512]{2,1,0:T(8,128)(2,1)S(1)}, u32[]{:S(2)}, u32[]{:S(2)}) collective-permute-start(bf16[4,64,512]{2,1,0:T(8,128)(2,1)S(1)} %pad_maximum_fusion.1), channel_id=1, source_target_pairs={{0,224},{8,40},{16,240},{24,56},{32,0},{40,72},{48,16},{56,88},{64... | collective-permute-start | bytes 786440 | tf_op jit(solution)/shard_map/ppermute | solution.py:26
  64.7 15.4 %all-to-all-start = ((bf16[8,32,256]{2,1,0:T(8,128)(2,1)}), bf16[8,32,256]{2,1,0:T(8,128)(2,1)S(1)}, u32[]{:S(2)}, u32[]{:S(2)}) async-start(bf16[8,32,256]{2,1,0:T(8,128)(2,1)} %split_cache.1), calls=%async_computation | async-start | bytes 262144 | tf_op jit(solution)/shard_map/all_to_all | solution.py:17
  72.7 21.9 %collective-permute-start.3 = (bf16[8,64,512]{2,1,0:T(8,128)(2,1)S(1)}, bf16[8,64,512]{2,1,0:T(8,128)(2,1)S(1)}, u32[]{:S(2)}, u32[]{:S(2)}) collective-permute-start(bf16[8,64,512]{2,1,0:T(8,128)(2,1)S(1)} %pad_maximum_fusion.mine_a), channel_id=1, source_target_pairs={{0,240},{8,24},{16,0},{24,40},{32,16},{40,56},{48,32},{56,72},{64,... | collective-permute-start | bytes 1572872 | tf_op jit(solution)/shard_map/ppermute | solution.py:26
  80.1 25.7 %all-to-all-start.1 = ((bf16[32,24,128]{2,1,0:T(8,128)(2,1)}), bf16[32,24,128]{2,1,0:T(8,128)(2,1)S(1)}, u32[]{:S(2)}, u32[]{:S(2)}) async-start(bf16[32,24,128]{2,1,0:T(8,128)(2,1)} %bitcast.5), calls=%async_computation.1 | async-start | bytes 393216 | tf_op jit(solution)/shard_map/all_to_all | solution.py:17
  88.8 81.4 %collective-permute-start.7 = (bf16[3,2048,128]{2,1,0:T(8,128)(2,1)S(1)}, bf16[3,2048,128]{2,1,0:T(8,128)(2,1)}, u32[]{:S(2)}, u32[]{:S(2)}) collective-permute-start(bf16[3,2048,128]{2,1,0:T(8,128)(2,1)S(1)} %give_weights.1), channel_id=1, source_target_pairs={{0,1},{1,0},{2,3},{3,2},{4,5},{5,4},{6,7},{7,6},{8,9},{9,8},{10,11... | collective-permute-start | bytes 4718600 | tf_op jit(solution)/shard_map/ppermute | solution.py:566
  91.6 16.5 %collective-permute-start.4 = (bf16[8,64,512]{2,1,0:T(8,128)(2,1)S(1)}, bf16[8,64,512]{2,1,0:T(8,128)(2,1)S(1)}, u32[]{:S(2)}, u32[]{:S(2)}) collective-permute-start(bf16[8,64,512]{2,1,0:T(8,128)(2,1)S(1)} %pad_maximum_fusion.mine_a), channel_id=1, source_target_pairs={{0,8},{8,0},{1,9},{9,1},{2,10},{10,2},{3,11},{11,3},{4,12},{12,4},... | collective-permute-start | bytes 1572872 | tf_op jit(solution)/shard_map/ppermute | solution.py:39
  94.6 13.6 %collective-permute-start.5 = (bf16[8,64,512]{2,1,0:T(8,128)(2,1)S(1)}, bf16[8,64,512]{2,1,0:T(8,128)(2,1)}, u32[]{:S(2)}, u32[]{:S(2)}) collective-permute-start(bf16[8,64,512]{2,1,0:T(8,128)(2,1)S(1)} %collective-permute-done.3.mine_b), channel_id=1, source_target_pairs={{0,8},{8,0},{1,9},{9,1},{2,10},{10,2},{3,11},{11,3},{4,12},{12,4},... | collective-permute-start | bytes 1572872 | tf_op jit(solution)/shard_map/ppermute | solution.py:39
  110.8 18.6 %all-to-all-start.2 = ((bf16[8,32,256]{2,1,0:T(8,128)(2,1)}), bf16[8,32,256]{2,1,0:T(8,128)(2,1)S(1)}, u32[]{:S(2)}, u32[]{:S(2)}) async-start(bf16[8,32,256]{2,1,0:T(8,128)(2,1)} %project_out.1), calls=%async_computation.2 | async-start | bytes 262144 | tf_op jit(solution)/shard_map/all_to_all | solution.py:17
  130.1 24.5 %all-to-all-start.3 = ((bf16[16,32,256]{2,1,0:T(8,128)(2,1)}), bf16[16,32,256]{2,1,0:T(8,128)(2,1)S(1)}, u32[]{:S(2)}, u32[]{:S(2)}) async-start(bf16[16,32,256]{2,1,0:T(8,128)(2,1)} %hidden_copies.1), calls=%async_computation.3 | async-start | bytes 524288 | tf_op jit(solution)/shard_map/all_to_all | solution.py:17
  154.6 10.0 %collective-permute-start.6 = (bf16[16,32,256]{2,1,0:T(8,128)(2,1)S(1)}, bf16[16,32,256]{2,1,0:T(8,128)(2,1)S(1)}, u32[]{:S(2)}, u32[]{:S(2)}) collective-permute-start(bf16[16,32,256]{2,1,0:T(8,128)(2,1)S(1)} %all-to-all-done.3), channel_id=1, source_target_pairs={{0,8},{8,0},{1,9},{9,1},{2,10},{10,2},{3,11},{11,3},{4,12},{12,4},... | collective-permute-start | bytes 786440 | tf_op jit(solution)/shard_map/ppermute | solution.py:39
  166.0 27.8 %all-to-all-start.4 = ((bf16[8,192,256]{2,1,0:T(8,128)(2,1)}), bf16[8,192,256]{2,1,0:T(8,128)(2,1)S(1)}, u32[]{:S(2)}, u32[]{:S(2)}) async-start(bf16[8,192,256]{2,1,0:T(8,128)(2,1)} %get-tuple-element.16), calls=%async_computation.4 | async-start | bytes 1572864 | tf_op jit(solution)/shard_map/all_to_all | solution.py:17
  197.4 33.4 %copy-start = (s32[32,8]{0,1:T(8,128)S(1)}, s32[32,8]{0,1:T(8,128)}, u32[]{:S(2)}) copy-start(s32[32,8]{0,1:T(8,128)} %param.19) | copy-start | bytes 3076
  197.4 33.4 %copy-start.1 = (f32[32,8]{0,1:T(8,128)S(1)}, f32[32,8]{0,1:T(8,128)}, u32[]{:S(2)}) copy-start(f32[32,8]{0,1:T(8,128)} %param.20) | copy-start | bytes 3076
  224.0 25.3 %all-to-all-start.6 = ((bf16[32,2,6,256]{3,1,2,0:T(2,128)(2,1)}), bf16[32,2,6,256]{3,1,2,0:T(2,128)(2,1)S(1)}, u32[]{:S(2)}, u32[]{:S(2)}) async-start(bf16[32,2,6,256]{3,1,2,0:T(2,128)(2,1)} %bitcast.23), calls=%async_computation.6 | async-start | bytes 393216 | tf_op jit(solution)/shard_map/all_to_all | solution.py:17

commit v7 on v6

--- a/solution.py
+++ b/solution.py
@@ -26,12 +26,12 @@
     return lax.ppermute(x, EXPERT, moves)
 
 
-def across_chips(x):
+def across_chips(x, shift):
     n = lax.axis_size("chip")
     moves = []
     for c in range(n):
-        moves.append((c * CORES, (c + 1) % n * CORES + 1))
-        moves.append((c * CORES + 1, (c - 1) % n * CORES))
+        moves.append((c * CORES, (c + shift) % n * CORES + 1))
+        moves.append((c * CORES + 1, (c - shift) % n * CORES))
     return lax.ppermute(x, EXPERT, moves)
 
 
@@ -376,96 +376,87 @@
     )(at, attn, *halves)
 
 
-def give_kernel(give, gate, up, down, out, mid, sem):
+def part_kernel(which, gate, up, down, give, keep, mid, sem):
     ff = down.shape[1]
-    third = pltpu.make_async_copy(down.at[give[0]], mid, sem.at[0])
-    copies = [
-        pltpu.make_async_copy(gate.at[give[0]], out.at[0], sem.at[1]),
-        pltpu.make_async_copy(up.at[give[0]], out.at[1], sem.at[2]),
-    ]
-    third.start()
+    copies = []
+    for k, out in enumerate((give, keep)):
+        copies += [
+            pltpu.make_async_copy(down.at[which[k]], mid.at[k], sem.at[3 * k]),
+            pltpu.make_async_copy(gate.at[which[k]], out.at[0], sem.at[3 * k + 1]),
+            pltpu.make_async_copy(up.at[which[k]], out.at[1], sem.at[3 * k + 2]),
+        ]
     for copy in copies:
         copy.start()
-    third.wait()
-    for t in range(down.shape[2] // HD):
-        out[2, t * ff : (t + 1) * ff, :] = mid[:, t * HD : (t + 1) * HD]
-    for copy in copies:
-        copy.wait()
-
-
-def give_weights(give, gate, up, down):
+    for k, out in enumerate((give, keep)):
+        copies[3 * k].wait()
+        for t in range(down.shape[2] // HD):
+            out[2, t * ff : (t + 1) * ff, :] = mid[k, :, t * HD : (t + 1) * HD]
+    for k in (0, 1):
+        copies[3 * k + 1].wait()
+        copies[3 * k + 2].wait()
+
+
+def part_weights(which, gate, up, down):
     hbm = pl.BlockSpec(memory_space=pltpu.HBM)
-    return pl.pallas_call(
-        give_kernel,
-        out_shape=jax.ShapeDtypeStruct((3, *gate.shape[1:]), bf16),
+    vmem = pl.BlockSpec(memory_space=pltpu.VMEM)
+    half = jax.ShapeDtypeStruct((3, *gate.shape[1:]), bf16)
+    return pl.pallas_call(
+        part_kernel,
+        out_shape=(half, half),
         in_specs=[pl.BlockSpec(memory_space=pltpu.SMEM), hbm, hbm, hbm],
-        out_specs=pl.BlockSpec(memory_space=pltpu.VMEM),
+        out_specs=(vmem, vmem),
         scratch_shapes=[
-            pltpu.VMEM(down.shape[1:], bf16),
-            pltpu.SemaphoreType.DMA((3,)),
+            pltpu.VMEM((2, *down.shape[1:]), bf16),
+            pltpu.SemaphoreType.DMA((6,)),
         ],
         cost_estimate=pl.CostEstimate(
-            flops=gate.size, bytes_accessed=6 * gate.size, transcendentals=0
-        ),
-        compiler_params=pltpu.CompilerParams(vmem_limit_bytes=6 << 20),
-        name="give_weights",
-    )(jnp.reshape(give, (1,)).astype(i32), *in_hbm(gate, up, down))
-
-
-def expert_kernel(keep, rows, got, gate_hbm, up_hbm, down_hbm, out, pair, down, sem):
+            flops=gate.size, bytes_accessed=12 * gate.size, transcendentals=0
+        ),
+        compiler_params=pltpu.CompilerParams(vmem_limit_bytes=8 << 20),
+        name="part_weights",
+    )(which, *in_hbm(gate, up, down))
+
+
+def expert_kernel(rows, kept, got, out):
     n_x, count, col_width = rows.shape
-    ff = pair.shape[2]
-    copies = [
-        pltpu.make_async_copy(gate_hbm.at[keep[0]], pair.at[0], sem.at[0]),
-        pltpu.make_async_copy(up_hbm.at[keep[0]], pair.at[1], sem.at[1]),
-        pltpu.make_async_copy(down_hbm.at[keep[0]], down, sem.at[2]),
-    ]
-    for copy in copies:
-        copy.start()
-    copies[0].wait()
-    copies[1].wait()
+    ff = kept.shape[2]
     total = jnp.zeros((count, 4 * ff), f32)
     for s in range(n_x):
         at = pl.ds(s * col_width, col_width)
         weight = jnp.concatenate(
-            [pair[0, at, :], got[0, at, :], pair[1, at, :], got[1, at, :]], 1
+            [kept[0, at, :], got[0, at, :], kept[1, at, :], got[1, at, :]], 1
         )
         total = total + jnp.dot(rows[s], weight, preferred_element_type=f32)
     gates, ups = total[:, : 2 * ff], total[:, 2 * ff :]
     act = (gates / (1.0 + jnp.exp(-gates)) * ups).astype(bf16)
-    copies[2].wait()
     tiles = col_width // HD
     for d in range(n_x):
-        theirs = [
-            got[2, pl.ds((d * tiles + t) * ff, ff), :] for t in range(tiles)
+        halves = [
+            jnp.concatenate(
+                [w[2, pl.ds((d * tiles + t) * ff, ff), :] for t in range(tiles)], 1
+            )
+            for w in (kept, got)
         ]
-        weight = jnp.concatenate(
-            [down[:, pl.ds(d * col_width, col_width)], jnp.concatenate(theirs, 1)], 0
-        )
+        weight = jnp.concatenate(halves, 0)
         out[d] = jnp.dot(act, weight, preferred_element_type=f32).astype(bf16)
 
 
-def run_expert(keep, rows, gate, up, down, got):
-    vmem = pl.BlockSpec(memory_space=pltpu.VMEM)
-    hbm = pl.BlockSpec(memory_space=pltpu.HBM)
-    flops = 2 * rows.size * gate.shape[2] * 6
-    moved = 2 * (2 * rows.size + got.size) + 3 * gate.size
+def run_expert(rows, kept, got):
+    vmem = pl.BlockSpec(memory_space=pltpu.VMEM)
+    ff = kept.shape[2]
     return pl.pallas_call(
         expert_kernel,
         out_shape=jax.ShapeDtypeStruct(rows.shape, bf16),
-        in_specs=[pl.BlockSpec(memory_space=pltpu.SMEM), vmem, vmem, hbm, hbm, hbm],
+        in_specs=[vmem, vmem, vmem],
         out_specs=vmem,
-        scratch_shapes=[
-            pltpu.VMEM((2, *gate.shape[1:]), bf16),
-            pltpu.VMEM(down.shape[1:], bf16),
-            pltpu.SemaphoreType.DMA((3,)),
-        ],
-        cost_estimate=pl.CostEstimate(
-            flops=flops, bytes_accessed=moved, transcendentals=rows.shape[1] * 2 * HD
+        cost_estimate=pl.CostEstimate(
+            flops=12 * rows.size * ff,
+            bytes_accessed=4 * (rows.size + got.size),
+            transcendentals=rows.shape[1] * 2 * ff,
         ),
         compiler_params=pltpu.CompilerParams(vmem_limit_bytes=12 << 20),
         name="run_expert",
-    )(jnp.reshape(keep, (1,)).astype(i32), rows, got, *in_hbm(gate, up, down))
+    )(rows, kept, got)
 
 
 def layer(
@@ -508,11 +499,12 @@
     cache_all = exchange(by_head, "tensor")
 
     w_own = out_weight.T
-    mine = jnp.stack([w_own, across_chips(w_own)])
-    shift = chips // 4
-    while shift > 1:
-        mine = jnp.concatenate([mine, along_chips(mine, shift)])
-        shift //= 2
+    far = chips // 4
+    own_far = along_chips(w_own, far)
+    pair = across_chips(w_own, 1)
+    pair_far = across_chips(w_own, far + 1)
+    mine = jnp.stack([w_own, pair, own_far, pair_far])
+    mine = jnp.concatenate([mine, along_chips(mine, far // 2)])
     mine_b = along_chips(mine, 1)
     theirs_a = other_core(mine)
     theirs_b = other_core(mine_b)
@@ -562,7 +554,8 @@
     keep = pos_x % experts_here
     give = 1 - keep
     swap = [(i, i ^ 1) for i in range(n_x)]
-    giving = give_weights(give, w_gate, w_up, w_down)
+    which = jnp.stack([give, keep]).astype(i32)
+    giving, keeping = part_weights(which, w_gate, w_up, w_down)
     got_weights = lax.ppermute(giving, "tensor", swap)
 
     near = exchange(hidden, "chip")
@@ -583,7 +576,7 @@
     )
     rows_in = exchange(by_dest, "tensor")
 
-    out = run_expert(keep, rows_in, w_gate, w_up, w_down, got_weights)
+    out = run_expert(rows_in, keeping, got_weights)
     parts = exchange(out, "tensor")
     parts = parts.reshape(n_x // experts_here, experts_here, n_e, capacity, col_width)
     summed = jnp.sum(parts.astype(f32), 0).astype(bf16)

time: 252 us -> 258 us (1.024)
  starting transfers between devices: 108 us -> 122 us
  waiting for transfers between devices: 90.9 us -> 83.2 us
    all_to_all x6, starting transfers between devices: 41 us -> 50.4 us  [exchange(): return lax.all_to_all(tiles, axis, split_axis=0, concat_axis=0, tiled=True)]
    all_to_all x6, waiting for transfers between devices: 77.4 us -> 73.2 us  [exchange(): return lax.all_to_all(tiles, axis, split_axis=0, concat_axis=0, tiled=True)]
    ppermute x1 -> x2, starting transfers between devices: 45 us -> 47 us  [across_chips(): return lax.ppermute(x, EXPERT, moves)]
  transfers between devices with their start and end apart: 14 -> 15, of which waited for: 10 -> 8; matrix products, arithmetic and copies ran while one was open for 2% -> 2% of each run, Pallas kernels for 5% -> 6%
where the time goes in v7:
time: 258 us; the launch traced here: 257 us
  starting transfers between devices  122 us (47%)
  waiting for transfers between devices  83.2 us (32%)
  blocking collectives  25.5 us (10%)
  Pallas kernels  16.8 us (7%)
  other arithmetic  4.82 us (2%)
  local copies, waits for them, and re-layouts  2.68 us (1%)
    all_to_all x6, waiting for transfers between devices, exchange(): return lax.all_to_all(tiles, axis, split_axis=0, concat_axis=0, tiled=True)  73.2 us
    all_to_all x6, starting transfers between devices, exchange(): return lax.all_to_all(tiles, axis, split_axis=0, concat_axis=0, tiled=True)  50.4 us
    ppermute x2, starting transfers between devices, across_chips(): return lax.ppermute(x, EXPERT, moves)  47 us
    all_to_all x1, blocking collectives, exchange(): return lax.all_to_all(tiles, axis, split_axis=0, concat_axis=0, tiled=True)  25.5 us
    ppermute x3, starting transfers between devices, other_core(): return lax.ppermute(x, 'core', [(0, 1), (1, 0)])  13.7 us
    ppermute x3, waiting for transfers between devices, along_chips(): return lax.ppermute(x, EXPERT, moves)  8.66 us
    ppermute x3, starting transfers between devices, along_chips(): return lax.ppermute(x, EXPERT, moves)  6.91 us
  transfers between devices with their start and end apart: 15, of which 8 were waited for; matrix products, arithmetic and copies ran while one was open for 2% of the time, Pallas kernels for 6%

profile of v7, /device:TPU:65, one launch (start us, length us, event | category | flops | bytes accessed | tf_op | source)
XLA Modules:
  0.0 256.5 jit_solution(1440333869896013070)
XLA Ops:
  0.0 45.0 %collective-permute-start = (bf16[64,512]{1,0:T(8,128)(2,1)}, bf16[64,512]{1,0:T(8,128)(2,1)S(1)}, u32[]{:S(2)}, u32[]{:S(2)}) collective-permute-start(bf16[64,512]{1,0:T(8,128)(2,1)} %bitcast.51), channel_id=1, source_target_pairs={{0,24},{8,240},{16,40},{24,0},{32,56},{40,16},{48,72},{56,32},{64,... | collective-permute-start | bytes 196616 | tf_op jit(solution)/shard_map/ppermute | solution.py:35
  45.1 2.0 collective-permute-start.1
  47.0 2.0 collective-permute-start.2
  49.0 1.5 split_cache.1
  50.5 7.0 %all-to-all-start = ((bf16[8,32,256]{2,1,0:T(8,128)(2,1)}), bf16[8,32,256]{2,1,0:T(8,128)(2,1)S(1)}, u32[]{:S(2)}, u32[]{:S(2)}) async-start(bf16[8,32,256]{2,1,0:T(8,128)(2,1)} %split_cache.1), calls=%async_computation | async-start | bytes 262144 | tf_op jit(solution)/shard_map/all_to_all | solution.py:17
  57.5 0.8 constant_dynamic-update-slice_fusion.4
  58.4 0.5 collective-permute-done.2
  58.9 0.9 pad_maximum_fusion
  59.7 2.8 %collective-permute-start.3 = (bf16[4,64,512]{2,1,0:T(8,128)(2,1)S(1)}, bf16[4,64,512]{2,1,0:T(8,128)(2,1)S(1)}, u32[]{:S(2)}, u32[]{:S(2)}) collective-permute-start(bf16[4,64,512]{2,1,0:T(8,128)(2,1)S(1)} %pad_maximum_fusion), channel_id=1, source_target_pairs={{0,224},{8,40},{16,240},{24,56},{32,0},{40,72},{48,16},{56,88},{64... | collective-permute-start | bytes 786440 | tf_op jit(solution)/shard_map/ppermute | solution.py:26
  62.6 8.7 %collective-permute-done.3 = bf16[4,64,512]{2,1,0:T(8,128)(2,1)S(1)} collective-permute-done((bf16[4,64,512]{2,1,0:T(8,128)(2,1)S(1)}, bf16[4,64,512]{2,1,0:T(8,128)(2,1)S(1)}, u32[]{:S(2)}, u32[]{:S(2)}) %collective-permute-start.3) | collective-permute-done | bytes 262176 | tf_op jit(solution)/shard_map/ppermute | solution.py:26
  71.2 2.2 collective-permute-start.4
  73.4 0.1 pad_add_fusion.at
  73.5 2.5 build_payload.1
  76.0 14.0 %all-to-all-start.1 = ((bf16[32,24,128]{2,1,0:T(8,128)(2,1)}), bf16[32,24,128]{2,1,0:T(8,128)(2,1)S(1)}, u32[]{:S(2)}, u32[]{:S(2)}) async-start(bf16[32,24,128]{2,1,0:T(8,128)(2,1)} %bitcast.5), calls=%async_computation.1 | async-start | bytes 393216 | tf_op jit(solution)/shard_map/all_to_all | solution.py:17
  90.0 0.1 pad_add_fusion.3.which
  90.1 3.6 %part_weights.1 = (bf16[3,2048,128]{2,1,0:T(8,128)(2,1)}, bf16[3,2048,128]{2,1,0:T(8,128)(2,1)S(1)}) custom-call(s32[2]{0:T(128)S(1)} %pad_add_fusion.3.which, bf16[2,2048,128]{2,1,0:T(8,128)(2,1)} %gate.1, bf16[2,2048,128]{2,1,0:T(8,128)(2,1)} %up.1, bf16[2,128,2048]{2,1,0:T(8,128)(2,1)} %down.1), custom_call_target="tpu_custom_call" | custom-call | flops 524288 | bytes 6291456 | tf_op jit(solution)/shard_map/part_weights/pallas_call | solution.py:403
  93.7 3.7 %collective-permute-start.8 = (bf16[3,2048,128]{2,1,0:T(8,128)(2,1)}, bf16[3,2048,128]{2,1,0:T(8,128)(2,1)}, u32[]{:S(2)}, u32[]{:S(2)}) collective-permute-start(bf16[3,2048,128]{2,1,0:T(8,128)(2,1)} %get-tuple-element.20), channel_id=1, source_target_pairs={{0,1},{1,0},{2,3},{3,2},{4,5},{5,4},{6,7},{7,6},{8,9},{9,8},{10,11... | collective-permute-start | bytes 4718600 | tf_op jit(solution)/shard_map/ppermute | solution.py:559
  98.0 2.9 %collective-permute-start.5 = (bf16[8,64,512]{2,1,0:T(8,128)(2,1)S(1)}, bf16[8,64,512]{2,1,0:T(8,128)(2,1)S(1)}, u32[]{:S(2)}, u32[]{:S(2)}) collective-permute-start(bf16[8,64,512]{2,1,0:T(8,128)(2,1)S(1)} %constant_dynamic-update-slice_fusion.mine_a), channel_id=1, source_target_pairs={{0,8},{8,0},{1,9},{9,1},{2,10},{10,2},{3,11},{11,3},{4,12},{12,4},... | collective-permute-start | bytes 1572872 | tf_op jit(solution)/shard_map/ppermute | solution.py:39
  101.0 2.0 collective-permute-start.6
  102.9 0.1 pad_add_fusion.2.at
  103.0 0.1 pad_add_fusion.1.at
  103.1 5.4 %all-to-all-done.1 = bf16[32,24,128]{2,1,0:T(8,128)(2,1)S(1)} async-done(((bf16[32,24,128]{2,1,0:T(8,128)(2,1)}), bf16[32,24,128]{2,1,0:T(8,128)(2,1)S(1)}, u32[]{:S(2)}, u32[]{:S(2)}) %all-to-all-start.1) | async-done | bytes 196640 | tf_op jit(solution)/shard_map/all_to_all | solution.py:17
  108.5 2.2 attend.1
  110.8 2.6 %project_out.1 = bf16[8,32,256]{2,1,0:T(8,128)(2,1)} custom-call(s32[2]{0:T(128)S(1)} %pad_add_fusion.1.at, bf16[32,512]{1,0:T(8,128)(2,1)S(1)} %get-tuple-element.15.attn, bf16[8,64,512]{2,1,0:T(8,128)(2,1)S(1)} %constant_dynamic-update-slice_fusion.mine_a, bf16[8,64,512]{2,1,0:T(8,128)(2,1)S(1)} %collective-permute-done.4.mine_b, ...), custom_call_target="tpu_custom_call" | custom-call | flops 67108864 | bytes 2097152 | tf_op jit(solution)/shard_map/project_out/pallas_call | solution.py:366
  113.4 6.9 %all-to-all-start.2 = ((bf16[8,32,256]{2,1,0:T(8,128)(2,1)}), bf16[8,32,256]{2,1,0:T(8,128)(2,1)S(1)}, u32[]{:S(2)}, u32[]{:S(2)}) async-start(bf16[8,32,256]{2,1,0:T(8,128)(2,1)} %project_out.1), calls=%async_computation.2 | async-start | bytes 262144 | tf_op jit(solution)/shard_map/all_to_all | solution.py:17
  120.4 0.1 slice_bitcast_fusion
  120.4 0.1 copy.36
  120.5 0.6 fusion.2
  121.1 16.4 %all-to-all-done.2.parts = bf16[8,32,256]{2,1,0:T(8,128)(2,1)S(1)} async-done(((bf16[8,32,256]{2,1,0:T(8,128)(2,1)}), bf16[8,32,256]{2,1,0:T(8,128)(2,1)S(1)}, u32[]{:S(2)}, u32[]{:S(2)}) %all-to-all-start.2) | async-done | bytes 131104 | tf_op jit(solution)/shard_map/all_to_all | solution.py:17
  137.5 0.7 hidden_copies.1
  138.3 12.0 %all-to-all-start.3 = ((bf16[16,32,256]{2,1,0:T(8,128)(2,1)}), bf16[16,32,256]{2,1,0:T(8,128)(2,1)S(1)}, u32[]{:S(2)}, u32[]{:S(2)}) async-start(bf16[16,32,256]{2,1,0:T(8,128)(2,1)} %hidden_copies.1), calls=%async_computation.3 | async-start | bytes 524288 | tf_op jit(solution)/shard_map/all_to_all | solution.py:17
  150.2 0.2 compare_reduce_fusion
  150.4 0.2 convolution_convert_fusion.1
  150.6 1.3 select_reduce_fusion
  151.9 0.1 fusion
  152.1 0.1 broadcast_add_fusion
  152.2 0.3 select_reduce_fusion.1
  152.4 10.3 %all-to-all-done.3 = bf16[16,32,256]{2,1,0:T(8,128)(2,1)S(1)} async-done(((bf16[16,32,256]{2,1,0:T(8,128)(2,1)}), bf16[16,32,256]{2,1,0:T(8,128)(2,1)S(1)}, u32[]{:S(2)}, u32[]{:S(2)}) %all-to-all-start.3) | async-done | bytes 262176 | tf_op jit(solution)/shard_map/all_to_all | solution.py:17
  162.8 8.9 %collective-permute-start.7 = (bf16[16,32,256]{2,1,0:T(8,128)(2,1)S(1)}, bf16[16,32,256]{2,1,0:T(8,128)(2,1)S(1)}, u32[]{:S(2)}, u32[]{:S(2)}) collective-permute-start(bf16[16,32,256]{2,1,0:T(8,128)(2,1)S(1)} %all-to-all-done.3), channel_id=1, source_target_pairs={{0,8},{8,0},{1,9},{9,1},{2,10},{10,2},{3,11},{11,3},{4,12},{12,4},... | collective-permute-start | bytes 786440 | tf_op jit(solution)/shard_map/ppermute | solution.py:39
  171.7 0.1 copy.37
  171.7 0.1 sub.24.experts_at
  171.9 0.1 copy.39.home_at
  172.0 0.8 collective-permute-done.7
  172.8 1.4 select_rows.1
  174.1 3.8 %all-to-all-start.4 = ((bf16[8,192,256]{2,1,0:T(8,128)(2,1)}), bf16[8,192,256]{2,1,0:T(8,128)(2,1)S(1)}, u32[]{:S(2)}, u32[]{:S(2)}) async-start(bf16[8,192,256]{2,1,0:T(8,128)(2,1)} %get-tuple-element.18), calls=%async_computation.4 | async-start | bytes 1572864 | tf_op jit(solution)/shard_map/all_to_all | solution.py:17
  177.9 23.4 %all-to-all-done.4.rows = bf16[8,192,256]{2,1,0:T(8,128)(2,1)S(1)} async-done(((bf16[8,192,256]{2,1,0:T(8,128)(2,1)}), bf16[8,192,256]{2,1,0:T(8,128)(2,1)S(1)}, u32[]{:S(2)}, u32[]{:S(2)}) %all-to-all-start.4) | async-done | bytes 786464 | tf_op jit(solution)/shard_map/all_to_all | solution.py:17
  201.3 2.3 run_expert.1
  203.6 0.0 copy-start
  203.6 0.0 copy-start.1
  203.6 25.5 %all_to_all.35 = bf16[8,192,256]{2,1,0:T(8,128)(2,1)S(1)} all-to-all(bf16[8,192,256]{2,1,0:T(8,128)(2,1)S(1)} %run_expert.1), channel_id=1, replica_groups=mesh['groups'=2,'chip'=16,'core'=2,'tensor'=8] {'tensor'}, dimensions={0} | all-to-all | bytes 1572864 | tf_op jit(solution)/shard_map/all_to_all | solution.py:17
  229.1 0.2 reduce.1
  229.3 0.9 copy.46
  230.2 6.7 %all-to-all-start.6 = ((bf16[32,2,6,256]{3,1,2,0:T(2,128)(2,1)}), bf16[32,2,6,256]{3,1,2,0:T(2,128)(2,1)S(1)}, u32[]{:S(2)}, u32[]{:S(2)}) async-start(bf16[32,2,6,256]{3,1,2,0:T(2,128)(2,1)} %bitcast.25), calls=%async_computation.6 | async-start | bytes 393216 | tf_op jit(solution)/shard_map/all_to_all | solution.py:17
  236.9 0.1 copy.40
  237.0 0.1 copy.42
  237.1 0.1 select_reduce_fusion.2
  237.3 0.1 copy.43
  237.3 0.1 fusion.4
  237.5 0.1 fusion.1
  237.6 0.1 copy.41
  237.8 17.7 %all-to-all-done.6 = bf16[32,2,6,256]{3,1,2,0:T(2,128)(2,1)S(1)} async-done(((bf16[32,2,6,256]{3,1,2,0:T(2,128)(2,1)}), bf16[32,2,6,256]{3,1,2,0:T(2,128)(2,1)S(1)}, u32[]{:S(2)}, u32[]{:S(2)}) %all-to-all-start.6) | async-done | bytes 196640 | tf_op jit(solution)/shard_map/all_to_all | solution.py:17
  255.5 0.1 reshape.168
  255.6 0.3 fusion.17
  255.9 0.6 add_convert_fusion
  (22 shorter events, 0.2 us)
Async XLA Ops:
  0.0 58.4 %collective-permute-start = (bf16[64,512]{1,0:T(8,128)(2,1)}, bf16[64,512]{1,0:T(8,128)(2,1)S(1)}, u32[]{:S(2)}, u32[]{:S(2)}) collective-permute-start(bf16[64,512]{1,0:T(8,128)(2,1)} %bitcast.51), channel_id=1, source_target_pairs={{0,24},{8,240},{16,40},{24,0},{32,56},{40,16},{48,72},{56,32},{64,... | collective-permute-start | bytes 196616 | tf_op jit(solution)/shard_map/ppermute | solution.py:35
  45.1 13.3 %collective-permute-start.1 = (bf16[64,512]{1,0:T(8,128)(2,1)}, bf16[64,512]{1,0:T(8,128)(2,1)S(1)}, u32[]{:S(2)}, u32[]{:S(2)}) collective-permute-start(bf16[64,512]{1,0:T(8,128)(2,1)} %bitcast.52), channel_id=1, source_target_pairs={{0,192},{8,72},{16,208},{24,88},{32,224},{40,104},{48,240},{56,120... | collective-permute-start | bytes 196616 | tf_op jit(solution)/shard_map/ppermute | solution.py:26
  47.0 11.8 %collective-permute-start.2 = (bf16[64,512]{1,0:T(8,128)(2,1)}, bf16[64,512]{1,0:T(8,128)(2,1)S(1)}, u32[]{:S(2)}, u32[]{:S(2)}) collective-permute-start(bf16[64,512]{1,0:T(8,128)(2,1)} %bitcast.53), channel_id=1, source_target_pairs={{0,88},{8,176},{16,104},{24,192},{32,120},{40,208},{48,136},{56,22... | collective-permute-start | bytes 196616 | tf_op jit(solution)/shard_map/ppermute | solution.py:35
  50.5 25.5 %all-to-all-start = ((bf16[8,32,256]{2,1,0:T(8,128)(2,1)}), bf16[8,32,256]{2,1,0:T(8,128)(2,1)S(1)}, u32[]{:S(2)}, u32[]{:S(2)}) async-start(bf16[8,32,256]{2,1,0:T(8,128)(2,1)} %split_cache.1), calls=%async_computation | async-start | bytes 262144 | tf_op jit(solution)/shard_map/all_to_all | solution.py:17
  59.7 11.5 %collective-permute-start.3 = (bf16[4,64,512]{2,1,0:T(8,128)(2,1)S(1)}, bf16[4,64,512]{2,1,0:T(8,128)(2,1)S(1)}, u32[]{:S(2)}, u32[]{:S(2)}) collective-permute-start(bf16[4,64,512]{2,1,0:T(8,128)(2,1)S(1)} %pad_maximum_fusion), channel_id=1, source_target_pairs={{0,224},{8,40},{16,240},{24,56},{32,0},{40,72},{48,16},{56,88},{64... | collective-permute-start | bytes 786440 | tf_op jit(solution)/shard_map/ppermute | solution.py:26
  71.2 29.7 %collective-permute-start.4 = (bf16[8,64,512]{2,1,0:T(8,128)(2,1)S(1)}, bf16[8,64,512]{2,1,0:T(8,128)(2,1)S(1)}, u32[]{:S(2)}, u32[]{:S(2)}) collective-permute-start(bf16[8,64,512]{2,1,0:T(8,128)(2,1)S(1)} %constant_dynamic-update-slice_fusion.mine_a), channel_id=1, source_target_pairs={{0,240},{8,24},{16,0},{24,40},{32,16},{40,56},{48,32},{56,72},{64,... | collective-permute-start | bytes 1572872 | tf_op jit(solution)/shard_map/ppermute | solution.py:26
  76.0 32.5 %all-to-all-start.1 = ((bf16[32,24,128]{2,1,0:T(8,128)(2,1)}), bf16[32,24,128]{2,1,0:T(8,128)(2,1)S(1)}, u32[]{:S(2)}, u32[]{:S(2)}) async-start(bf16[32,24,128]{2,1,0:T(8,128)(2,1)} %bitcast.5), calls=%async_computation.1 | async-start | bytes 393216 | tf_op jit(solution)/shard_map/all_to_all | solution.py:17
  93.7 84.2 %collective-permute-start.8 = (bf16[3,2048,128]{2,1,0:T(8,128)(2,1)}, bf16[3,2048,128]{2,1,0:T(8,128)(2,1)}, u32[]{:S(2)}, u32[]{:S(2)}) collective-permute-start(bf16[3,2048,128]{2,1,0:T(8,128)(2,1)} %get-tuple-element.20), channel_id=1, source_target_pairs={{0,1},{1,0},{2,3},{3,2},{4,5},{5,4},{6,7},{7,6},{8,9},{9,8},{10,11... | collective-permute-start | bytes 4718600 | tf_op jit(solution)/shard_map/ppermute | solution.py:559
  98.0 12.8 %collective-permute-start.5 = (bf16[8,64,512]{2,1,0:T(8,128)(2,1)S(1)}, bf16[8,64,512]{2,1,0:T(8,128)(2,1)S(1)}, u32[]{:S(2)}, u32[]{:S(2)}) collective-permute-start(bf16[8,64,512]{2,1,0:T(8,128)(2,1)S(1)} %constant_dynamic-update-slice_fusion.mine_a), channel_id=1, source_target_pairs={{0,8},{8,0},{1,9},{9,1},{2,10},{10,2},{3,11},{11,3},{4,12},{12,4},... | collective-permute-start | bytes 1572872 | tf_op jit(solution)/shard_map/ppermute | solution.py:39
  101.0 9.8 %collective-permute-start.6 = (bf16[8,64,512]{2,1,0:T(8,128)(2,1)S(1)}, bf16[8,64,512]{2,1,0:T(8,128)(2,1)}, u32[]{:S(2)}, u32[]{:S(2)}) collective-permute-start(bf16[8,64,512]{2,1,0:T(8,128)(2,1)S(1)} %collective-permute-done.4.mine_b), channel_id=1, source_target_pairs={{0,8},{8,0},{1,9},{9,1},{2,10},{10,2},{3,11},{11,3},{4,12},{12,4},... | collective-permute-start | bytes 1572872 | tf_op jit(solution)/shard_map/ppermute | solution.py:39
  113.4 24.1 %all-to-all-start.2 = ((bf16[8,32,256]{2,1,0:T(8,128)(2,1)}), bf16[8,32,256]{2,1,0:T(8,128)(2,1)S(1)}, u32[]{:S(2)}, u32[]{:S(2)}) async-start(bf16[8,32,256]{2,1,0:T(8,128)(2,1)} %project_out.1), calls=%async_computation.2 | async-start | bytes 262144 | tf_op jit(solution)/shard_map/all_to_all | solution.py:17
  138.3 24.5 %all-to-all-start.3 = ((bf16[16,32,256]{2,1,0:T(8,128)(2,1)}), bf16[16,32,256]{2,1,0:T(8,128)(2,1)S(1)}, u32[]{:S(2)}, u32[]{:S(2)}) async-start(bf16[16,32,256]{2,1,0:T(8,128)(2,1)} %hidden_copies.1), calls=%async_computation.3 | async-start | bytes 524288 | tf_op jit(solution)/shard_map/all_to_all | solution.py:17
  162.8 10.0 %collective-permute-start.7 = (bf16[16,32,256]{2,1,0:T(8,128)(2,1)S(1)}, bf16[16,32,256]{2,1,0:T(8,128)(2,1)S(1)}, u32[]{:S(2)}, u32[]{:S(2)}) collective-permute-start(bf16[16,32,256]{2,1,0:T(8,128)(2,1)S(1)} %all-to-all-done.3), channel_id=1, source_target_pairs={{0,8},{8,0},{1,9},{9,1},{2,10},{10,2},{3,11},{11,3},{4,12},{12,4},... | collective-permute-start | bytes 786440 | tf_op jit(solution)/shard_map/ppermute | solution.py:39
  174.1 27.2 %all-to-all-start.4 = ((bf16[8,192,256]{2,1,0:T(8,128)(2,1)}), bf16[8,192,256]{2,1,0:T(8,128)(2,1)S(1)}, u32[]{:S(2)}, u32[]{:S(2)}) async-start(bf16[8,192,256]{2,1,0:T(8,128)(2,1)} %get-tuple-element.18), calls=%async_computation.4 | async-start | bytes 1572864 | tf_op jit(solution)/shard_map/all_to_all | solution.py:17
  203.6 33.3 %copy-start = (s32[32,8]{0,1:T(8,128)S(1)}, s32[32,8]{0,1:T(8,128)}, u32[]{:S(2)}) copy-start(s32[32,8]{0,1:T(8,128)} %param.19) | copy-start | bytes 3076
  203.6 33.4 %copy-start.1 = (f32[32,8]{0,1:T(8,128)S(1)}, f32[32,8]{0,1:T(8,128)}, u32[]{:S(2)}) copy-start(f32[32,8]{0,1:T(8,128)} %param.20) | copy-start | bytes 3076
  230.2 25.3 %all-to-all-start.6 = ((bf16[32,2,6,256]{3,1,2,0:T(2,128)(2,1)}), bf16[32,2,6,256]{3,1,2,0:T(2,128)(2,1)S(1)}, u32[]{:S(2)}, u32[]{:S(2)}) async-start(bf16[32,2,6,256]{3,1,2,0:T(2,128)(2,1)} %bitcast.25), calls=%async_computation.6 | async-start | bytes 393216 | tf_op jit(solution)/shard_map/all_to_all | solution.py:17

commit v8 on v7

--- a/solution.py
+++ b/solution.py
@@ -26,12 +26,12 @@
     return lax.ppermute(x, EXPERT, moves)
 
 
-def across_chips(x, shift):
+def across_chips(x):
     n = lax.axis_size("chip")
     moves = []
     for c in range(n):
-        moves.append((c * CORES, (c + shift) % n * CORES + 1))
-        moves.append((c * CORES + 1, (c - shift) % n * CORES))
+        moves.append((c * CORES, (c + 1) % n * CORES + 1))
+        moves.append((c * CORES + 1, (c - 1) % n * CORES))
     return lax.ppermute(x, EXPERT, moves)
 
 
@@ -499,12 +499,11 @@
     cache_all = exchange(by_head, "tensor")
 
     w_own = out_weight.T
-    far = chips // 4
-    own_far = along_chips(w_own, far)
-    pair = across_chips(w_own, 1)
-    pair_far = across_chips(w_own, far + 1)
-    mine = jnp.stack([w_own, pair, own_far, pair_far])
-    mine = jnp.concatenate([mine, along_chips(mine, far // 2)])
+    mine = jnp.stack([w_own, across_chips(w_own)])
+    shift = chips // 4
+    while shift > 1:
+        mine = jnp.concatenate([mine, along_chips(mine, shift)])
+        shift //= 2
     mine_b = along_chips(mine, 1)
     theirs_a = other_core(mine)
     theirs_b = other_core(mine_b)
@@ -553,10 +552,13 @@
 
     keep = pos_x % experts_here
     give = 1 - keep
-    swap = [(i, i ^ 1) for i in range(n_x)]
+    swap = []
+    for i in range(n_x):
+        swap.append((i, i ^ 1))
+        swap.append((n_x + i, n_x + (i + (1 if i % 2 else -1)) % n_x))
     which = jnp.stack([give, keep]).astype(i32)
     giving, keeping = part_weights(which, w_gate, w_up, w_down)
-    got_weights = lax.ppermute(giving, "tensor", swap)
+    got_weights = lax.ppermute(giving, ("core", "tensor"), swap)
 
     near = exchange(hidden, "chip")
     across = other_core(near)

time: 258 us -> 237 us (0.919)
  starting transfers between devices: 122 us -> 101 us
    all_to_all x6, starting transfers between devices: 50.4 us -> 34.4 us  [exchange(): return lax.all_to_all(tiles, axis, split_axis=0, concat_axis=0, tiled=True)]
    all_to_all x6, waiting for transfers between devices: 73.2 us -> 68.6 us  [exchange(): return lax.all_to_all(tiles, axis, split_axis=0, concat_axis=0, tiled=True)]
    ppermute x2 -> x1, starting transfers between devices: 47 us -> 45 us  [across_chips(): return lax.ppermute(x, EXPERT, moves)]
  transfers between devices with their start and end apart: 15 -> 14, of which waited for: 8 -> 10; matrix products, arithmetic and copies ran while one was open for 2% -> 2% of each run, Pallas kernels for 6% -> 6%
where the time goes in v8:
time: 237 us; the launch traced here: 236 us
  starting transfers between devices  101 us (43%)
  waiting for transfers between devices  82.1 us (35%)
  blocking collectives  25.5 us (11%)
  Pallas kernels  16.8 us (7%)
  other arithmetic  6.56 us (3%)
    all_to_all x6, waiting for transfers between devices, exchange(): return lax.all_to_all(tiles, axis, split_axis=0, concat_axis=0, tiled=True)  68.6 us
    ppermute x1, starting transfers between devices, across_chips(): return lax.ppermute(x, EXPERT, moves)  45 us
    all_to_all x6, starting transfers between devices, exchange(): return lax.all_to_all(tiles, axis, split_axis=0, concat_axis=0, tiled=True)  34.4 us
    all_to_all x1, blocking collectives, exchange(): return lax.all_to_all(tiles, axis, split_axis=0, concat_axis=0, tiled=True)  25.5 us
    ppermute x3, starting transfers between devices, other_core(): return lax.ppermute(x, 'core', [(0, 1), (1, 0)])  13.7 us
    ppermute x3, waiting for transfers between devices, along_chips(): return lax.ppermute(x, EXPERT, moves)  10.5 us
    ppermute x3, starting transfers between devices, along_chips(): return lax.ppermute(x, EXPERT, moves)  5.85 us
  transfers between devices with their start and end apart: 14, of which 10 were waited for; matrix products, arithmetic and copies ran while one was open for 2% of the time, Pallas kernels for 6%

profile of v8, /device:TPU:65, one launch (start us, length us, event | category | flops | bytes accessed | tf_op | source)
XLA Modules:
  0.0 235.5 jit_solution(4197116132697233041)
XLA Ops:
  0.0 45.0 %collective-permute-start = (bf16[64,512]{1,0:T(8,128)(2,1)}, bf16[64,512]{1,0:T(8,128)(2,1)S(1)}, u32[]{:S(2)}, u32[]{:S(2)}) collective-permute-start(bf16[64,512]{1,0:T(8,128)(2,1)} %bitcast.45), channel_id=1, source_target_pairs={{0,24},{8,240},{16,40},{24,0},{32,56},{40,16},{48,72},{56,32},{64,... | collective-permute-start | bytes 196616 | tf_op jit(solution)/shard_map/ppermute | solution.py:35
  45.1 2.1 collective-permute-done
  47.2 0.9 pad_maximum_fusion.2
  48.1 2.0 collective-permute-start.1
  50.0 10.4 %collective-permute-done.1 = bf16[2,64,512]{2,1,0:T(8,128)(2,1)S(1)} collective-permute-done((bf16[2,64,512]{2,1,0:T(8,128)(2,1)S(1)}, bf16[2,64,512]{2,1,0:T(8,128)(2,1)S(1)}, u32[]{:S(2)}, u32[]{:S(2)}) %collective-permute-start.1) | collective-permute-done | bytes 131104 | tf_op jit(solution)/shard_map/ppermute | solution.py:26
  60.4 0.9 pad_maximum_fusion.1
  61.3 2.0 collective-permute-start.2
  63.2 1.5 split_cache.1
  64.7 6.9 %all-to-all-start = ((bf16[8,32,256]{2,1,0:T(8,128)(2,1)}), bf16[8,32,256]{2,1,0:T(8,128)(2,1)S(1)}, u32[]{:S(2)}, u32[]{:S(2)}) async-start(bf16[8,32,256]{2,1,0:T(8,128)(2,1)} %split_cache.1), calls=%async_computation | async-start | bytes 262144 | tf_op jit(solution)/shard_map/all_to_all | solution.py:17
  71.7 0.2 collective-permute-done.2
  71.8 0.9 pad_maximum_fusion.mine_a
  72.7 2.0 collective-permute-start.3
  74.7 0.1 pad_add_fusion.at
  74.8 2.5 %build_payload.1 = bf16[768,128]{1,0:T(8,128)(2,1)} custom-call(s32[3]{0:T(128)S(1)} %pad_add_fusion.at, s32[1,32]{1,0:T(1,128)} %bitcast.53, s32[8,32]{1,0:T(8,128)} %bitcast.52, bf16[32,4096]{1,0:T(8,128)(2,1)} %queries.1, bf16[32,1024]{1,0:T(8,128)(2,1)} %own_kv.1, bf16[32,2048]{1,0:T(8,128)(2,1)} %residual.1), custom_call_target="tpu_custom_call" | custom-call | flops 75497472 | bytes 393216 | tf_op jit(solution)/shard_map/build_payload/pallas_call | solution.py:130
  77.3 2.8 %all-to-all-done.cache = bf16[8,32,256]{2,1,0:T(8,128)(2,1)S(1)} async-done(((bf16[8,32,256]{2,1,0:T(8,128)(2,1)}), bf16[8,32,256]{2,1,0:T(8,128)(2,1)S(1)}, u32[]{:S(2)}, u32[]{:S(2)}) %all-to-all-start) | async-done | bytes 131104 | tf_op jit(solution)/shard_map/all_to_all | solution.py:17
  80.1 7.2 %all-to-all-start.1 = ((bf16[32,24,128]{2,1,0:T(8,128)(2,1)}), bf16[32,24,128]{2,1,0:T(8,128)(2,1)S(1)}, u32[]{:S(2)}, u32[]{:S(2)}) async-start(bf16[32,24,128]{2,1,0:T(8,128)(2,1)} %bitcast.5), calls=%async_computation.1 | async-start | bytes 393216 | tf_op jit(solution)/shard_map/all_to_all | solution.py:17
  87.4 0.1 pad_add_fusion.3.which
  87.4 3.6 %part_weights.1 = (bf16[3,2048,128]{2,1,0:T(8,128)(2,1)}, bf16[3,2048,128]{2,1,0:T(8,128)(2,1)S(1)}) custom-call(s32[2]{0:T(128)S(1)} %pad_add_fusion.3.which, bf16[2,2048,128]{2,1,0:T(8,128)(2,1)} %gate.1, bf16[2,2048,128]{2,1,0:T(8,128)(2,1)} %up.1, bf16[2,128,2048]{2,1,0:T(8,128)(2,1)} %down.1), custom_call_target="tpu_custom_call" | custom-call | flops 524288 | bytes 6291456 | tf_op jit(solution)/shard_map/part_weights/pallas_call | solution.py:403
  91.0 2.0 collective-permute-start.7
  93.7 3.2 %collective-permute-start.4 = (bf16[8,64,512]{2,1,0:T(8,128)(2,1)S(1)}, bf16[8,64,512]{2,1,0:T(8,128)(2,1)S(1)}, u32[]{:S(2)}, u32[]{:S(2)}) collective-permute-start(bf16[8,64,512]{2,1,0:T(8,128)(2,1)S(1)} %pad_maximum_fusion.mine_a), channel_id=1, source_target_pairs={{0,8},{8,0},{1,9},{9,1},{2,10},{10,2},{3,11},{11,3},{4,12},{12,4},... | collective-permute-start | bytes 1572872 | tf_op jit(solution)/shard_map/ppermute | solution.py:39
  96.9 2.0 collective-permute-start.5
  98.8 0.1 pad_add_fusion.2.at
  98.9 0.1 pad_add_fusion.1.at
  99.0 6.9 %all-to-all-done.1 = bf16[32,24,128]{2,1,0:T(8,128)(2,1)S(1)} async-done(((bf16[32,24,128]{2,1,0:T(8,128)(2,1)}), bf16[32,24,128]{2,1,0:T(8,128)(2,1)S(1)}, u32[]{:S(2)}, u32[]{:S(2)}) %all-to-all-start.1) | async-done | bytes 196640 | tf_op jit(solution)/shard_map/all_to_all | solution.py:17
  105.9 2.2 attend.1
  108.2 2.6 %project_out.1 = bf16[8,32,256]{2,1,0:T(8,128)(2,1)} custom-call(s32[2]{0:T(128)S(1)} %pad_add_fusion.1.at, bf16[32,512]{1,0:T(8,128)(2,1)S(1)} %get-tuple-element.15.attn, bf16[8,64,512]{2,1,0:T(8,128)(2,1)S(1)} %pad_maximum_fusion.mine_a, bf16[8,64,512]{2,1,0:T(8,128)(2,1)S(1)} %collective-permute-done.3.mine_b, ...), custom_call_target="tpu_custom_call" | custom-call | flops 67108864 | bytes 2097152 | tf_op jit(solution)/shard_map/project_out/pallas_call | solution.py:366
  110.8 3.9 %all-to-all-start.2 = ((bf16[8,32,256]{2,1,0:T(8,128)(2,1)}), bf16[8,32,256]{2,1,0:T(8,128)(2,1)S(1)}, u32[]{:S(2)}, u32[]{:S(2)}) async-start(bf16[8,32,256]{2,1,0:T(8,128)(2,1)} %project_out.1), calls=%async_computation.2 | async-start | bytes 262144 | tf_op jit(solution)/shard_map/all_to_all | solution.py:17
  114.7 0.1 slice_bitcast_fusion
  114.7 0.1 copy.36
  114.8 0.6 fusion.2
  115.4 7.2 %all-to-all-done.2.parts = bf16[8,32,256]{2,1,0:T(8,128)(2,1)S(1)} async-done(((bf16[8,32,256]{2,1,0:T(8,128)(2,1)}), bf16[8,32,256]{2,1,0:T(8,128)(2,1)S(1)}, u32[]{:S(2)}, u32[]{:S(2)}) %all-to-all-start.2) | async-done | bytes 131104 | tf_op jit(solution)/shard_map/all_to_all | solution.py:17
  122.6 0.7 hidden_copies.1
  123.3 5.6 %all-to-all-start.3 = ((bf16[16,32,256]{2,1,0:T(8,128)(2,1)}), bf16[16,32,256]{2,1,0:T(8,128)(2,1)S(1)}, u32[]{:S(2)}, u32[]{:S(2)}) async-start(bf16[16,32,256]{2,1,0:T(8,128)(2,1)} %hidden_copies.1), calls=%async_computation.3 | async-start | bytes 524288 | tf_op jit(solution)/shard_map/all_to_all | solution.py:17
  129.0 0.2 compare_reduce_fusion
  129.1 0.2 convolution_convert_fusion.1
  129.3 1.3 select_reduce_fusion
  130.6 0.1 fusion
  130.8 0.1 broadcast_add_fusion
  130.9 0.3 select_reduce_fusion.1
  131.2 10.5 %all-to-all-done.3 = bf16[16,32,256]{2,1,0:T(8,128)(2,1)S(1)} async-done(((bf16[16,32,256]{2,1,0:T(8,128)(2,1)}), bf16[16,32,256]{2,1,0:T(8,128)(2,1)S(1)}, u32[]{:S(2)}, u32[]{:S(2)}) %all-to-all-start.3) | async-done | bytes 262176 | tf_op jit(solution)/shard_map/all_to_all | solution.py:17
  141.7 8.6 %collective-permute-start.6 = (bf16[16,32,256]{2,1,0:T(8,128)(2,1)S(1)}, bf16[16,32,256]{2,1,0:T(8,128)(2,1)S(1)}, u32[]{:S(2)}, u32[]{:S(2)}) collective-permute-start(bf16[16,32,256]{2,1,0:T(8,128)(2,1)S(1)} %all-to-all-done.3), channel_id=1, source_target_pairs={{0,8},{8,0},{1,9},{9,1},{2,10},{10,2},{3,11},{11,3},{4,12},{12,4},... | collective-permute-start | bytes 786440 | tf_op jit(solution)/shard_map/ppermute | solution.py:39
  150.3 0.1 copy.37
  150.4 0.1 sub.24.experts_at
  150.5 0.1 copy.39.home_at
  150.6 0.8 collective-permute-done.6
  151.4 1.4 select_rows.1
  152.7 4.1 %all-to-all-start.4 = ((bf16[8,192,256]{2,1,0:T(8,128)(2,1)}), bf16[8,192,256]{2,1,0:T(8,128)(2,1)S(1)}, u32[]{:S(2)}, u32[]{:S(2)}) async-start(bf16[8,192,256]{2,1,0:T(8,128)(2,1)} %get-tuple-element.18), calls=%async_computation.4 | async-start | bytes 1572864 | tf_op jit(solution)/shard_map/all_to_all | solution.py:17
  156.9 23.6 %all-to-all-done.4.rows = bf16[8,192,256]{2,1,0:T(8,128)(2,1)S(1)} async-done(((bf16[8,192,256]{2,1,0:T(8,128)(2,1)}), bf16[8,192,256]{2,1,0:T(8,128)(2,1)S(1)}, u32[]{:S(2)}, u32[]{:S(2)}) %all-to-all-start.4) | async-done | bytes 786464 | tf_op jit(solution)/shard_map/all_to_all | solution.py:17
  180.4 2.3 run_expert.1
  182.8 25.5 %all_to_all.35 = bf16[8,192,256]{2,1,0:T(8,128)(2,1)S(1)} all-to-all(bf16[8,192,256]{2,1,0:T(8,128)(2,1)S(1)} %run_expert.1), channel_id=1, replica_groups=mesh['groups'=2,'chip'=16,'core'=2,'tensor'=8] {'tensor'}, dimensions={0} | all-to-all | bytes 1572864 | tf_op jit(solution)/shard_map/all_to_all | solution.py:17
  208.3 0.2 reduce.1
  208.5 0.9 copy.46
  209.4 6.6 %all-to-all-start.6 = ((bf16[32,2,6,256]{3,1,2,0:T(2,128)(2,1)}), bf16[32,2,6,256]{3,1,2,0:T(2,128)(2,1)S(1)}, u32[]{:S(2)}, u32[]{:S(2)}) async-start(bf16[32,2,6,256]{3,1,2,0:T(2,128)(2,1)} %bitcast.23), calls=%async_computation.6 | async-start | bytes 393216 | tf_op jit(solution)/shard_map/all_to_all | solution.py:17
  216.0 0.1 copy.40
  216.1 0.1 copy.42
  216.1 0.1 select_reduce_fusion.2
  216.3 0.1 copy.43
  216.4 0.1 fusion.4
  216.5 0.1 fusion.1
  216.6 0.1 copy.41
  216.8 17.7 %all-to-all-done.6 = bf16[32,2,6,256]{3,1,2,0:T(2,128)(2,1)S(1)} async-done(((bf16[32,2,6,256]{3,1,2,0:T(2,128)(2,1)}), bf16[32,2,6,256]{3,1,2,0:T(2,128)(2,1)S(1)}, u32[]{:S(2)}, u32[]{:S(2)}) %all-to-all-start.6) | async-done | bytes 196640 | tf_op jit(solution)/shard_map/all_to_all | solution.py:17
  234.5 0.1 reshape.168
  234.6 0.3 fusion.17
  234.9 0.6 add_convert_fusion
  (17 shorter events, 0.2 us)
Async XLA Ops:
  0.0 47.2 %collective-permute-start = (bf16[64,512]{1,0:T(8,128)(2,1)}, bf16[64,512]{1,0:T(8,128)(2,1)S(1)}, u32[]{:S(2)}, u32[]{:S(2)}) collective-permute-start(bf16[64,512]{1,0:T(8,128)(2,1)} %bitcast.45), channel_id=1, source_target_pairs={{0,24},{8,240},{16,40},{24,0},{32,56},{40,16},{48,72},{56,32},{64,... | collective-permute-start | bytes 196616 | tf_op jit(solution)/shard_map/ppermute | solution.py:35
  48.1 12.3 %collective-permute-start.1 = (bf16[2,64,512]{2,1,0:T(8,128)(2,1)S(1)}, bf16[2,64,512]{2,1,0:T(8,128)(2,1)S(1)}, u32[]{:S(2)}, u32[]{:S(2)}) collective-permute-start(bf16[2,64,512]{2,1,0:T(8,128)(2,1)S(1)} %pad_maximum_fusion.2), channel_id=1, source_target_pairs={{0,192},{8,72},{16,208},{24,88},{32,224},{40,104},{48,240},{56,120... | collective-permute-start | bytes 393224 | tf_op jit(solution)/shard_map/ppermute | solution.py:26
  61.3 10.6 %collective-permute-start.2 = (bf16[4,64,512]{2,1,0:T(8,128)(2,1)S(1)}, bf16[4,64,512]{2,1,0:T(8,128)(2,1)S(1)}, u32[]{:S(2)}, u32[]{:S(2)}) collective-permute-start(bf16[4,64,512]{2,1,0:T(8,128)(2,1)S(1)} %pad_maximum_fusion.1), channel_id=1, source_target_pairs={{0,224},{8,40},{16,240},{24,56},{32,0},{40,72},{48,16},{56,88},{64... | collective-permute-start | bytes 786440 | tf_op jit(solution)/shard_map/ppermute | solution.py:26
  64.7 15.4 %all-to-all-start = ((bf16[8,32,256]{2,1,0:T(8,128)(2,1)}), bf16[8,32,256]{2,1,0:T(8,128)(2,1)S(1)}, u32[]{:S(2)}, u32[]{:S(2)}) async-start(bf16[8,32,256]{2,1,0:T(8,128)(2,1)} %split_cache.1), calls=%async_computation | async-start | bytes 262144 | tf_op jit(solution)/shard_map/all_to_all | solution.py:17
  72.7 24.1 %collective-permute-start.3 = (bf16[8,64,512]{2,1,0:T(8,128)(2,1)S(1)}, bf16[8,64,512]{2,1,0:T(8,128)(2,1)S(1)}, u32[]{:S(2)}, u32[]{:S(2)}) collective-permute-start(bf16[8,64,512]{2,1,0:T(8,128)(2,1)S(1)} %pad_maximum_fusion.mine_a), channel_id=1, source_target_pairs={{0,240},{8,24},{16,0},{24,40},{32,16},{40,56},{48,32},{56,72},{64,... | collective-permute-start | bytes 1572872 | tf_op jit(solution)/shard_map/ppermute | solution.py:26
  80.1 25.7 %all-to-all-start.1 = ((bf16[32,24,128]{2,1,0:T(8,128)(2,1)}), bf16[32,24,128]{2,1,0:T(8,128)(2,1)S(1)}, u32[]{:S(2)}, u32[]{:S(2)}) async-start(bf16[32,24,128]{2,1,0:T(8,128)(2,1)} %bitcast.5), calls=%async_computation.1 | async-start | bytes 393216 | tf_op jit(solution)/shard_map/all_to_all | solution.py:17
  91.0 65.9 %collective-permute-start.7 = (bf16[3,2048,128]{2,1,0:T(8,128)(2,1)}, bf16[3,2048,128]{2,1,0:T(8,128)(2,1)}, u32[]{:S(2)}, u32[]{:S(2)}) collective-permute-start(bf16[3,2048,128]{2,1,0:T(8,128)(2,1)} %get-tuple-element.20), channel_id=1, source_target_pairs={{0,1},{8,15},{1,0},{9,10},{2,3},{10,9},{3,2},{11,12},{4,5},{12,11}... | collective-permute-start | bytes 4718600 | tf_op jit(solution)/shard_map/ppermute | solution.py:561
  93.7 14.5 %collective-permute-start.4 = (bf16[8,64,512]{2,1,0:T(8,128)(2,1)S(1)}, bf16[8,64,512]{2,1,0:T(8,128)(2,1)S(1)}, u32[]{:S(2)}, u32[]{:S(2)}) collective-permute-start(bf16[8,64,512]{2,1,0:T(8,128)(2,1)S(1)} %pad_maximum_fusion.mine_a), channel_id=1, source_target_pairs={{0,8},{8,0},{1,9},{9,1},{2,10},{10,2},{3,11},{11,3},{4,12},{12,4},... | collective-permute-start | bytes 1572872 | tf_op jit(solution)/shard_map/ppermute | solution.py:39
  96.9 11.3 %collective-permute-start.5 = (bf16[8,64,512]{2,1,0:T(8,128)(2,1)S(1)}, bf16[8,64,512]{2,1,0:T(8,128)(2,1)}, u32[]{:S(2)}, u32[]{:S(2)}) collective-permute-start(bf16[8,64,512]{2,1,0:T(8,128)(2,1)S(1)} %collective-permute-done.3.mine_b), channel_id=1, source_target_pairs={{0,8},{8,0},{1,9},{9,1},{2,10},{10,2},{3,11},{11,3},{4,12},{12,4},... | collective-permute-start | bytes 1572872 | tf_op jit(solution)/shard_map/ppermute | solution.py:39
  110.8 11.8 %all-to-all-start.2 = ((bf16[8,32,256]{2,1,0:T(8,128)(2,1)}), bf16[8,32,256]{2,1,0:T(8,128)(2,1)S(1)}, u32[]{:S(2)}, u32[]{:S(2)}) async-start(bf16[8,32,256]{2,1,0:T(8,128)(2,1)} %project_out.1), calls=%async_computation.2 | async-start | bytes 262144 | tf_op jit(solution)/shard_map/all_to_all | solution.py:17
  123.3 18.3 %all-to-all-start.3 = ((bf16[16,32,256]{2,1,0:T(8,128)(2,1)}), bf16[16,32,256]{2,1,0:T(8,128)(2,1)S(1)}, u32[]{:S(2)}, u32[]{:S(2)}) async-start(bf16[16,32,256]{2,1,0:T(8,128)(2,1)} %hidden_copies.1), calls=%async_computation.3 | async-start | bytes 524288 | tf_op jit(solution)/shard_map/all_to_all | solution.py:17
  141.7 9.7 %collective-permute-start.6 = (bf16[16,32,256]{2,1,0:T(8,128)(2,1)S(1)}, bf16[16,32,256]{2,1,0:T(8,128)(2,1)S(1)}, u32[]{:S(2)}, u32[]{:S(2)}) collective-permute-start(bf16[16,32,256]{2,1,0:T(8,128)(2,1)S(1)} %all-to-all-done.3), channel_id=1, source_target_pairs={{0,8},{8,0},{1,9},{9,1},{2,10},{10,2},{3,11},{11,3},{4,12},{12,4},... | collective-permute-start | bytes 786440 | tf_op jit(solution)/shard_map/ppermute | solution.py:39
  152.7 27.7 %all-to-all-start.4 = ((bf16[8,192,256]{2,1,0:T(8,128)(2,1)}), bf16[8,192,256]{2,1,0:T(8,128)(2,1)S(1)}, u32[]{:S(2)}, u32[]{:S(2)}) async-start(bf16[8,192,256]{2,1,0:T(8,128)(2,1)} %get-tuple-element.18), calls=%async_computation.4 | async-start | bytes 1572864 | tf_op jit(solution)/shard_map/all_to_all | solution.py:17
  182.8 33.2 %copy-start = (s32[32,8]{0,1:T(8,128)S(1)}, s32[32,8]{0,1:T(8,128)}, u32[]{:S(2)}) copy-start(s32[32,8]{0,1:T(8,128)} %param.19) | copy-start | bytes 3076
  182.8 33.3 %copy-start.1 = (f32[32,8]{0,1:T(8,128)S(1)}, f32[32,8]{0,1:T(8,128)}, u32[]{:S(2)}) copy-start(f32[32,8]{0,1:T(8,128)} %param.20) | copy-start | bytes 3076
  209.4 25.1 %all-to-all-start.6 = ((bf16[32,2,6,256]{3,1,2,0:T(2,128)(2,1)}), bf16[32,2,6,256]{3,1,2,0:T(2,128)(2,1)S(1)}, u32[]{:S(2)}, u32[]{:S(2)}) async-start(bf16[32,2,6,256]{3,1,2,0:T(2,128)(2,1)} %bitcast.23), calls=%async_computation.6 | async-start | bytes 393216 | tf_op jit(solution)/shard_map/all_to_all | solution.py:17
